TPU v7x, 16 devices: a whole 2x2x2 slice. The times are simulated.
16 devices in a mesh: dp: 2 (over z), sp: 8 (over y, x, core).
Axes of the slice: x: 2, y: 2, z: 2, core: 2. Of those that a mesh axis runs over, the one named last changes fastest.
Arguments:
- hidden: bfloat16 [6144, 3072], P(('dp', 'sp')), parts along dimension 0
- grad_out: bfloat16 [6144, 3072], P(('dp', 'sp')), parts along dimension 0
- positions: int32 [6144], P(('dp', 'sp')), parts along dimension 0
- doc_ids: int32 [6144], P(('dp', 'sp')), parts along dimension 0
- w_q: bfloat16 [3072, 3072], replicated
- w_k: bfloat16 [3072, 1024], replicated
- w_v: bfloat16 [3072, 1024], replicated
- w_o: bfloat16 [3072, 3072], replicated
Outputs:
- output 1: bfloat16 [6144, 3072], P(('dp', 'sp')), parts along dimension 0
- output 2: bfloat16 [6144, 3072], P(('dp', 'sp')), parts along dimension 0
- output 3: float32 [6144, 3072], P('dp'), parts along dimension 0
- output 4: float32 [6144, 1024], P('dp'), parts along dimension 0
- output 5: float32 [6144, 1024], P('dp'), parts along dimension 0
- output 6: float32 [6144, 3072], P('dp'), parts along dimension 0
There are 2 independent parts. A program takes and returns all parts, laid end to end along the dimension named above; an argument that names none is the same for every part.
All inputs are finite; a program needn't handle non-finite values.
Results may differ from a plain program's by a relative error of at most 0.0106679.
Values are sent between devices in bfloat16 or wider.
A program may use at most 1 GiB of HBM per device.

v0:
```python
import jax
import jax.numpy as jnp
from jax import lax
from jax.sharding import PartitionSpec as P, NamedSharding

HEAD_DIM = 128
ROPE_THETA = 500000.0
ROPE_FACTOR = 8.0
ROPE_LOW = 1.0
ROPE_HIGH = 4.0
ROPE_OLD_CTX = 8192.0
SCORE_LIMIT = 32 * 1024 * 1024
NEG_BIG = -1.0e30


def rope_freqs():
    half_idx = jnp.arange(HEAD_DIM // 2, dtype=jnp.float32)
    inv_freq = jnp.power(ROPE_THETA, -2.0 * half_idx / HEAD_DIM)
    wavelen = 2.0 * jnp.pi / inv_freq
    smooth = (ROPE_OLD_CTX / wavelen - ROPE_LOW) / (ROPE_HIGH - ROPE_LOW)
    mixed_freq = (1.0 - smooth) * inv_freq / ROPE_FACTOR + smooth * inv_freq
    scaled = jnp.where(wavelen > ROPE_OLD_CTX / ROPE_LOW, inv_freq / ROPE_FACTOR, mixed_freq)
    return jnp.where(wavelen < ROPE_OLD_CTX / ROPE_HIGH, inv_freq, scaled)


def rope_tables(pos_vec):
    angles = pos_vec.astype(jnp.float32)[:, None] * rope_freqs()[None, :]
    return jnp.cos(angles)[:, None, :], jnp.sin(angles)[:, None, :]


def rotate(values, cos_tab, sin_tab):
    half_dim = values.shape[-1] // 2
    first_half = values[..., :half_dim]
    second_half = values[..., half_dim:]
    return jnp.concatenate([first_half * cos_tab - second_half * sin_tab, second_half * cos_tab + first_half * sin_tab], axis=-1)


def block_rows(n_query, head_count, n_keys):
    block_len = n_query
    while block_len % 16 == 0 and head_count * block_len * n_keys > SCORE_LIMIT:
        block_len = block_len // 2
    return block_len


def dot_last(lhs_mat, rhs_mat):
    return lax.dot_general(lhs_mat, rhs_mat, (((1,), (1,)), ((), ())), preferred_element_type=jnp.float32)


def dot_first(lhs_mat, rhs_mat):
    return lax.dot_general(lhs_mat, rhs_mat, (((0,), (0,)), ((), ())), preferred_element_type=jnp.float32)


def block_probs(q_blk, k_all, pos_blk, doc_blk, k_pos, k_doc, score_scale):
    scores = jnp.einsum("qhgd,shd->hgqs", q_blk, k_all, preferred_element_type=jnp.float32) * score_scale
    allowed = (k_pos[None, :] <= pos_blk[:, None]) & (k_doc[None, :] == doc_blk[:, None])
    scores = jnp.where(allowed, scores, NEG_BIG)
    row_peak = jnp.max(scores, axis=-1, keepdims=True)
    exp_vals = jnp.exp(scores - row_peak)
    return exp_vals / jnp.sum(exp_vals, axis=-1, keepdims=True)


def attention_fwd(q_grp, k_all, v_all, q_pos, q_doc, k_pos, k_doc):
    n_query, kv_count, group_size, head_dim = q_grp.shape
    block_len = block_rows(n_query, kv_count * group_size, k_all.shape[0])
    n_blocks = n_query // block_len
    score_scale = head_dim ** -0.5

    def fwd_block(block_in):
        q_blk, pos_blk, doc_blk = block_in
        prob_f32 = block_probs(q_blk, k_all, pos_blk, doc_blk, k_pos, k_doc, score_scale)
        context = jnp.einsum("hgqs,shd->qhgd", prob_f32.astype(jnp.bfloat16), v_all, preferred_element_type=jnp.float32)
        return context.astype(jnp.bfloat16)

    blocks = (q_grp.reshape(n_blocks, block_len, kv_count, group_size, head_dim), q_pos.reshape(n_blocks, block_len), q_doc.reshape(n_blocks, block_len))
    return lax.map(fwd_block, blocks).reshape(n_query, kv_count, group_size, head_dim)


def attention_bwd(q_grp, k_all, v_all, d_ctx, q_pos, q_doc, k_pos, k_doc):
    n_query, kv_count, group_size, head_dim = q_grp.shape
    block_len = block_rows(n_query, kv_count * group_size, k_all.shape[0])
    n_blocks = n_query // block_len
    score_scale = head_dim ** -0.5

    def bwd_block(acc_pair, block_in):
        dk_acc, dv_acc = acc_pair
        q_blk, dctx_blk, pos_blk, doc_blk = block_in
        prob_f32 = block_probs(q_blk, k_all, pos_blk, doc_blk, k_pos, k_doc, score_scale)
        d_prob = jnp.einsum("qhgd,shd->hgqs", dctx_blk, v_all, preferred_element_type=jnp.float32)
        row_dot = jnp.sum(prob_f32 * d_prob, axis=-1, keepdims=True)
        d_score = (prob_f32 * (d_prob - row_dot) * score_scale).astype(jnp.bfloat16)
        dq_blk = jnp.einsum("hgqs,shd->qhgd", d_score, k_all, preferred_element_type=jnp.float32).astype(jnp.bfloat16)
        dk_acc = dk_acc + jnp.einsum("hgqs,qhgd->shd", d_score, q_blk, preferred_element_type=jnp.float32)
        dv_acc = dv_acc + jnp.einsum("hgqs,qhgd->shd", prob_f32.astype(jnp.bfloat16), dctx_blk, preferred_element_type=jnp.float32)
        return (dk_acc, dv_acc), dq_blk

    zero_acc = jnp.zeros(k_all.shape, jnp.float32)
    blocks = (q_grp.reshape(n_blocks, block_len, kv_count, group_size, head_dim), d_ctx.reshape(n_blocks, block_len, kv_count, group_size, head_dim), q_pos.reshape(n_blocks, block_len), q_doc.reshape(n_blocks, block_len))
    (dk_acc, dv_acc), dq_blocks = lax.scan(bwd_block, (zero_acc, zero_acc), blocks)
    return dq_blocks.reshape(n_query, kv_count, group_size, head_dim), dk_acc, dv_acc


def project_qkv(hidden, w_q, w_k, w_v, cos_tab, sin_tab):
    tokens = hidden.shape[0]
    q_pre = jnp.dot(hidden, w_q, preferred_element_type=jnp.float32).reshape(tokens, -1, HEAD_DIM)
    k_pre = jnp.dot(hidden, w_k, preferred_element_type=jnp.float32).reshape(tokens, -1, HEAD_DIM)
    v_pre = jnp.dot(hidden, w_v, preferred_element_type=jnp.float32).reshape(tokens, -1, HEAD_DIM)
    q_rot = rotate(q_pre, cos_tab, sin_tab).astype(jnp.bfloat16)
    k_rot = rotate(k_pre, cos_tab, sin_tab).astype(jnp.bfloat16)
    return q_rot, k_rot, v_pre.astype(jnp.bfloat16)


def input_grads(hidden, dq_rot, dk_rot, dv_val, cos_tab, sin_tab, w_q, w_k, w_v):
    tokens = hidden.shape[0]
    dq_pre = rotate(dq_rot, cos_tab, -sin_tab).astype(jnp.bfloat16).reshape(tokens, -1)
    dk_pre = rotate(dk_rot, cos_tab, -sin_tab).astype(jnp.bfloat16).reshape(tokens, -1)
    dv_pre = dv_val.reshape(tokens, -1)
    grad_hidden = (dot_last(dq_pre, w_q) + dot_last(dk_pre, w_k) + dot_last(dv_pre, w_v)).astype(jnp.bfloat16)
    return grad_hidden, dot_first(hidden, dq_pre), dot_first(hidden, dk_pre), dot_first(hidden, dv_pre)


def solution(mesh):
    sp_size = mesh.shape["sp"]

    def device_step(hidden, grad_out, positions, doc_ids, w_q, w_k, w_v, w_o):
        tokens = hidden.shape[0]
        seq_len = tokens * sp_size
        num_q = w_q.shape[1] // HEAD_DIM
        num_kv = w_k.shape[1] // HEAD_DIM
        local_q = num_q // sp_size
        local_kv = max(1, num_kv // sp_size)
        repeat = max(1, sp_size // num_kv)
        cos_tab, sin_tab = rope_tables(positions)
        q_rot, k_rot, v_val = project_qkv(hidden, w_q, w_k, w_v, cos_tab, sin_tab)
        if repeat > 1:
            k_rot = jnp.repeat(k_rot, repeat, axis=1)
            v_val = jnp.repeat(v_val, repeat, axis=1)
        q_heads = lax.all_to_all(q_rot, "sp", 1, 0, tiled=True).reshape(seq_len, local_kv, local_q // local_kv, HEAD_DIM)
        k_heads = lax.all_to_all(k_rot, "sp", 1, 0, tiled=True)
        v_heads = lax.all_to_all(v_val, "sp", 1, 0, tiled=True)
        pos_all = lax.all_gather(positions, "sp", tiled=True)
        doc_all = lax.all_gather(doc_ids, "sp", tiled=True)
        ctx_heads = attention_fwd(q_heads, k_heads, v_heads, pos_all, doc_all, pos_all, doc_all)
        ctx_flat = lax.all_to_all(ctx_heads.reshape(seq_len, local_q, HEAD_DIM), "sp", 0, 1, tiled=True).reshape(tokens, num_q * HEAD_DIM)
        attn_out = jnp.dot(ctx_flat, w_o, preferred_element_type=jnp.float32).astype(jnp.bfloat16)
        d_ctx = dot_last(grad_out, w_o).astype(jnp.bfloat16).reshape(tokens, num_q, HEAD_DIM)
        grad_wo = dot_first(ctx_flat, grad_out)
        d_ctx_heads = lax.all_to_all(d_ctx, "sp", 1, 0, tiled=True).reshape(seq_len, local_kv, local_q // local_kv, HEAD_DIM)
        dq_heads, dk_heads, dv_heads = attention_bwd(q_heads, k_heads, v_heads, d_ctx_heads, pos_all, doc_all, pos_all, doc_all)
        dq_rot = lax.all_to_all(dq_heads.reshape(seq_len, local_q, HEAD_DIM), "sp", 0, 1, tiled=True)
        dk_back = lax.all_to_all(dk_heads.astype(jnp.bfloat16), "sp", 0, 1, tiled=True)
        dv_back = lax.all_to_all(dv_heads.astype(jnp.bfloat16), "sp", 0, 1, tiled=True)
        if repeat > 1:
            dk_back = jnp.sum(dk_back.reshape(tokens, num_kv, repeat, HEAD_DIM), axis=2, dtype=jnp.float32)
            dv_back = jnp.sum(dv_back.reshape(tokens, num_kv, repeat, HEAD_DIM), axis=2, dtype=jnp.float32).astype(jnp.bfloat16)
        grad_hidden, grad_wq, grad_wk, grad_wv = input_grads(hidden, dq_rot, dk_back, dv_back, cos_tab, sin_tab, w_q, w_k, w_v)
        grad_wq, grad_wk, grad_wv, grad_wo = lax.psum((grad_wq, grad_wk, grad_wv, grad_wo), "sp")
        return attn_out, grad_hidden, grad_wq, grad_wk, grad_wv, grad_wo

    tok_spec = P(("dp", "sp"), None)
    vec_spec = P(("dp", "sp"))
    rep_spec = P(None, None)
    part_spec = P("dp", None)
    return jax.shard_map(device_step, mesh=mesh, in_specs=(tok_spec, tok_spec, vec_spec, vec_spec, rep_spec, rep_spec, rep_spec, rep_spec), out_specs=(tok_spec, tok_spec, part_spec, part_spec, part_spec, part_spec), check_vma=False)
```

profile of v0, /device:TPU:1, one launch (start us, length us, event | category | flops | bytes accessed | tf_op | source)
XLA Modules:
  0.0 1883.8 jit_solution(7458266037098250692)
XLA Ops:
  8.9 10.8 convolution_bitcast_fusion.4
  20.7 1.5 fusion.44
  22.2 1.5 fusion.41
  23.6 1.7 subtract_convert_fusion
  25.4 2.7 pad_maximum_fusion
  28.1 5.2 all-to-all-start.2
  33.3 4.7 convolution_bitcast_fusion.5
  38.8 26.7 %all-gather = s32[8,1,384]{2,1,0:T(1,128)S(1)} all-gather(s32[1,1,384]{2,1,0:T(1,128)S(1)} %reshape.215), channel_id=1, replica_groups=mesh['dp'=2,'sp'=8] {'sp'}, dimensions={0}, use_global_device_ids=true | all-gather | bytes 13824 | tf_op jit(solution)/shard_map/all_gather | solution.py:140
  65.5 8.0 all-gather.1
  73.5 11.2 fusion.35
  84.7 2.0 copy.162
  87.4 1.3 pad_maximum_fusion.2
  88.7 10.1 compare_and_fusion
  98.8 3.6 all-to-all-start.1
  102.4 5.4 fusion.40
  108.8 3.3 copy.107
  112.1 7.1 all-to-all-start.4
  119.2 43.0 %fusion.6 = (f32[3,3072]{1,0:T(4,128)S(1)}, f32[3072,3072,3]{1,0,2:T(8,128)}) fusion(pred[3072,3072]{0,1:T(8,128)(4,1)} %compare_and_fusion, bf16[3072,128,1]{1,0,2:T(8,128)(2,1)S(1)} %bitcast.202, bf16[3072,3,128]{2,0,1:T(8,128)(2,1)} %bitcast.196), kind=kOutput, calls=%fused_computation.10 | convolution fusion | flops 7332682752 | bytes 125865984 | tf_op jit(solution)/shard_map/while/body/eval_jaxpr/qhgd,shd->hgqs/dot_general | solution.py:54
  162.2 4.5 all-to-all-start
  166.7 37.5 %fusion.5 = f32[3,3072]{1,0:T(4,128)S(1)} fusion(f32[3072,3072,3]{1,0,2:T(8,128)} %get-tuple-element.119, f32[3,3072]{1,0:T(4,128)S(1)} %get-tuple-element.118, pred[3072,3072]{0,1:T(8,128)(4,1)} %compare_and_fusion), kind=kLoop, calls=%fused_computation.9 | loop fusion | flops 113236992 | bytes 122757120 | tf_op jit(solution)/shard_map/while/body/eval_jaxpr/reduce_sum | solution.py:59
  204.2 3.3 copy.113
  207.5 89.8 %fusion = (f32[3,3072]{1,0:T(4,128)S(1)}, f32[3072,3072,3]{1,0,2:T(8,128)}) fusion(f32[3,3072]{1,0:T(4,128)S(1)} %fusion.5, f32[3,3072]{1,0:T(4,128)S(1)} %get-tuple-element.118, f32[3072,3072,3]{1,0,2:T(8,128)} %get-tuple-element.119, pred[3072,3072]{0,1:T(8,128)(4,1)} %compare_and_fusion, bf16[3072,128,1]{1,0,2:T(8,128)(2,1)S(1)} %bitcast.212, ...), kind=kOutput, calls=%fused_computation.3 | convolution fusion | flops 7417617408 | bytes 239185920 | tf_op jit(solution)/shard_map/while/body/eval_jaxpr/qhgd,shd->hgqs/dot_general | solution.py:88
  297.4 91.0 %fusion.7 = bf16[3,3072,3072]{1,2,0:T(8,128)(2,1)} fusion(f32[3072,3072,3]{1,0,2:T(8,128)} %get-tuple-element.121, f32[3,3072]{1,0:T(4,128)S(1)} %get-tuple-element.120, f32[3,3072]{1,0:T(4,128)S(1)} %fusion.5, f32[3,3072]{1,0:T(4,128)S(1)} %get-tuple-element.118, f32[3072,3072,3]{1,0,2:T(8,128)} %get-tuple-element.119, pred[3072,3072]{0,1:T(8,128)(4,1)} %compare_and_fusion), kind=kLoop, calls=%fused_computation.11 | loop fusion | flops 226492416 | bytes 292663296 | tf_op jit(solution)/shard_map/reshape.43
  388.4 25.1 %fusion.34 = bf16[3072,1,128]{0,2,1:T(8,128)(2,1)S(1)} fusion(bf16[3072,3,128]{2,0,1:T(8,128)(2,1)} %bitcast.197, bf16[3,3072,3072]{1,2,0:T(8,128)(2,1)} %fusion.7), kind=kOutput, calls=%fused_computation.43 | convolution fusion | flops 7248150528 | bytes 59768832 | tf_op jit(solution)/shard_map/while/body/eval_jaxpr/hgqs,qhgd->shd/dot_general | solution.py:92
  414.0 1.8 reduce.4
  415.9 1.5 copy.165
  418.4 4.7 all-to-all-start.6
  423.1 46.3 %fusion.31 = bf16[3072,1,128]{0,2,1:T(8,128)(2,1)} fusion(bf16[3072,3,128]{2,0,1:T(8,128)(2,1)} %bitcast.211, f32[3,3072]{1,0:T(4,128)S(1)} %fusion.5, f32[3,3072]{1,0:T(4,128)S(1)} %get-tuple-element.118, f32[3072,3072,3]{1,0,2:T(8,128)} %get-tuple-element.119, pred[3072,3072]{0,1:T(8,128)(4,1)} %compare_and_fusion), kind=kOutput, calls=%fused_computation.42 | convolution fusion | flops 7389708288 | bytes 125902848 | tf_op jit(solution)/shard_map/while/body/eval_jaxpr/hgqs,qhgd->shd/dot_general | solution.py:93
  469.4 3.1 reduce.3
  472.4 2.3 copy.164
  474.7 2.8 reshape.225
  477.5 4.2 all-to-all-start.7
  481.7 22.0 %fusion.23 = bf16[3072,3,128]{0,2,1:T(8,128)(2,1)} fusion(bf16[3072,128,1]{1,0,2:T(8,128)(2,1)S(1)} %bitcast.203, bf16[3,3072,3072]{1,2,0:T(8,128)(2,1)} %fusion.7), kind=kOutput, calls=%fused_computation.37 | convolution fusion | flops 7248936960 | bytes 59768832 | tf_op jit(solution)/shard_map/while/body/eval_jaxpr/hgqs,shd->qhgd/dot_general | solution.py:91
  503.8 5.7 copy.117
  509.5 4.6 all-to-all-start.5
  514.1 47.8 %fusion.20 = bf16[3072,3,128]{0,2,1:T(8,128)(2,1)} fusion(bf16[3072,128,1]{1,0,2:T(8,128)(2,1)S(1)} %bitcast.213, f32[3,3072]{1,0:T(4,128)S(1)} %fusion.5, f32[3,3072]{1,0:T(4,128)S(1)} %get-tuple-element.118, f32[3072,3072,3]{1,0,2:T(8,128)} %get-tuple-element.119, pred[3072,3072]{0,1:T(8,128)(4,1)} %compare_and_fusion), kind=kOutput, calls=%fused_computation.36 | convolution fusion | flops 7390494720 | bytes 125902848 | tf_op jit(solution)/shard_map/while/body/eval_jaxpr/hgqs,shd->qhgd/dot_general | solution.py:71
  561.9 5.7 copy.109
  567.6 5.5 reshape.228
  573.1 1.5 copy.142
  576.6 1.5 copy.124
  578.1 5.5 reshape.226
  583.6 2.4 copy.143
  586.0 2.3 copy.128
  588.3 6.6 convolution_bitcast_fusion.2
  594.9 6.6 convolution_bitcast_fusion.1
  601.5 4.4 all-to-all-start.3
  606.1 2.2 copy.118
  608.6 2.1 fusion.14
  610.7 2.7 pad_maximum_fusion.1
  613.4 4.3 copy.120
  617.7 18.1 convolution_bitcast_fusion
  635.8 4.1 all-to-all-done.3
  639.9 3.6 copy.110
  643.5 4.3 copy.111
  647.8 20.4 %fusion.48 = f32[3072,3072]{1,0:T(8,128)} fusion(bf16[384,3072]{0,1:T(8,128)(2,1)} %bitcast.194, bf16[384,3072]{1,0:T(8,128)(2,1)} %param.9), kind=kOutput, calls=%fused_computation.74 | convolution fusion | flops 7247757312 | bytes 42467328 | tf_op jit(solution)/shard_map/dot_general | solution.py:50
  668.2 7.7 fusion.46
  676.0 7.9 fusion.47
  683.9 8.9 convolution_convert_fusion.2
  692.8 15.5 add_convert_fusion
  708.3 1078.3 %all-reduce.3.cloned.1.call-done = (f32[3072,3072]{0,1:T(8,128)}, f32[3072,1024]{0,1:T(8,128)}, f32[3072,1024]{0,1:T(8,128)}, f32[3072,3072]{1,0:T(8,128)}) async-done(((f32[3072,3072]{0,1:T(8,128)}, f32[3072,1024]{0,1:T(8,128)}, f32[3072,1024]{0,1:T(8,128)}, f32[3072,3072]{1,0:T(8,128)}), (f32[3072,3072]{0,1:T(8,128)}, f32[3072,1024]{0,1:T(8,128)}, f32[3072,1024]{0,1:T(8,128)}, ...) | async-done | bytes 100663312 | tf_op jit(solution)/shard_map/psum | solution.py:156
  1786.6 36.8 %copy.129 = f32[3072,3072]{1,0:T(8,128)} copy(f32[3072,3072]{0,1:T(8,128)} %get-tuple-element.99) | data formatting | bytes 75497472
  1823.4 12.6 copy.130
  1836.0 12.6 copy.131
  1848.6 27.9 %copy.170 = f32[3072,3072]{1,0:T(8,128)} copy(f32[3072,3072]{1,0:T(8,128)} %get-tuple-element.127) | data formatting | bytes 75497472
  (62 shorter events, 9.3 us)
Async XLA Ops:
  7.2 1.7 copy-start
  23.6 63.1 %copy-start.2 = (f32[384,64]{1,0:T(8,128)}, f32[384,64]{1,0:T(8,128)S(1)}, u32[]{:S(2)}) copy-start(f32[384,64]{1,0:T(8,128)S(1)} %get-tuple-element.117) | copy-start | bytes 294916
  25.3 7.9 copy-start.12
  28.1 70.7 %all-to-all-start.2 = ((bf16[384,24,128]{2,0,1:T(8,128)(2,1)}), bf16[384,24,128]{2,0,1:T(8,128)(2,1)}, u32[]{:S(2)}, u32[]{:S(2)}) async-start(bf16[384,24,128]{2,0,1:T(8,128)(2,1)} %pad_maximum_fusion), calls=%async_computation.2 | async-start | bytes 4718592 | tf_op jit(solution)/shard_map/all_to_all | solution.py:137
  38.0 27.5 %copy-start.13 = (s32[384]{0:T(512)S(1)}, s32[384]{0:T(512)}, u32[]{:S(2)}) copy-start(s32[384]{0:T(512)} %param.11) | copy-start | bytes 4612
  38.0 35.6 %copy-start.8 = (bf16[384,3072]{1,0:T(8,128)(2,1)S(1)}, bf16[384,3072]{1,0:T(8,128)(2,1)}, u32[]{:S(2)}) copy-start(bf16[384,3072]{1,0:T(8,128)(2,1)} %param.9) | copy-start | bytes 7077892
  98.8 13.3 all-to-all-start.1
  112.1 50.1 %copy-start.4 = (bf16[384,8,128]{2,0,1:T(8,128)(2,1)}, bf16[384,8,128]{2,0,1:T(8,128)(2,1)S(1)}, u32[]{:S(2)}) copy-start(bf16[384,8,128]{2,0,1:T(8,128)(2,1)S(1)} %all-to-all-done.1) | copy-start | bytes 2359300
  112.1 50.1 %all-to-all-start.4 = ((bf16[384,24,128]{2,0,1:T(8,128)(2,1)}), bf16[384,24,128]{2,0,1:T(8,128)(2,1)}, u32[]{:S(2)}, u32[]{:S(2)}) async-start(bf16[384,24,128]{2,0,1:T(8,128)(2,1)} %bitcast.198), calls=%async_computation.4 | async-start | bytes 4718592 | tf_op jit(solution)/shard_map/all_to_all | solution.py:147
  162.2 45.3 %all-to-all-start = ((bf16[384,8,128]{2,0,1:T(8,128)(2,1)}), bf16[384,8,128]{2,0,1:T(8,128)(2,1)S(1)}, u32[]{:S(2)}, u32[]{:S(2)}) async-start(bf16[384,8,128]{2,0,1:T(8,128)(2,1)} %bitcast.208), calls=%async_computation | async-start | bytes 1572864 | tf_op jit(solution)/shard_map/all_to_all | solution.py:139
  207.5 89.8 %copy-start.10 = (bf16[384,8,128]{2,0,1:T(8,128)(2,1)}, bf16[384,8,128]{2,0,1:T(8,128)(2,1)S(1)}, u32[]{:S(2)}) copy-start(bf16[384,8,128]{2,0,1:T(8,128)(2,1)S(1)} %all-to-all-done) | copy-start | bytes 2359300
  418.4 59.1 %all-to-all-start.6 = ((bf16[8,2,24576]{2,1,0:T(2,128)(2,1)}), bf16[8,2,24576]{2,1,0:T(2,128)(2,1)}, u32[]{:S(2)}, u32[]{:S(2)}) async-start(bf16[8,2,24576]{2,1,0:T(2,128)(2,1)} %reshape.227), calls=%async_computation.6 | async-start | bytes 1572864 | tf_op jit(solution)/shard_map/all_to_all | solution.py:150
  469.4 12.4 copy-start.5
  477.5 31.9 %all-to-all-start.7 = ((bf16[8,2,24576]{2,1,0:T(2,128)(2,1)}), bf16[8,2,24576]{2,1,0:T(2,128)(2,1)}, u32[]{:S(2)}, u32[]{:S(2)}) async-start(bf16[8,2,24576]{2,1,0:T(2,128)(2,1)} %reshape.225), calls=%async_computation.7 | async-start | bytes 1572864 | tf_op jit(solution)/shard_map/all_to_all | solution.py:151
  503.8 10.3 copy-start.11
  509.5 92.0 %all-to-all-start.5 = ((bf16[3072,3,128]{2,1,0:T(4,128)(2,1)}), bf16[3072,3,128]{2,1,0:T(4,128)(2,1)}, u32[]{:S(2)}, u32[]{:S(2)}) async-start(bf16[3072,3,128]{2,1,0:T(4,128)(2,1)} %copy.117), calls=%async_computation.5 | async-start | bytes 6291456 | tf_op jit(solution)/shard_map/all_to_all | solution.py:149
  561.9 12.7 copy-start.3
  561.9 12.7 copy-start.9
  588.3 6.6 copy-start.6
  601.5 38.4 %all-to-all-start.3 = ((bf16[3072,3,128]{2,1,0:T(4,128)(2,1)}), bf16[3072,3,128]{2,1,0:T(4,128)(2,1)}, u32[]{:S(2)}, u32[]{:S(2)}) async-start(bf16[3072,3,128]{2,1,0:T(4,128)(2,1)} %copy.109), calls=%async_computation.3 | async-start | bytes 6291456 | tf_op jit(solution)/shard_map/all_to_all | solution.py:143
  605.9 1180.7 %all-reduce.3.cloned.1.call-start = ((), (), s32[]{:S(2)}) async-start(), calls=%async_computation.8 | async-start | bytes 201326592 | tf_op jit(solution)/shard_map/psum | solution.py:156
  668.2 7.8 copy-start.7
  668.2 15.7 slice-start
  668.2 15.7 slice-start.1
  668.2 15.6 slice-start.2
  676.0 7.9 copy-start.1
  676.0 7.9 slice-start.3
  676.0 7.9 slice-start.4
Sparse Core Ops, SparseCore 0:
  668.3 1118.2 all-reduce.2
where the time goes:
time: 1890 us; the launch traced here: 1880 us
  waiting for transfers between devices  1080 us (57%)
  matrix products  398 us (21%)
  other arithmetic  159 us (8%)
  local copies, waits for them, and re-layouts  157 us (8%)
  starting transfers between devices  38.5 us (2%)
  blocking collectives  34.7 us (2%)
    psum x1, waiting for transfers between devices, device_step(): lax.psum((grad_wq, grad_wk, grad_wv, grad_wo), 'sp')  1080 us
    unnamed x54, local copies, waits for them, and re-layouts  115 us
    another operation x5, other arithmetic  96.1 us
    dot_general x1, matrix products, bwd_block(): jnp.einsum('qhgd,shd->hgqs', dctx_blk, v_all, preferred_element_type=jnp....  89.8 us
    dot_general x4, matrix products, dot_first(): lax.dot_general(lhs_mat, rhs_mat, (((0,), (0,)), ((), ())), preferred_ele...  51.6 us
    dot_general x1, matrix products, fwd_block(): jnp.einsum('hgqs,shd->qhgd', prob_f32.astype(jnp.bfloat16), v_all, prefer...  47.8 us
    dot_general x1, matrix products, bwd_block(): jnp.einsum('hgqs,qhgd->shd', prob_f32.astype(jnp.bfloat16), dctx_blk, pre...  46.3 us
    dot_general x1, matrix products, block_probs(): jnp.einsum('qhgd,shd->hgqs', q_blk, k_all, preferred_element_type=jnp.flo...  43 us
  transfers between devices with their start and end apart: 9, of which 2 were waited for; matrix products, arithmetic and copies ran while one was open for 19% of the time, Pallas kernels for 0%

commit v1 on v0

v1 whole, which is shorter than its diff:
```python
import functools
import math

import jax
import jax.numpy as jnp
from jax import lax
from jax.experimental import pallas as pl
from jax.experimental.pallas import tpu as pltpu
from jax.sharding import PartitionSpec as P


HEAD_DIM = 128
HALF = HEAD_DIM // 2
ROPE_THETA = 500000.0
ROPE_FACTOR = 8.0
ROPE_LOW = 1.0
ROPE_HIGH = 4.0
ROPE_OLD_CTX = 8192.0
NEG_BIG = -1.0e30
BLK = 256
F32 = jnp.float32
BF16 = jnp.bfloat16


def rope_freqs():
    half_idx = jnp.arange(HALF, dtype=F32)
    inv_freq = jnp.power(ROPE_THETA, -2.0 * half_idx / HEAD_DIM)
    wavelen = 2.0 * jnp.pi / inv_freq
    smooth = (ROPE_OLD_CTX / wavelen - ROPE_LOW) / (ROPE_HIGH - ROPE_LOW)
    mixed_freq = (1.0 - smooth) * inv_freq / ROPE_FACTOR + smooth * inv_freq
    scaled = jnp.where(wavelen > ROPE_OLD_CTX / ROPE_LOW, inv_freq / ROPE_FACTOR, mixed_freq)
    return jnp.where(wavelen < ROPE_OLD_CTX / ROPE_HIGH, inv_freq, scaled)


def dot_nn(lhs, rhs):
    return lax.dot_general(lhs, rhs, (((1,), (0,)), ((), ())), preferred_element_type=F32)


def dot_nt(lhs, rhs):
    return lax.dot_general(lhs, rhs, (((1,), (1,)), ((), ())), preferred_element_type=F32)


def dot_tn(lhs, rhs):
    return lax.dot_general(lhs, rhs, (((0,), (0,)), ((), ())), preferred_element_type=F32)


def dot_tt(lhs, rhs):
    return lax.dot_general(lhs, rhs, (((0,), (1,)), ((), ())), preferred_element_type=F32)


def proj_kernel(group, x_ref, g_ref, wq_ref, wk_ref, wv_ref, wo_ref, cos_ref, sin_ref, out_ref):
    cos_tab, sin_tab = cos_ref[...], sin_ref[...]

    def rope(val):
        return (val * cos_tab + pltpu.roll(val, HALF, 1) * sin_tab).astype(BF16)

    width = group * HEAD_DIM
    q_val = dot_nn(x_ref[...], wq_ref[...])
    for head in range(group):
        cols = slice(head * HEAD_DIM, (head + 1) * HEAD_DIM)
        out_ref[0, :, cols] = rope(q_val[:, cols])
    out_ref[0, :, width:2 * width] = dot_nt(g_ref[...], wo_ref[...]).astype(BF16)
    out_ref[0, :, 2 * width:2 * width + HEAD_DIM] = rope(dot_nn(x_ref[...], wk_ref[...]))
    out_ref[0, :, 2 * width + HEAD_DIM:] = dot_nn(x_ref[...], wv_ref[...]).astype(BF16)


def project(hidden, grad_out, w_q, w_k, w_v, w_o, cos_tab, sin_tab, n_dev, group):
    tokens, width = hidden.shape
    cols = group * HEAD_DIM
    total = 2 * cols + 2 * HEAD_DIM
    flops = 2 * tokens * width * n_dev * total
    return pl.pallas_call(
        functools.partial(proj_kernel, group),
        grid=(n_dev,),
        in_specs=[
            pl.BlockSpec((tokens, width), lambda i: (0, 0)),
            pl.BlockSpec((tokens, width), lambda i: (0, 0)),
            pl.BlockSpec((width, cols), lambda i: (0, i)),
            pl.BlockSpec((width, HEAD_DIM), lambda i: (0, i)),
            pl.BlockSpec((width, HEAD_DIM), lambda i: (0, i)),
            pl.BlockSpec((cols, width), lambda i: (i, 0)),
            pl.BlockSpec((tokens, HEAD_DIM), lambda i: (0, 0)),
            pl.BlockSpec((tokens, HEAD_DIM), lambda i: (0, 0)),
        ],
        out_specs=pl.BlockSpec((1, tokens, total), lambda i: (i, 0, 0)),
        out_shape=jax.ShapeDtypeStruct((n_dev, tokens, total), BF16),
        compiler_params=pltpu.CompilerParams(dimension_semantics=("arbitrary",), vmem_limit_bytes=48 * 1024 * 1024),
        cost_estimate=pl.CostEstimate(flops=flops, bytes_accessed=60_000_000, transcendentals=0),
        name="project",
    )(hidden, grad_out, w_q, w_k, w_v, w_o, cos_tab, sin_tab)


def attn_kernel(group, lo_ref, q_ref, do_ref, k_ref, v_ref, start_ref, cos_ref, sin_ref,
                ctx_lo, ctx_hi, dq_lo, dq_hi, dk_ref, dv_ref,
                s_scr, dp_scr, dk_acc, dv_acc, kt_scr, vt_scr, ctx_acc, dq_acc):
    blk = pl.program_id(0)
    n_blk = pl.num_programs(0)
    seq = k_ref.shape[0]
    scale = HEAD_DIM ** -0.5
    exp_scale = scale * math.log2(math.e)

    @pl.when(blk == 0)
    def _():
        dk_acc[...] = jnp.zeros_like(dk_acc)
        dv_acc[...] = jnp.zeros_like(dv_acc)

        @pl.loop(0, seq // BLK)
        def _(c):
            rows = pl.ds(pl.multiple_of(c * BLK, BLK), BLK)
            kt_scr[:, rows] = k_ref[rows, :].astype(F32).T.astype(BF16)
            vt_scr[:, rows] = v_ref[rows, :].astype(F32).T.astype(BF16)

    first = lo_ref[blk]
    last = blk + 1
    heads = [slice(h * HEAD_DIM, (h + 1) * HEAD_DIM) for h in range(group)]
    lanes = [slice(h * BLK, (h + 1) * BLK) for h in range(group)]
    starts = start_ref[...]
    q_idx = blk * BLK + lax.broadcasted_iota(jnp.int32, (1, BLK), 1)
    key_iota = lax.broadcasted_iota(jnp.int32, (BLK, BLK), 0)

    def score_step(c, peaks):
        rows = pl.ds(pl.multiple_of(c * BLK, BLK), BLK)
        key_idx = key_iota + c * BLK
        allowed = (key_idx >= starts) & (key_idx <= q_idx)
        k_blk = k_ref[rows, :]
        out = []
        for h in range(group):
            scores = jnp.where(allowed, dot_nt(k_blk, q_ref[:, heads[h]]), NEG_BIG)
            s_scr[rows, lanes[h]] = scores
            out.append(jnp.maximum(peaks[h], jnp.max(scores, axis=0, keepdims=True)))
        return tuple(out)

    peaks = lax.fori_loop(first, last, score_step, tuple(jnp.full((1, BLK), NEG_BIG, F32) for _ in range(group)))
    peaks = tuple(peak * exp_scale for peak in peaks)

    def exp_step(c, sums):
        rows = pl.ds(pl.multiple_of(c * BLK, BLK), BLK)
        v_blk = v_ref[rows, :]
        out = []
        for h in range(group):
            probs = jnp.exp2(s_scr[rows, lanes[h]] * exp_scale - peaks[h])
            d_prob = dot_nt(v_blk, do_ref[:, heads[h]])
            s_scr[rows, lanes[h]] = probs
            dp_scr[rows, lanes[h]] = d_prob
            out.append(sums[2 * h] + jnp.sum(probs, axis=0, keepdims=True))
            out.append(sums[2 * h + 1] + jnp.sum(probs * d_prob, axis=0, keepdims=True))
        return tuple(out)

    sums = lax.fori_loop(first, last, exp_step, tuple(jnp.zeros((1, BLK), F32) for _ in range(2 * group)))
    inv_sum = [1.0 / sums[2 * h] for h in range(group)]
    row_dot = [sums[2 * h + 1] * inv_sum[h] for h in range(group)]

    ctx_acc[...] = jnp.zeros_like(ctx_acc)
    dq_acc[...] = jnp.zeros_like(dq_acc)

    def grad_step(c, carry):
        rows = pl.ds(pl.multiple_of(c * BLK, BLK), BLK)
        k_t, v_t = kt_scr[:, rows], vt_scr[:, rows]
        dk_sum, dv_sum = dk_acc[rows, :], dv_acc[rows, :]
        for h in range(group):
            probs = s_scr[rows, lanes[h]] * inv_sum[h]
            probs_bf = probs.astype(BF16)
            d_score = (probs * (dp_scr[rows, lanes[h]] - row_dot[h]) * scale).astype(BF16)
            ctx_acc[:, lanes[h]] += dot_nn(v_t, probs_bf)
            dq_acc[:, lanes[h]] += dot_nn(k_t, d_score)
            dk_sum = dk_sum + dot_nn(d_score, q_ref[:, heads[h]])
            dv_sum = dv_sum + dot_nn(probs_bf, do_ref[:, heads[h]])
        dk_acc[rows, :] = dk_sum
        dv_acc[rows, :] = dv_sum
        return carry

    lax.fori_loop(first, last, grad_step, 0)

    def unrope(val, cos_tab, sin_tab):
        upper, lower = val[:HALF], val[HALF:]
        return (upper * cos_tab + lower * sin_tab).astype(BF16), (lower * cos_tab - upper * sin_tab).astype(BF16)

    own = pl.ds(pl.multiple_of(blk * BLK, BLK), BLK)
    cos_q, sin_q = cos_ref[:, own], sin_ref[:, own]
    half = ctx_lo.shape[0]
    for h in range(group):
        ctx_val = ctx_acc[:, lanes[h]].astype(BF16)
        dq_val = unrope(dq_acc[:, lanes[h]].astype(BF16).astype(F32), cos_q, sin_q)
        for part in range(2):
            row = h * HEAD_DIM + part * HALF
            ctx_out, dq_out = (ctx_lo, dq_lo) if row < half else (ctx_hi, dq_hi)
            place = slice(row % half, row % half + HALF)
            ctx_out[place, :] = ctx_val[part * HALF:(part + 1) * HALF]
            dq_out[place, :] = dq_val[part]

    @pl.when(blk == n_blk - 1)
    def _():
        @pl.loop(0, seq // BLK)
        def _(c):
            rows = pl.ds(pl.multiple_of(c * BLK, BLK), BLK)
            upper, lower = unrope(dk_acc[rows, :].T.astype(BF16).astype(F32), cos_ref[:, rows], sin_ref[:, rows])
            dk_ref[:HALF, rows] = upper
            dk_ref[HALF:, rows] = lower
            dv_ref[:, rows] = dv_acc[rows, :].T.astype(BF16)


def attention(packed, first_blk, starts, cos_t, sin_t, group):
    seq = packed.shape[0]
    cols = group * HEAD_DIM
    n_blk = seq // BLK
    grid_spec = pltpu.PrefetchScalarGridSpec(
        num_scalar_prefetch=1,
        grid=(n_blk,),
        in_specs=[
            pl.BlockSpec((BLK, cols), lambda i, lo: (i, 0)),
            pl.BlockSpec((BLK, cols), lambda i, lo: (i, 1)),
            pl.BlockSpec((seq, HEAD_DIM), lambda i, lo: (0, 2 * group)),
            pl.BlockSpec((seq, HEAD_DIM), lambda i, lo: (0, 2 * group + 1)),
            pl.BlockSpec((1, BLK), lambda i, lo: (0, i)),
            pl.BlockSpec((HALF, seq), lambda i, lo: (0, 0)),
            pl.BlockSpec((HALF, seq), lambda i, lo: (0, 0)),
        ],
        out_specs=[
            pl.BlockSpec((cols // 2, BLK), lambda i, lo: (0, i)),
            pl.BlockSpec((cols // 2, BLK), lambda i, lo: (0, i)),
            pl.BlockSpec((cols // 2, BLK), lambda i, lo: (0, i)),
            pl.BlockSpec((cols // 2, BLK), lambda i, lo: (0, i)),
            pl.BlockSpec((HEAD_DIM, seq), lambda i, lo: (0, 0)),
            pl.BlockSpec((HEAD_DIM, seq), lambda i, lo: (0, 0)),
        ],
        scratch_shapes=[
            pltpu.VMEM((seq, group * BLK), F32),
            pltpu.VMEM((seq, group * BLK), F32),
            pltpu.VMEM((seq, HEAD_DIM), F32),
            pltpu.VMEM((seq, HEAD_DIM), F32),
            pltpu.VMEM((HEAD_DIM, seq), BF16),
            pltpu.VMEM((HEAD_DIM, seq), BF16),
            pltpu.VMEM((HEAD_DIM, group * BLK), F32),
            pltpu.VMEM((HEAD_DIM, group * BLK), F32),
        ],
    )
    return pl.pallas_call(
        functools.partial(attn_kernel, group),
        grid_spec=grid_spec,
        out_shape=[
            jax.ShapeDtypeStruct((cols // 2, seq), BF16),
            jax.ShapeDtypeStruct((cols // 2, seq), BF16),
            jax.ShapeDtypeStruct((cols // 2, seq), BF16),
            jax.ShapeDtypeStruct((cols // 2, seq), BF16),
            jax.ShapeDtypeStruct((HEAD_DIM, seq), BF16),
            jax.ShapeDtypeStruct((HEAD_DIM, seq), BF16),
        ],
        compiler_params=pltpu.CompilerParams(dimension_semantics=("arbitrary",), vmem_limit_bytes=56 * 1024 * 1024),
        cost_estimate=pl.CostEstimate(flops=60 * seq * seq * HEAD_DIM, bytes_accessed=12_000_000, transcendentals=group * seq * seq // 2),
        name="attention",
    )(first_blk, packed, packed, packed, packed, starts, cos_t, sin_t)


def assemble_kernel(turn, me_ref, *refs):
    out_ref = refs[-1]
    for rel, ref in enumerate(refs[:-1]):
        tokens = ref.shape[0]
        place = pl.ds(pl.multiple_of((me_ref[0] ^ rel) * tokens, tokens), tokens)
        if turn:
            out_ref[:, place] = ref[...].T
        else:
            out_ref[place, :] = ref[...]


def assemble(pieces, me, turn):
    tokens, width = pieces[0].shape
    seq = tokens * len(pieces)
    col_blk = 512
    if turn:
        out_spec, shape = pl.BlockSpec((col_blk, seq), lambda i, me: (i, 0)), (width, seq)
    else:
        out_spec, shape = pl.BlockSpec((seq, col_blk), lambda i, me: (0, i)), (seq, width)
    return pl.pallas_call(
        functools.partial(assemble_kernel, turn),
        grid_spec=pltpu.PrefetchScalarGridSpec(
            num_scalar_prefetch=1,
            grid=(width // col_blk,),
            in_specs=[pl.BlockSpec((tokens, col_blk), lambda i, me: (0, i)) for _ in pieces],
            out_specs=out_spec,
        ),
        out_shape=jax.ShapeDtypeStruct(shape, BF16),
        compiler_params=pltpu.CompilerParams(dimension_semantics=("arbitrary",), vmem_limit_bytes=32 * 1024 * 1024),
        cost_estimate=pl.CostEstimate(flops=0, bytes_accessed=4 * seq * width, transcendentals=0),
    )(me, *pieces)


def own_kernel(rows, me_ref, *refs):
    out_ref = refs[-1]
    for rel in range(len(refs[:-1]) // len(rows)):
        base = (me_ref[0] ^ rel) * sum(rows)
        for part, height in enumerate(rows):
            place = pl.ds(pl.multiple_of(base + sum(rows[:part]), HALF), height)
            out_ref[place, :] = refs[rel * len(rows) + part][...]


def own_columns(pieces, me, tokens):
    rows = tuple(part.shape[0] for part in pieces[0])
    flat = [part for piece in pieces for part in piece]
    total = sum(rows) * len(pieces)
    return pl.pallas_call(
        functools.partial(own_kernel, rows),
        grid_spec=pltpu.PrefetchScalarGridSpec(
            num_scalar_prefetch=1,
            grid=(1,),
            in_specs=[pl.BlockSpec((part.shape[0], tokens), lambda i, me: (0, me[0])) for part in flat],
            out_specs=pl.BlockSpec((total, tokens), lambda i, me: (0, 0)),
        ),
        out_shape=jax.ShapeDtypeStruct((total, tokens), BF16),
        compiler_params=pltpu.CompilerParams(dimension_semantics=("arbitrary",), vmem_limit_bytes=16 * 1024 * 1024),
        cost_estimate=pl.CostEstimate(flops=0, bytes_accessed=4 * total * tokens, transcendentals=0),
    )(me, *flat)


def wgrad_kernel(by_rows, rels, n_out, me_ref, big_ref, *refs):
    n_in = len(refs) - 3 - n_out
    in_refs, out_refs = refs[:n_in - n_out], refs[n_in:n_in + n_out]
    cat, acc, sems = refs[-3:]
    step, n_steps = pl.program_id(0), pl.num_programs(0)
    slot = lax.rem(step, 2)
    blk = 512
    unit = cat.shape[0] // (len(rels) * n_out)

    def copies(at_step, at_slot):
        out = []
        wide = pl.ds(pl.multiple_of(at_step * blk, blk), blk)
        for o in range(n_out):
            for j, rel in enumerate(rels):
                part = pl.ds((o * len(rels) + j) * unit, unit)
                place = pl.ds(pl.multiple_of((me_ref[0] ^ rel) * unit, unit), unit)
                if by_rows:
                    src, dst = acc.at[at_slot, part, :], out_refs[o].at[place, wide]
                else:
                    src, dst = acc.at[at_slot, :, part], out_refs[o].at[wide, place]
                out.append(pltpu.make_async_copy(src, dst, sems.at[at_slot, o * len(rels) + j]))
        return out

    @pl.when(step == 0)
    def _():
        row = 0
        for ref in in_refs:
            cat[row:row + ref.shape[0], :] = ref[...]
            row += ref.shape[0]

    @pl.when(step >= 2)
    def _():
        for copy in copies(step - 2, slot):
            copy.wait()

    if by_rows:
        acc[slot] = dot_nn(cat[...], big_ref[...])
    else:
        acc[slot] = dot_nt(big_ref[...], cat[...])
    for copy in copies(step, slot):
        copy.start()

    @pl.when(step == n_steps - 1)
    def _():
        for copy in copies(step - 1, 1 - slot):
            copy.wait()
        for copy in copies(step, slot):
            copy.wait()


def weight_grad(big, parts, rels, me, prev, by_rows, n_out, n_dev):
    seq = big.shape[0] if by_rows else big.shape[1]
    width = big.shape[1] if by_rows else big.shape[0]
    rows = sum(part.shape[0] for part in parts)
    unit = rows // (len(rels) * n_out)
    cols = unit * n_dev
    blk = 512
    shape = (cols, width) if by_rows else (width, cols)
    big_spec = pl.BlockSpec((seq, blk), lambda i, me: (0, i)) if by_rows else pl.BlockSpec((blk, seq), lambda i, me: (i, 0))
    acc_shape = (2, rows, blk) if by_rows else (2, blk, rows)
    prev = [] if prev is None else list(prev)
    any_spec = pl.BlockSpec(memory_space=pl.ANY)
    n_fixed = 2 + len(parts)
    body = functools.partial(wgrad_kernel, by_rows, rels, n_out)
    if not prev:
        inner = body
        body = lambda me_ref, big_ref, *refs: inner(me_ref, big_ref, *refs[:len(parts)], *([None] * n_out), *refs[len(parts):])
    return pl.pallas_call(
        body,
        grid_spec=pltpu.PrefetchScalarGridSpec(
            num_scalar_prefetch=1,
            grid=(width // blk,),
            in_specs=[big_spec] + [pl.BlockSpec(part.shape, lambda i, me: (0, 0), pipeline_mode=pl.Buffered(1)) for part in parts] + [any_spec] * len(prev),
            out_specs=[any_spec] * n_out,
            scratch_shapes=[
                pltpu.VMEM((rows, seq), BF16),
                pltpu.VMEM(acc_shape, F32),
                pltpu.SemaphoreType.DMA((2, len(rels) * n_out)),
            ],
        ),
        out_shape=[jax.ShapeDtypeStruct(shape, F32)] * n_out,
        input_output_aliases={n_fixed + o: o for o in range(len(prev))},
        compiler_params=pltpu.CompilerParams(dimension_semantics=("arbitrary",), vmem_limit_bytes=60 * 1024 * 1024),
        cost_estimate=pl.CostEstimate(flops=2 * rows * width * seq, bytes_accessed=4 * width * rows + 2 * seq * (width + rows), transcendentals=0),
    )(me, big, *parts, *prev)


CORE, SIDE_X, SIDE_Y = 1, 2, 4


def solution(mesh):
    n_dev = mesh.shape["sp"]

    def swap(values, bit):
        return lax.ppermute(values, "sp", [(i, i ^ bit) for i in range(n_dev)])

    def reach(first, second):
        return tuple({0: own, SIDE_X: swap(own, SIDE_X), SIDE_Y: swap(own, SIDE_Y)} for own in (first, second))

    def relay(got):
        one, two = got
        one[SIDE_X | SIDE_Y] = swap(one[SIDE_Y], SIDE_X)
        two[SIDE_X | SIDE_Y] = swap(two[SIDE_X], SIDE_Y)
        for part in got:
            for rel in (0, SIDE_X, SIDE_Y):
                part[rel | CORE] = swap(part[rel], CORE)

    def finish(got, dep=None):
        for part in got:
            far = part[SIDE_X | SIDE_Y]
            part[SIDE_X | SIDE_Y | CORE] = swap(far if dep is None else after(far, dep), CORE)

    def after(value, dep):
        return lax.optimization_barrier((value, dep))[0]

    def hold(got, dep):
        for part in got:
            for rel in (SIDE_X, SIDE_Y):
                part[rel] = after(part[rel], dep)

    def device_body(hidden, grad_out, positions, doc_ids, w_q, w_k, w_v, w_o):
        tokens = hidden.shape[0]
        seq = tokens * n_dev
        group = w_q.shape[1] // w_k.shape[1]
        freqs = rope_freqs()
        me = lax.axis_index("sp").astype(jnp.int32)
        me_arr = me[None]
        idx_all = lax.all_gather(jnp.stack([positions, doc_ids])[None], "sp", axis=0, tiled=True)
        idx_all, hidden, grad_out = lax.optimization_barrier((idx_all, hidden, grad_out))
        pos_all = idx_all[:, 0, :].reshape(seq)
        doc_all = idx_all[:, 1, :].reshape(seq)
        starts = jnp.sum((doc_all[None, :] < doc_all[:, None]).astype(jnp.int32), axis=1)
        first_blk = starts[::BLK] // BLK

        angles = positions.astype(F32)[:, None] * freqs[None, :]
        cos_loc, sin_loc = jnp.cos(angles), jnp.sin(angles)
        cos_tab = jnp.concatenate([cos_loc, cos_loc], axis=1)
        sin_tab = jnp.concatenate([-sin_loc, sin_loc], axis=1)
        angles_t = freqs[:, None] * pos_all.astype(F32)[None, :]
        cos_t, sin_t = jnp.cos(angles_t), jnp.sin(angles_t)

        every = tuple(range(n_dev))
        groups = ((0, 1), (2, 3, 4, 5), (6, 7))

        def pairs(got, rels):
            return [half[r] for r in rels for half in got]

        x_got = reach(hidden, grad_out)
        packed = project(hidden, grad_out, w_q, w_k, w_v, w_o, cos_tab, sin_tab, n_dev, group)
        packed = lax.all_to_all(packed, "sp", 0, 0, tiled=True).reshape(seq, -1)
        ctx_lo, ctx_hi, dq_lo, dq_hi, dk_t, dv_t = attention(packed, first_blk, starts[None, :], cos_t, sin_t, group)
        for rel in (SIDE_X, SIDE_Y):
            x_got[1][rel] = after(x_got[1][rel], dk_t)
        relay(x_got)
        kv_got = reach(dk_t, dv_t)
        ctx_got = reach(ctx_lo, ctx_hi)
        dq_got = reach(dq_lo, dq_hi)
        finish(x_got, dk_t)
        x_turned = assemble([x_got[0][r] for r in every], me_arr, True)
        g_all = assemble([x_got[1][r] for r in every], after(me_arr, x_turned), False)
        hold(kv_got, x_turned)
        relay(kv_got)
        (g_q,) = weight_grad(x_turned, pairs(dq_got, (0,)) + [swap(dq_got[0][0], CORE), swap(dq_got[1][0], CORE)], groups[0], after(me_arr, g_all), None, False, 1, n_dev)
        finish(kv_got, g_q)
        g_k, g_v = weight_grad(x_turned, [kv_got[0][r] for r in every] + [kv_got[1][r] for r in every], every, after(me_arr, g_q), None, False, 2, n_dev)
        hold(ctx_got, g_k)
        relay(ctx_got)
        (g_o,) = weight_grad(g_all, pairs(ctx_got, groups[0]), groups[0], after(me_arr, g_k), None, True, 1, n_dev)
        (g_o,) = weight_grad(g_all, pairs(ctx_got, groups[1]), groups[1], me_arr, (g_o,), True, 1, n_dev)
        finish(ctx_got, g_o)
        hold(dq_got, g_o)
        relay(dq_got)
        (g_o,) = weight_grad(g_all, pairs(ctx_got, groups[2]), groups[2], me_arr, (g_o,), True, 1, n_dev)
        own_ctx = own_columns([[half[r] for half in ctx_got] for r in every], after(me_arr, g_o), tokens)
        attn_out = dot_tn(own_ctx, w_o).astype(BF16)
        (g_q,) = weight_grad(x_turned, pairs(dq_got, groups[1]), groups[1], after(me_arr, attn_out), (g_q,), False, 1, n_dev)
        finish(dq_got, g_q)
        (g_q,) = weight_grad(x_turned, pairs(dq_got, groups[2]), groups[2], me_arr, (g_q,), False, 1, n_dev)
        own_k = own_columns([[kv_got[0][r]] for r in every], after(me_arr, g_k), tokens)
        own_v = own_columns([[kv_got[1][r]] for r in every], after(me_arr, g_k), tokens)
        own_q = own_columns([[half[r] for half in dq_got] for r in every], me_arr, tokens)
        grad_hidden = (dot_tt(own_q, w_q) + dot_tt(own_k, w_k) + dot_tt(own_v, w_v)).astype(BF16)
        g_q, g_o = [g_q], [g_o]
        return attn_out, grad_hidden, g_q[0], g_k, g_v, g_o[0]

    tok_spec = P(("dp", "sp"), None)
    vec_spec = P(("dp", "sp"))
    rep_spec = P(None, None)
    part_spec = P("dp", None)
    return jax.shard_map(device_body, mesh=mesh, in_specs=(tok_spec, tok_spec, vec_spec, vec_spec, rep_spec, rep_spec, rep_spec, rep_spec), out_specs=(tok_spec, tok_spec, part_spec, part_spec, part_spec, part_spec), check_vma=False)
```

time: 1890 us -> 770 us (0.41)
  waiting for transfers between devices: 1080 us -> 297 us
  matrix products: 398 us -> 40.6 us
  Pallas kernels: 0 us -> 344 us
  other arithmetic: 159 us -> 9.8 us
  local copies, waits for them, and re-layouts: 157 us -> 16.7 us
  blocking collectives: 34.7 us -> 10.4 us
    psum x1 -> x0, waiting for transfers between devices: 1080 us -> none  [device_step(): lax.psum((grad_wq, grad_wk, grad_wv, grad_wo), 'sp')]
    dot_general x18 -> x4, matrix products: 398 us -> 40.6 us  [the longest x3 27.9 us: dot_tt(): lax.dot_general(lhs, rhs, (((0,), (1,)), ((), ())), preferred_element_typ...]
    pallas_call x0 -> x15, Pallas kernels: none -> 344 us  [the longest x7 208 us: weight_grad(): pl.pallas_call(body, grid_spec=pltpu.PrefetchScalarGridSpec(num_scalar_pr...]
    ppermute x0 -> x56, waiting for transfers between devices: none -> 297 us  [swap(): return lax.ppermute(values, 'sp', [(i, i ^ bit) for i in range(n_dev)])]
    unnamed x54 -> x60, local copies, waits for them, and re-layouts: 115 us -> 15.2 us
    another operation x5 -> x0, other arithmetic: 96.1 us -> none
    ppermute x0 -> x56, starting transfers between devices: none -> 39.7 us  [swap(): return lax.ppermute(values, 'sp', [(i, i ^ bit) for i in range(n_dev)])]
    reduce_sum x1, other arithmetic: 37.5 us -> 3.81 us  [device_body(): jnp.sum((doc_all[None, :] < doc_all[:, None]).astype(jnp.int32), axis=1)]
  transfers between devices with their start and end apart: 9 -> 57, of which waited for: 2 -> 10; matrix products, arithmetic and copies ran while one was open for 19% -> 4% of each run, Pallas kernels for 0% -> 37%
where the time goes in v1:
time: 770 us; the launch traced here: 765 us
  Pallas kernels  344 us (45%)
  waiting for transfers between devices  297 us (39%)
  starting transfers between devices  45.2 us (6%)
  matrix products  40.6 us (5%)
  local copies, waits for them, and re-layouts  16.7 us (2%)
  blocking collectives  10.4 us (1%)
  other arithmetic  9.8 us (1%)
    ppermute x56, waiting for transfers between devices, swap(): return lax.ppermute(values, 'sp', [(i, i ^ bit) for i in range(n_dev)])  297 us
    pallas_call x7, Pallas kernels, weight_grad(): pl.pallas_call(body, grid_spec=pltpu.PrefetchScalarGridSpec(num_scalar_pr...  208 us
    pallas_call x1, Pallas kernels, attention(): pl.pallas_call(functools.partial(attn_kernel, group), grid_spec=grid_spec...  67.5 us
    ppermute x56, starting transfers between devices, swap(): return lax.ppermute(values, 'sp', [(i, i ^ bit) for i in range(n_dev)])  39.7 us
    pallas_call x1, Pallas kernels, project(): pl.pallas_call(functools.partial(proj_kernel, group), grid=(n_dev,), in_s...  35.1 us
    dot_general x3, matrix products, dot_tt(): lax.dot_general(lhs, rhs, (((0,), (1,)), ((), ())), preferred_element_typ...  27.9 us
    pallas_call x2, Pallas kernels, assemble(): pl.pallas_call(functools.partial(assemble_kernel, turn), grid_spec=pltpu....  27.5 us
  transfers between devices with their start and end apart: 57, of which 10 were waited for; matrix products, arithmetic and copies ran while one was open for 4% of the time, Pallas kernels for 37%

profile of v1, /device:TPU:1, one launch (start us, length us, event | category | flops | bytes accessed | tf_op | source)
XLA Modules:
  0.0 765.2 jit_solution(12066613142843892928)
XLA Ops:
  2.7 10.4 %all-gather.1 = s32[8,2,384]{2,1,0:T(2,128)S(1)} all-gather(s32[1,2,384]{2,1,0:T(2,128)S(1)} %add_bitcast_fusion), channel_id=2, replica_groups=mesh['dp'=2,'sp'=8] {'sp'}, dimensions={0}, use_global_device_ids=true | all-gather | bytes 27648 | tf_op jit(solution)/shard_map/all_gather | solution.py:441
  14.1 1.7 copy-done.9
  15.8 1.7 copy-done.11
  17.4 35.1 %project.1 = bf16[8,384,1024]{2,1,0:T(8,128)(2,1)} custom-call(bf16[384,3072]{1,0:T(8,128)(2,1)S(1)} %copy-done.9, bf16[384,3072]{1,0:T(8,128)(2,1)S(1)} %copy-done.11, bf16[3072,3072]{1,0:T(8,128)(2,1)} %wq_ref.1, bf16[3072,1024]{1,0:T(8,128)(2,1)} %wk_ref.1, bf16[3072,1024]{1,0:T(8,128)(2,1)} %wv_ref.1, bf16[3072,3072]{1,0:T(8,128)(2,1)} %wo_ref.1, ...), custom_call_target="tpu_custom_call" | custom-call | flops 19327352832 | bytes 60000000 | tf_op jit(solution)/shard_map/project/pallas_call | solution.py:72
  52.5 5.5 all-to-all-start
  58.0 1.4 collective-permute-start.3
  59.4 1.2 collective-permute-start.1
  60.6 0.9 collective-permute-start
  61.9 3.8 convert_reduce_fusion
  66.3 3.8 multiply_sine_fusion
  70.1 108.1 %collective-permute-done.3.refs_4_ = bf16[384,3072]{1,0:T(8,128)(2,1)} collective-permute-done((bf16[384,3072]{1,0:T(8,128)(2,1)S(1)}, bf16[384,3072]{1,0:T(8,128)(2,1)}, u32[]{:S(2)}, u32[]{:S(2)}) %collective-permute-start.3) | collective-permute-done | bytes 2359328 | tf_op jit(solution)/shard_map/ppermute | solution.py:408
  178.2 1.6 collective-permute-start.7
  180.8 48.2 %collective-permute-done.8.refs_2_ = bf16[384,3072]{1,0:T(8,128)(2,1)} collective-permute-done((bf16[384,3072]{1,0:T(8,128)(2,1)}, bf16[384,3072]{1,0:T(8,128)(2,1)}, u32[]{:S(2)}, u32[]{:S(2)}) %collective-permute-start.8) | collective-permute-done | bytes 2359328 | tf_op jit(solution)/shard_map/ppermute | solution.py:408
  228.9 1.5 collective-permute-start.2
  230.4 67.5 %attention.1 = (bf16[192,3072]{1,0:T(8,128)(2,1)}, bf16[192,3072]{1,0:T(8,128)(2,1)}, bf16[192,3072]{1,0:T(8,128)(2,1)}, bf16[192,3072]{1,0:T(8,128)(2,1)}, bf16...) custom-call(s32[12]{0:T(128)} %and_select_fusion.lo_ref, bf16[3072,1024]{1,0:T(8,128)(2,1)} %bitcast.3.q_ref.do_ref.k_ref.v_ref, ...), custom_call_target="tpu_custom_call" | custom-call | flops 72477573120 | bytes 12000000 | tf_op jit(solution)/shard_map/attention/pallas_call | solution.py:237
  298.0 1.2 collective-permute-start.12
  300.6 50.5 %collective-permute-done.12.refs_6_ = bf16[384,3072]{1,0:T(8,128)(2,1)} collective-permute-done((bf16[384,3072]{1,0:T(8,128)(2,1)}, bf16[384,3072]{1,0:T(8,128)(2,1)}, u32[]{:S(2)}, u32[]{:S(2)}) %collective-permute-start.12) | collective-permute-done | bytes 2359328 | tf_op jit(solution)/shard_map/ppermute | solution.py:408
  351.1 1.2 collective-permute-start.20
  352.3 15.6 %collective-permute-done.27.refs_12_.refs_4_ = bf16[128,3072]{1,0:T(8,128)(2,1)} collective-permute-done((bf16[128,3072]{1,0:T(8,128)(2,1)}, bf16[128,3072]{1,0:T(8,128)(2,1)}, u32[]{:S(2)}, u32[]{:S(2)}) %collective-permute-start.27) | collective-permute-done | bytes 786464 | tf_op jit(solution)/shard_map/ppermute | solution.py:408
  367.9 1.4 collective-permute-start.11
  369.4 15.4 %collective-permute-done.20.refs_4_ = bf16[128,3072]{1,0:T(8,128)(2,1)} collective-permute-done((bf16[128,3072]{1,0:T(8,128)(2,1)}, bf16[128,3072]{1,0:T(8,128)(2,1)}, u32[]{:S(2)}, u32[]{:S(2)}) %collective-permute-start.20) | collective-permute-done | bytes 786464 | tf_op jit(solution)/shard_map/ppermute | solution.py:408
  385.1 18.2 %collective-permute-done.18.refs_2_ = bf16[128,3072]{1,0:T(8,128)(2,1)} collective-permute-done((bf16[128,3072]{1,0:T(8,128)(2,1)}, bf16[128,3072]{1,0:T(8,128)(2,1)}, u32[]{:S(2)}, u32[]{:S(2)}) %collective-permute-start.18) | collective-permute-done | bytes 786464 | tf_op jit(solution)/shard_map/ppermute | solution.py:408
  403.3 1.8 collective-permute-start.15
  405.1 1.4 copy-done.13
  406.5 1.7 copy-done.14
  408.1 14.4 %shard_map.127.big_ref = bf16[3072,3072]{1,0:T(8,128)(2,1)} custom-call(s32[1]{0:T(128)} %bitcast.me_ref, bf16[384,3072]{1,0:T(8,128)(2,1)S(1)} %copy-done.10, bf16[384,3072]{1,0:T(8,128)(2,1)} %collective-permute-done.refs_1_, bf16[384,3072]{1,0:T(8,128)(2,1)} %collective-permute-done.1.refs_2_, bf16[384,3072]{1,0:T(8,128)(2,1)} %collective-permute-done.2.refs_3_, ...), custom_call_target="tpu_custom_call" | custom-call | bytes 37748736 | tf_op jit(solution)/shard_map/pallas_call | solution.py:273
  422.6 1.3 collective-permute-start.29
  424.7 13.1 %shard_map.128.big_ref = bf16[3072,3072]{1,0:T(8,128)(2,1)} custom-call(s32[1]{0:T(128)} %bitcast.me_ref, bf16[384,3072]{1,0:T(8,128)(2,1)S(1)} %copy-done.12, bf16[384,3072]{1,0:T(8,128)(2,1)} %collective-permute-done.7.refs_1_, bf16[384,3072]{1,0:T(8,128)(2,1)} %collective-permute-done.8.refs_2_, bf16[384,3072]{1,0:T(8,128)(2,1)} %collective-permute-done.9.refs_3_, ...), custom_call_target="tpu_custom_call" | custom-call | bytes 37748736 | tf_op jit(solution)/shard_map/pallas_call | solution.py:273
  438.8 2.7 collective-permute-done.29.refs_14_.refs_6_
  441.8 20.7 %shard_map.129.refs_8_ = f32[3072,3072]{1,0:T(8,128)} custom-call(s32[1]{0:T(128)} %bitcast.me_ref, bf16[3072,3072]{1,0:T(8,128)(2,1)} %shard_map.127.big_ref, bf16[192,3072]{1,0:T(8,128)(2,1)} %get-tuple-element.56.refs_0_, bf16[192,3072]{1,0:T(8,128)(2,1)} %get-tuple-element.57.refs_1_, bf16[192,3072]{1,0:T(8,128)(2,1)} %copy-done.4, ...), custom_call_target="tpu_custom_call" | custom-call | flops 14495514624 | bytes 33030144 | tf_op jit(solution)/shard_map/pallas_call | solution.py:381
  462.5 2.6 collective-permute-start.21
  465.7 1.1 collective-permute-done.37.refs_5_.refs_9_
  466.8 1.4 collective-permute-start.23
  468.7 0.9 collective-permute-start.34
  469.6 1.2 collective-permute-start.14
  470.8 0.9 copy-done.21
  471.7 0.9 collective-permute-start.41
  472.7 0.9 copy-done.25
  474.4 49.6 %shard_map.130 = (f32[3072,1024]{1,0:T(8,128)}, f32[3072,1024]{1,0:T(8,128)}) custom-call(s32[1]{0:T(128)} %bitcast.me_ref, bf16[3072,3072]{1,0:T(8,128)(2,1)} %shard_map.127.big_ref, bf16[128,3072]{1,0:T(8,128)(2,1)} %get-tuple-element.48.refs_0_, bf16[128,3072]{1,0:T(8,128)(2,1)} %collective-permute-done.17.refs_1_, ...), custom_call_target="tpu_custom_call" | custom-call | flops 38654705664 | bytes 56623104 | tf_op jit(solution)/shard_map/pallas_call | solution.py:381
  524.0 0.9 collective-permute-start.48
  526.2 20.5 %shard_map.131.refs_8_ = f32[3072,3072]{1,0:T(8,128)} custom-call(s32[1]{0:T(128)} %bitcast.me_ref, bf16[3072,3072]{1,0:T(8,128)(2,1)} %shard_map.128.big_ref, bf16[192,3072]{1,0:T(8,128)(2,1)} %get-tuple-element.54.refs_0_, bf16[192,3072]{1,0:T(8,128)(2,1)} %get-tuple-element.68.refs_1_, bf16[192,3072]{1,0:T(8,128)(2,1)} %collective-permute-done.40.refs_2_, ...), custom_call_target="tpu_custom_call" | custom-call | flops 14495514624 | bytes 33030144 | tf_op jit(solution)/shard_map/pallas_call | solution.py:381
  548.7 1.1 collective-permute-start.33
  549.7 37.9 %shard_map.132.refs_4_ = f32[3072,3072]{1,0:T(8,128)} custom-call(s32[1]{0:T(128)} %bitcast.me_ref, bf16[3072,3072]{1,0:T(8,128)(2,1)} %shard_map.128.big_ref, bf16[192,3072]{1,0:T(8,128)(2,1)} %collective-permute-done.34.refs_0_.refs_4_, bf16[192,3072]{1,0:T(8,128)(2,1)} %collective-permute-done.32.refs_1_.refs_5_, ...), custom_call_target="tpu_custom_call", output_to_operand_aliasing={{}: (10, {})} | custom-call | flops 28991029248 | bytes 47185920 | tf_op jit(solution)/shard_map/pallas_call | solution.py:381
  587.6 14.3 %collective-permute-done.33.refs_1_.refs_13_ = bf16[192,3072]{1,0:T(8,128)(2,1)} collective-permute-done((bf16[192,3072]{1,0:T(8,128)(2,1)}, bf16[192,3072]{1,0:T(8,128)(2,1)}, u32[]{:S(2)}, u32[]{:S(2)}) %collective-permute-start.33) | collective-permute-done | bytes 1179680 | tf_op jit(solution)/shard_map/ppermute | solution.py:408
  602.6 1.4 collective-permute-start.42
  605.3 23.2 %collective-permute-done.44.refs_0_.refs_4_ = bf16[192,3072]{1,0:T(8,128)(2,1)} collective-permute-done((bf16[192,3072]{1,0:T(8,128)(2,1)S(1)}, bf16[192,3072]{1,0:T(8,128)(2,1)}, u32[]{:S(2)}, u32[]{:S(2)}) %collective-permute-start.44) | collective-permute-done | bytes 1179680 | tf_op jit(solution)/shard_map/ppermute | solution.py:408
  628.4 2.0 collective-permute-start.46
  631.0 20.5 %shard_map.133 = f32[3072,3072]{1,0:T(8,128)} custom-call(s32[1]{0:T(128)} %bitcast.me_ref, bf16[3072,3072]{1,0:T(8,128)(2,1)} %shard_map.128.big_ref, bf16[192,3072]{1,0:T(8,128)(2,1)} %collective-permute-done.31.refs_0_.refs_12_, bf16[192,3072]{1,0:T(8,128)(2,1)} %collective-permute-done.33.refs_1_.refs_13_, ...), custom_call_target="tpu_custom_call", output_to_operand_aliasing={{}: (6, {})} | custom-call | flops 14495514624 | bytes 33030144 | tf_op jit(solution)/shard_map/pallas_call | solution.py:381
  651.4 1.3 copy-done.16
  652.7 1.8 shard_map.134
  654.5 12.6 %convolution_convert_fusion = bf16[384,3072]{1,0:T(8,128)(2,1)} fusion(bf16[3072,384]{1,0:T(8,128)(2,1)S(1)} %shard_map.134, bf16[3072,3072]{1,0:T(8,128)(2,1)} %wo_ref.1), kind=kOutput, calls=%fused_computation.2 | convolution fusion | flops 7248936960 | bytes 23592960 | tf_op jit(solution)/shard_map/dot_general | solution.py:44
  667.8 37.8 %shard_map.135.refs_4_ = f32[3072,3072]{1,0:T(8,128)} custom-call(s32[1]{0:T(128)} %bitcast.me_ref, bf16[3072,3072]{1,0:T(8,128)(2,1)} %shard_map.127.big_ref, bf16[192,3072]{1,0:T(8,128)(2,1)} %collective-permute-done.44.refs_0_.refs_4_, bf16[192,3072]{1,0:T(8,128)(2,1)} %collective-permute-done.45.refs_1_.refs_5_, ...), custom_call_target="tpu_custom_call", output_to_operand_aliasing={{}: (10, {})} | custom-call | flops 28991029248 | bytes 47185920 | tf_op jit(solution)/shard_map/pallas_call | solution.py:381
  706.3 1.2 copy-done.20
  707.5 1.1 copy-done.24
  708.6 1.1 copy-done.26
  709.7 1.2 shard_map.138
  711.1 1.2 shard_map.137
  712.3 7.7 %fusion.2 = f32[384,3072]{1,0:T(8,128)} fusion(bf16[1024,384]{1,0:T(8,128)(2,1)S(1)} %shard_map.137, bf16[3072,1024]{1,0:T(8,128)(2,1)} %wk_ref.1), kind=kOutput, calls=%fused_computation.19 | convolution fusion | flops 2415919104 | bytes 11796480 | tf_op jit(solution)/shard_map/dot_general | solution.py:48
  720.1 1.8 shard_map.136
  721.9 1.0 copy-done.7
  722.9 1.1 copy-done.8
  724.0 13.5 %fusion.1 = f32[384,3072]{1,0:T(8,128)} fusion(bf16[3072,384]{1,0:T(8,128)(2,1)S(1)} %shard_map.136, bf16[3072,3072]{1,0:T(8,128)(2,1)} %wq_ref.1), kind=kOutput, calls=%fused_computation.18 | convolution fusion | flops 7247757312 | bytes 25952256 | tf_op jit(solution)/shard_map/dot_general | solution.py:48
  737.5 6.7 add_convert_fusion
  744.2 20.7 %shard_map.139 = f32[3072,3072]{1,0:T(8,128)} custom-call(s32[1]{0:T(128)} %bitcast.me_ref, bf16[3072,3072]{1,0:T(8,128)(2,1)} %shard_map.127.big_ref, bf16[192,3072]{1,0:T(8,128)(2,1)} %copy-done.6, bf16[192,3072]{1,0:T(8,128)(2,1)} %collective-permute-done.53.refs_13_.refs_1_, bf16[192,3072]{1,0:T(8,128)(2,1)} %copy-done.7, ...), custom_call_target="tpu_custom_call", output_to_operand_aliasing={{}: (6, {})} | custom-call | flops 14495514624 | bytes 33030144 | tf_op jit(solution)/shard_map/pallas_call | solution.py:381
  (143 shorter events, 17.7 us)
Async XLA Ops:
  52.5 177.9 %all-to-all-start = ((bf16[8,384,1024]{2,1,0:T(8,128)(2,1)}), bf16[8,384,1024]{2,1,0:T(8,128)(2,1)}, u32[]{:S(2)}, u32[]{:S(2)}) async-start(bf16[8,384,1024]{2,1,0:T(8,128)(2,1)} %project.1), calls=%async_computation | async-start | bytes 12582912 | tf_op jit(solution)/shard_map/all_to_all | solution.py:463
  58.0 120.2 %collective-permute-start.3 = (bf16[384,3072]{1,0:T(8,128)(2,1)S(1)}, bf16[384,3072]{1,0:T(8,128)(2,1)}, u32[]{:S(2)}, u32[]{:S(2)}) collective-permute-start(bf16[384,3072]{1,0:T(8,128)(2,1)S(1)} %copy-done.10), channel_id=1, source_target_pairs={{0,4},{1,5},{2,6},{3,7},{4,0},{5,1},{6,2},{7,3},{8,12},{9,13},{10,... | collective-permute-start | bytes 7077896 | tf_op jit(solution)/shard_map/ppermute | solution.py:408
  59.4 120.4 %collective-permute-start.1 = (bf16[384,3072]{1,0:T(8,128)(2,1)S(1)}, bf16[384,3072]{1,0:T(8,128)(2,1)}, u32[]{:S(2)}, u32[]{:S(2)}) collective-permute-start(bf16[384,3072]{1,0:T(8,128)(2,1)S(1)} %copy-done.10), channel_id=1, source_target_pairs={{0,2},{1,3},{2,0},{3,1},{4,6},{5,7},{6,4},{7,5},{8,10},{9,11},{10,... | collective-permute-start | bytes 7077896 | tf_op jit(solution)/shard_map/ppermute | solution.py:408
  60.6 119.9 %collective-permute-start = (bf16[384,3072]{1,0:T(8,128)(2,1)S(1)}, bf16[384,3072]{1,0:T(8,128)(2,1)}, u32[]{:S(2)}, u32[]{:S(2)}) collective-permute-start(bf16[384,3072]{1,0:T(8,128)(2,1)S(1)} %copy-done.10), channel_id=1, source_target_pairs={{0,1},{1,0},{2,3},{3,2},{4,5},{5,4},{6,7},{7,6},{8,9},{9,8},{10,11... | collective-permute-start | bytes 7077896 | tf_op jit(solution)/shard_map/ppermute | solution.py:408
  61.6 167.4 %collective-permute-start.8 = (bf16[384,3072]{1,0:T(8,128)(2,1)}, bf16[384,3072]{1,0:T(8,128)(2,1)}, u32[]{:S(2)}, u32[]{:S(2)}) collective-permute-start(bf16[384,3072]{1,0:T(8,128)(2,1)} %refs_0_.1), channel_id=1, source_target_pairs={{0,2},{1,3},{2,0},{3,1},{4,6},{5,7},{6,4},{7,5},{8,10},{9,11},{10,... | collective-permute-start | bytes 7077896 | tf_op jit(solution)/shard_map/ppermute | solution.py:408
  61.8 237.4 %collective-permute-start.10 = (bf16[384,3072]{1,0:T(8,128)(2,1)}, bf16[384,3072]{1,0:T(8,128)(2,1)}, u32[]{:S(2)}, u32[]{:S(2)}) collective-permute-start(bf16[384,3072]{1,0:T(8,128)(2,1)} %refs_0_.1), channel_id=1, source_target_pairs={{0,4},{1,5},{2,6},{3,7},{4,0},{5,1},{6,2},{7,3},{8,12},{9,13},{10,... | collective-permute-start | bytes 7077896 | tf_op jit(solution)/shard_map/ppermute | solution.py:408
  65.7 164.8 %copy-start.27 = (s32[3072]{0:T(1024)}, s32[3072]{0:T(1024)S(1)}, u32[]{:S(2)}) copy-start(s32[3072]{0:T(1024)S(1)} %convert_reduce_fusion) | copy-start | bytes 36868
  178.2 121.3 %collective-permute-start.7 = (bf16[384,3072]{1,0:T(8,128)(2,1)}, bf16[384,3072]{1,0:T(8,128)(2,1)}, u32[]{:S(2)}, u32[]{:S(2)}) collective-permute-start(bf16[384,3072]{1,0:T(8,128)(2,1)} %refs_0_.1), channel_id=1, source_target_pairs={{0,1},{1,0},{2,3},{3,2},{4,5},{5,4},{6,7},{7,6},{8,9},{9,8},{10,11... | collective-permute-start | bytes 7077896 | tf_op jit(solution)/shard_map/ppermute | solution.py:408
  179.8 118.1 %collective-permute-start.5 = (bf16[384,3072]{1,0:T(8,128)(2,1)}, bf16[384,3072]{1,0:T(8,128)(2,1)}, u32[]{:S(2)}, u32[]{:S(2)}) collective-permute-start(bf16[384,3072]{1,0:T(8,128)(2,1)} %collective-permute-done.3.refs_4_), channel_id=1, source_target_pairs={{0,2},{1,3},{2,0},{3,1},{4,6},{5,7},{6,4},{7,5},{8,10},{9,11},{10,... | collective-permute-start | bytes 7077896 | tf_op jit(solution)/shard_map/ppermute | solution.py:408
  180.5 119.4 %collective-permute-start.4 = (bf16[384,3072]{1,0:T(8,128)(2,1)}, bf16[384,3072]{1,0:T(8,128)(2,1)}, u32[]{:S(2)}, u32[]{:S(2)}) collective-permute-start(bf16[384,3072]{1,0:T(8,128)(2,1)} %collective-permute-done.3.refs_4_), channel_id=1, source_target_pairs={{0,1},{1,0},{2,3},{3,2},{4,5},{5,4},{6,7},{7,6},{8,9},{9,8},{10,11... | collective-permute-start | bytes 7077896 | tf_op jit(solution)/shard_map/ppermute | solution.py:408
  228.9 70.9 %collective-permute-start.2 = (bf16[384,3072]{1,0:T(8,128)(2,1)}, bf16[384,3072]{1,0:T(8,128)(2,1)}, u32[]{:S(2)}, u32[]{:S(2)}) collective-permute-start(bf16[384,3072]{1,0:T(8,128)(2,1)} %collective-permute-done.1.refs_2_), channel_id=1, source_target_pairs={{0,1},{1,0},{2,3},{3,2},{4,5},{5,4},{6,7},{7,6},{8,9},{9,8},{10,11... | collective-permute-start | bytes 7077896 | tf_op jit(solution)/shard_map/ppermute | solution.py:408
  298.0 53.1 %collective-permute-start.12 = (bf16[384,3072]{1,0:T(8,128)(2,1)}, bf16[384,3072]{1,0:T(8,128)(2,1)}, u32[]{:S(2)}, u32[]{:S(2)}) collective-permute-start(bf16[384,3072]{1,0:T(8,128)(2,1)} %collective-permute-done.8.refs_2_), channel_id=1, source_target_pairs={{0,4},{1,5},{2,6},{3,7},{4,0},{5,1},{6,2},{7,3},{8,12},{9,13},{10,... | collective-permute-start | bytes 7077896 | tf_op jit(solution)/shard_map/ppermute | solution.py:408
  299.2 105.8 %collective-permute-start.6 = (bf16[384,3072]{1,0:T(8,128)(2,1)}, bf16[384,3072]{1,0:T(8,128)(2,1)S(1)}, u32[]{:S(2)}, u32[]{:S(2)}) collective-permute-start(bf16[384,3072]{1,0:T(8,128)(2,1)} %collective-permute-done.5.refs_6_), channel_id=1, source_target_pairs={{0,1},{1,0},{2,3},{3,2},{4,5},{5,4},{6,7},{7,6},{8,9},{9,8},{10,11... | collective-permute-start | bytes 7077896 | tf_op jit(solution)/shard_map/ppermute | solution.py:408
  299.5 68.4 %collective-permute-start.27 = (bf16[128,3072]{1,0:T(8,128)(2,1)}, bf16[128,3072]{1,0:T(8,128)(2,1)}, u32[]{:S(2)}, u32[]{:S(2)}) collective-permute-start(bf16[128,3072]{1,0:T(8,128)(2,1)} %get-tuple-element.62.refs_8_.refs_0_), channel_id=1, source_target_pairs={{0,4},{1,5},{2,6},{3,7},{4,0},{5,1},{6,2},{7,3},{8,12},{9,13},{10,... | collective-permute-start | bytes 2359304 | tf_op jit(solution)/shard_map/ppermute | solution.py:408
  299.8 69.5 %collective-permute-start.25 = (bf16[128,3072]{1,0:T(8,128)(2,1)}, bf16[128,3072]{1,0:T(8,128)(2,1)}, u32[]{:S(2)}, u32[]{:S(2)}) collective-permute-start(bf16[128,3072]{1,0:T(8,128)(2,1)} %get-tuple-element.62.refs_8_.refs_0_), channel_id=1, source_target_pairs={{0,2},{1,3},{2,0},{3,1},{4,6},{5,7},{6,4},{7,5},{8,10},{9,11},{10,... | collective-permute-start | bytes 2359304 | tf_op jit(solution)/shard_map/ppermute | solution.py:408
  299.8 122.7 %collective-permute-start.9 = (bf16[384,3072]{1,0:T(8,128)(2,1)}, bf16[384,3072]{1,0:T(8,128)(2,1)}, u32[]{:S(2)}, u32[]{:S(2)}) collective-permute-start(bf16[384,3072]{1,0:T(8,128)(2,1)} %collective-permute-done.8.refs_2_), channel_id=1, source_target_pairs={{0,1},{1,0},{2,3},{3,2},{4,5},{5,4},{6,7},{7,6},{8,9},{9,8},{10,11... | collective-permute-start | bytes 7077896 | tf_op jit(solution)/shard_map/ppermute | solution.py:408
  351.1 33.7 %collective-permute-start.20 = (bf16[128,3072]{1,0:T(8,128)(2,1)}, bf16[128,3072]{1,0:T(8,128)(2,1)}, u32[]{:S(2)}, u32[]{:S(2)}) collective-permute-start(bf16[128,3072]{1,0:T(8,128)(2,1)} %get-tuple-element.48.refs_0_), channel_id=1, source_target_pairs={{0,4},{1,5},{2,6},{3,7},{4,0},{5,1},{6,2},{7,3},{8,12},{9,13},{10,... | collective-permute-start | bytes 2359304 | tf_op jit(solution)/shard_map/ppermute | solution.py:408
  367.9 55.9 %collective-permute-start.11 = (bf16[384,3072]{1,0:T(8,128)(2,1)}, bf16[384,3072]{1,0:T(8,128)(2,1)}, u32[]{:S(2)}, u32[]{:S(2)}) collective-permute-start(bf16[384,3072]{1,0:T(8,128)(2,1)} %collective-permute-done.10.refs_4_), channel_id=1, source_target_pairs={{0,1},{1,0},{2,3},{3,2},{4,5},{5,4},{6,7},{7,6},{8,9},{9,8},{10,11... | collective-permute-start | bytes 7077896 | tf_op jit(solution)/shard_map/ppermute | solution.py:408
  369.4 55.2 %collective-permute-start.13 = (bf16[384,3072]{1,0:T(8,128)(2,1)}, bf16[384,3072]{1,0:T(8,128)(2,1)}, u32[]{:S(2)}, u32[]{:S(2)}) collective-permute-start(bf16[384,3072]{1,0:T(8,128)(2,1)} %collective-permute-done.12.refs_6_), channel_id=1, source_target_pairs={{0,1},{1,0},{2,3},{3,2},{4,5},{5,4},{6,7},{7,6},{8,9},{9,8},{10,11... | collective-permute-start | bytes 7077896 | tf_op jit(solution)/shard_map/ppermute | solution.py:408
  384.8 18.5 %collective-permute-start.18 = (bf16[128,3072]{1,0:T(8,128)(2,1)}, bf16[128,3072]{1,0:T(8,128)(2,1)}, u32[]{:S(2)}, u32[]{:S(2)}) collective-permute-start(bf16[128,3072]{1,0:T(8,128)(2,1)} %get-tuple-element.48.refs_0_), channel_id=1, source_target_pairs={{0,2},{1,3},{2,0},{3,1},{4,6},{5,7},{6,4},{7,5},{8,10},{9,11},{10,... | collective-permute-start | bytes 2359304 | tf_op jit(solution)/shard_map/ppermute | solution.py:408
  403.3 34.5 %collective-permute-start.15 = (bf16[192,3072]{1,0:T(8,128)(2,1)}, bf16[192,3072]{1,0:T(8,128)(2,1)S(1)}, u32[]{:S(2)}, u32[]{:S(2)}) collective-permute-start(bf16[192,3072]{1,0:T(8,128)(2,1)} %get-tuple-element.56.refs_0_), channel_id=1, source_target_pairs={{0,1},{1,0},{2,3},{3,2},{4,5},{5,4},{6,7},{7,6},{8,9},{9,8},{10,11... | collective-permute-start | bytes 3538952 | tf_op jit(solution)/shard_map/ppermute | solution.py:408
  406.5 31.6 %collective-permute-start.16 = (bf16[192,3072]{1,0:T(8,128)(2,1)}, bf16[192,3072]{1,0:T(8,128)(2,1)}, u32[]{:S(2)}, u32[]{:S(2)}) collective-permute-start(bf16[192,3072]{1,0:T(8,128)(2,1)} %get-tuple-element.57.refs_1_), channel_id=1, source_target_pairs={{0,1},{1,0},{2,3},{3,2},{4,5},{5,4},{6,7},{7,6},{8,9},{9,8},{10,11... | collective-permute-start | bytes 3538952 | tf_op jit(solution)/shard_map/ppermute | solution.py:408
  408.1 16.5 %copy-start.12 = (bf16[384,3072]{1,0:T(8,128)(2,1)S(1)}, bf16[384,3072]{1,0:T(8,128)(2,1)}, u32[]{:S(2)}) copy-start(bf16[384,3072]{1,0:T(8,128)(2,1)} %refs_0_.1) | copy-start | bytes 7077892
  422.6 18.9 %collective-permute-start.29 = (bf16[128,3072]{1,0:T(8,128)(2,1)}, bf16[128,3072]{1,0:T(8,128)(2,1)}, u32[]{:S(2)}, u32[]{:S(2)}) collective-permute-start(bf16[128,3072]{1,0:T(8,128)(2,1)} %collective-permute-done.25.refs_10_.refs_2_), channel_id=1, source_target_pairs={{0,4},{1,5},{2,6},{3,7},{4,0},{5,1},{6,2},{7,3},{8,12},{9,13},{10,... | collective-permute-start | bytes 2359304 | tf_op jit(solution)/shard_map/ppermute | solution.py:408
  423.8 41.3 %collective-permute-start.24 = (bf16[128,3072]{1,0:T(8,128)(2,1)}, bf16[128,3072]{1,0:T(8,128)(2,1)}, u32[]{:S(2)}, u32[]{:S(2)}) collective-permute-start(bf16[128,3072]{1,0:T(8,128)(2,1)} %get-tuple-element.62.refs_8_.refs_0_), channel_id=1, source_target_pairs={{0,1},{1,0},{2,3},{3,2},{4,5},{5,4},{6,7},{7,6},{8,9},{9,8},{10,11... | collective-permute-start | bytes 2359304 | tf_op jit(solution)/shard_map/ppermute | solution.py:408
  424.6 40.6 %collective-permute-start.17 = (bf16[128,3072]{1,0:T(8,128)(2,1)}, bf16[128,3072]{1,0:T(8,128)(2,1)}, u32[]{:S(2)}, u32[]{:S(2)}) collective-permute-start(bf16[128,3072]{1,0:T(8,128)(2,1)} %get-tuple-element.48.refs_0_), channel_id=1, source_target_pairs={{0,1},{1,0},{2,3},{3,2},{4,5},{5,4},{6,7},{7,6},{8,9},{9,8},{10,11... | collective-permute-start | bytes 2359304 | tf_op jit(solution)/shard_map/ppermute | solution.py:408
  437.8 30.4 %copy-start.2 = (bf16[192,3072]{1,0:T(8,128)(2,1)S(1)}, bf16[192,3072]{1,0:T(8,128)(2,1)}, u32[]{:S(2)}) copy-start(bf16[192,3072]{1,0:T(8,128)(2,1)} %get-tuple-element.54.refs_0_) | copy-start | bytes 3538948
  437.8 29.0 %collective-permute-start.37 = (bf16[192,3072]{1,0:T(8,128)(2,1)}, bf16[192,3072]{1,0:T(8,128)(2,1)}, u32[]{:S(2)}, u32[]{:S(2)}) collective-permute-start(bf16[192,3072]{1,0:T(8,128)(2,1)} %get-tuple-element.68.refs_1_), channel_id=1, source_target_pairs={{0,4},{1,5},{2,6},{3,7},{4,0},{5,1},{6,2},{7,3},{8,12},{9,13},{10,... | collective-permute-start | bytes 3538952 | tf_op jit(solution)/shard_map/ppermute | solution.py:408
  438.1 30.1 %collective-permute-start.19 = (bf16[128,3072]{1,0:T(8,128)(2,1)}, bf16[128,3072]{1,0:T(8,128)(2,1)}, u32[]{:S(2)}, u32[]{:S(2)}) collective-permute-start(bf16[128,3072]{1,0:T(8,128)(2,1)} %collective-permute-done.18.refs_2_), channel_id=1, source_target_pairs={{0,1},{1,0},{2,3},{3,2},{4,5},{5,4},{6,7},{7,6},{8,9},{9,8},{10,11... | collective-permute-start | bytes 2359304 | tf_op jit(solution)/shard_map/ppermute | solution.py:408
  441.5 21.0 %collective-permute-start.22 = (bf16[128,3072]{1,0:T(8,128)(2,1)}, bf16[128,3072]{1,0:T(8,128)(2,1)}, u32[]{:S(2)}, u32[]{:S(2)}) collective-permute-start(bf16[128,3072]{1,0:T(8,128)(2,1)} %collective-permute-done.20.refs_4_), channel_id=1, source_target_pairs={{0,2},{1,3},{2,0},{3,1},{4,6},{5,7},{6,4},{7,5},{8,10},{9,11},{10,... | collective-permute-start | bytes 2359304 | tf_op jit(solution)/shard_map/ppermute | solution.py:408
  462.5 5.7 collective-permute-start.21
  465.1 3.6 collective-permute-start.26
  465.2 4.4 collective-permute-start.28
  466.8 4.0 collective-permute-start.23
  468.2 4.5 collective-permute-start.30
  468.2 55.8 %copy-start = (bf16[192,3072]{1,0:T(8,128)(2,1)S(1)}, bf16[192,3072]{1,0:T(8,128)(2,1)}, u32[]{:S(2)}) copy-start(bf16[192,3072]{1,0:T(8,128)(2,1)} %get-tuple-element.56.refs_0_) | copy-start | bytes 3538948
  468.2 57.5 %collective-permute-start.40 = (bf16[192,3072]{1,0:T(8,128)(2,1)S(1)}, bf16[192,3072]{1,0:T(8,128)(2,1)}, u32[]{:S(2)}, u32[]{:S(2)}) collective-permute-start(bf16[192,3072]{1,0:T(8,128)(2,1)S(1)} %copy-done.2), channel_id=1, source_target_pairs={{0,1},{1,0},{2,3},{3,2},{4,5},{5,4},{6,7},{7,6},{8,9},{9,8},{10,11... | collective-permute-start | bytes 3538952 | tf_op jit(solution)/shard_map/ppermute | solution.py:408
  468.7 55.3 %collective-permute-start.34 = (bf16[192,3072]{1,0:T(8,128)(2,1)S(1)}, bf16[192,3072]{1,0:T(8,128)(2,1)}, u32[]{:S(2)}, u32[]{:S(2)}) collective-permute-start(bf16[192,3072]{1,0:T(8,128)(2,1)S(1)} %copy-done.2), channel_id=1, source_target_pairs={{0,2},{1,3},{2,0},{3,1},{4,6},{5,7},{6,4},{7,5},{8,10},{9,11},{10,... | collective-permute-start | bytes 3538952 | tf_op jit(solution)/shard_map/ppermute | solution.py:408
  469.6 55.3 %collective-permute-start.14 = (bf16[192,3072]{1,0:T(8,128)(2,1)S(1)}, bf16[192,3072]{1,0:T(8,128)(2,1)}, u32[]{:S(2)}, u32[]{:S(2)}) collective-permute-start(bf16[192,3072]{1,0:T(8,128)(2,1)S(1)} %copy-done.2), channel_id=1, source_target_pairs={{0,4},{1,5},{2,6},{3,7},{4,0},{5,1},{6,2},{7,3},{8,12},{9,13},{10,... | collective-permute-start | bytes 3538952 | tf_op jit(solution)/shard_map/ppermute | solution.py:408
  471.7 54.5 %collective-permute-start.41 = (bf16[192,3072]{1,0:T(8,128)(2,1)}, bf16[192,3072]{1,0:T(8,128)(2,1)}, u32[]{:S(2)}, u32[]{:S(2)}) collective-permute-start(bf16[192,3072]{1,0:T(8,128)(2,1)} %get-tuple-element.68.refs_1_), channel_id=1, source_target_pairs={{0,1},{1,0},{2,3},{3,2},{4,5},{5,4},{6,7},{7,6},{8,9},{9,8},{10,11... | collective-permute-start | bytes 3538952 | tf_op jit(solution)/shard_map/ppermute | solution.py:408
  473.5 51.3 %collective-permute-start.32 = (bf16[192,3072]{1,0:T(8,128)(2,1)}, bf16[192,3072]{1,0:T(8,128)(2,1)}, u32[]{:S(2)}, u32[]{:S(2)}) collective-permute-start(bf16[192,3072]{1,0:T(8,128)(2,1)} %get-tuple-element.68.refs_1_), channel_id=1, source_target_pairs={{0,2},{1,3},{2,0},{3,1},{4,6},{5,7},{6,4},{7,5},{8,10},{9,11},{10,... | collective-permute-start | bytes 3538952 | tf_op jit(solution)/shard_map/ppermute | solution.py:408
  524.0 22.7 %copy-start.1 = (bf16[192,3072]{1,0:T(8,128)(2,1)S(1)}, bf16[192,3072]{1,0:T(8,128)(2,1)}, u32[]{:S(2)}) copy-start(bf16[192,3072]{1,0:T(8,128)(2,1)} %get-tuple-element.57.refs_1_) | copy-start | bytes 3538948
  524.0 80.5 %collective-permute-start.48 = (bf16[192,3072]{1,0:T(8,128)(2,1)S(1)}, bf16[192,3072]{1,0:T(8,128)(2,1)}, u32[]{:S(2)}, u32[]{:S(2)}) collective-permute-start(bf16[192,3072]{1,0:T(8,128)(2,1)S(1)} %copy-done), channel_id=1, source_target_pairs={{0,4},{1,5},{2,6},{3,7},{4,0},{5,1},{6,2},{7,3},{8,12},{9,13},{10,... | collective-permute-start | bytes 3538952 | tf_op jit(solution)/shard_map/ppermute | solution.py:408
  524.9 21.8 %collective-permute-start.38 = (bf16[192,3072]{1,0:T(8,128)(2,1)}, bf16[192,3072]{1,0:T(8,128)(2,1)}, u32[]{:S(2)}, u32[]{:S(2)}) collective-permute-start(bf16[192,3072]{1,0:T(8,128)(2,1)} %collective-permute-done.14.refs_4_.refs_8_), channel_id=1, source_target_pairs={{0,1},{1,0},{2,3},{3,2},{4,5},{5,4},{6,7},{7,6},{8,9},{9,8},{10,11... | collective-permute-start | bytes 3538952 | tf_op jit(solution)/shard_map/ppermute | solution.py:408
  525.7 21.5 %collective-permute-start.36 = (bf16[192,3072]{1,0:T(8,128)(2,1)}, bf16[192,3072]{1,0:T(8,128)(2,1)}, u32[]{:S(2)}, u32[]{:S(2)}) collective-permute-start(bf16[192,3072]{1,0:T(8,128)(2,1)} %collective-permute-done.32.refs_1_.refs_5_), channel_id=1, source_target_pairs={{0,1},{1,0},{2,3},{3,2},{4,5},{5,4},{6,7},{7,6},{8,9},{9,8},{10,11... | collective-permute-start | bytes 3538952 | tf_op jit(solution)/shard_map/ppermute | solution.py:408
  525.7 22.1 %collective-permute-start.35 = (bf16[192,3072]{1,0:T(8,128)(2,1)}, bf16[192,3072]{1,0:T(8,128)(2,1)S(1)}, u32[]{:S(2)}, u32[]{:S(2)}) collective-permute-start(bf16[192,3072]{1,0:T(8,128)(2,1)} %collective-permute-done.34.refs_0_.refs_4_), channel_id=1, source_target_pairs={{0,1},{1,0},{2,3},{3,2},{4,5},{5,4},{6,7},{7,6},{8,9},{9,8},{10,11... | collective-permute-start | bytes 3538952 | tf_op jit(solution)/shard_map/ppermute | solution.py:408
  526.2 22.5 %collective-permute-start.39 = (bf16[192,3072]{1,0:T(8,128)(2,1)}, bf16[192,3072]{1,0:T(8,128)(2,1)}, u32[]{:S(2)}, u32[]{:S(2)}) collective-permute-start(bf16[192,3072]{1,0:T(8,128)(2,1)} %collective-permute-done.37.refs_5_.refs_9_), channel_id=1, source_target_pairs={{0,1},{1,0},{2,3},{3,2},{4,5},{5,4},{6,7},{7,6},{8,9},{9,8},{10,11... | collective-permute-start | bytes 3538952 | tf_op jit(solution)/shard_map/ppermute | solution.py:408
  546.7 57.3 %collective-permute-start.49 = (bf16[192,3072]{1,0:T(8,128)(2,1)S(1)}, bf16[192,3072]{1,0:T(8,128)(2,1)}, u32[]{:S(2)}, u32[]{:S(2)}) collective-permute-start(bf16[192,3072]{1,0:T(8,128)(2,1)S(1)} %copy-done.1), channel_id=1, source_target_pairs={{0,4},{1,5},{2,6},{3,7},{4,0},{5,1},{6,2},{7,3},{8,12},{9,13},{10,... | collective-permute-start | bytes 3538952 | tf_op jit(solution)/shard_map/ppermute | solution.py:408
  547.2 56.9 %collective-permute-start.45 = (bf16[192,3072]{1,0:T(8,128)(2,1)S(1)}, bf16[192,3072]{1,0:T(8,128)(2,1)}, u32[]{:S(2)}, u32[]{:S(2)}) collective-permute-start(bf16[192,3072]{1,0:T(8,128)(2,1)S(1)} %copy-done.1), channel_id=1, source_target_pairs={{0,2},{1,3},{2,0},{3,1},{4,6},{5,7},{6,4},{7,5},{8,10},{9,11},{10,... | collective-permute-start | bytes 3538952 | tf_op jit(solution)/shard_map/ppermute | solution.py:408
  547.8 54.8 %collective-permute-start.31 = (bf16[192,3072]{1,0:T(8,128)(2,1)}, bf16[192,3072]{1,0:T(8,128)(2,1)}, u32[]{:S(2)}, u32[]{:S(2)}) collective-permute-start(bf16[192,3072]{1,0:T(8,128)(2,1)} %collective-permute-done.14.refs_4_.refs_8_), channel_id=1, source_target_pairs={{0,2},{1,3},{2,0},{3,1},{4,6},{5,7},{6,4},{7,5},{8,10},{9,11},{10,... | collective-permute-start | bytes 3538952 | tf_op jit(solution)/shard_map/ppermute | solution.py:408
  548.7 53.3 %collective-permute-start.33 = (bf16[192,3072]{1,0:T(8,128)(2,1)}, bf16[192,3072]{1,0:T(8,128)(2,1)}, u32[]{:S(2)}, u32[]{:S(2)}) collective-permute-start(bf16[192,3072]{1,0:T(8,128)(2,1)} %collective-permute-done.32.refs_1_.refs_5_), channel_id=1, source_target_pairs={{0,4},{1,5},{2,6},{3,7},{4,0},{5,1},{6,2},{7,3},{8,12},{9,13},{10,... | collective-permute-start | bytes 3538952 | tf_op jit(solution)/shard_map/ppermute | solution.py:408
  587.6 63.8 %copy-start.3 = (bf16[192,3072]{1,0:T(8,128)(2,1)S(1)}, bf16[192,3072]{1,0:T(8,128)(2,1)}, u32[]{:S(2)}) copy-start(bf16[192,3072]{1,0:T(8,128)(2,1)} %get-tuple-element.54.refs_0_) | copy-start | bytes 3538948
  601.9 26.5 %collective-permute-start.44 = (bf16[192,3072]{1,0:T(8,128)(2,1)S(1)}, bf16[192,3072]{1,0:T(8,128)(2,1)}, u32[]{:S(2)}, u32[]{:S(2)}) collective-permute-start(bf16[192,3072]{1,0:T(8,128)(2,1)S(1)} %copy-done), channel_id=1, source_target_pairs={{0,2},{1,3},{2,0},{3,1},{4,6},{5,7},{6,4},{7,5},{8,10},{9,11},{10,... | collective-permute-start | bytes 3538952 | tf_op jit(solution)/shard_map/ppermute | solution.py:408
  602.6 27.9 %collective-permute-start.42 = (bf16[192,3072]{1,0:T(8,128)(2,1)}, bf16[192,3072]{1,0:T(8,128)(2,1)}, u32[]{:S(2)}, u32[]{:S(2)}) collective-permute-start(bf16[192,3072]{1,0:T(8,128)(2,1)} %collective-permute-done.31.refs_0_.refs_12_), channel_id=1, source_target_pairs={{0,1},{1,0},{2,3},{3,2},{4,5},{5,4},{6,7},{7,6},{8,9},{9,8},{10,11... | collective-permute-start | bytes 3538952 | tf_op jit(solution)/shard_map/ppermute | solution.py:408
  604.0 26.4 %collective-permute-start.43 = (bf16[192,3072]{1,0:T(8,128)(2,1)}, bf16[192,3072]{1,0:T(8,128)(2,1)}, u32[]{:S(2)}, u32[]{:S(2)}) collective-permute-start(bf16[192,3072]{1,0:T(8,128)(2,1)} %collective-permute-done.33.refs_1_.refs_13_), channel_id=1, source_target_pairs={{0,1},{1,0},{2,3},{3,2},{4,5},{5,4},{6,7},{7,6},{8,9},{9,8},{10,11... | collective-permute-start | bytes 3538952 | tf_op jit(solution)/shard_map/ppermute | solution.py:408
  604.1 101.6 %collective-permute-start.53 = (bf16[192,3072]{1,0:T(8,128)(2,1)}, bf16[192,3072]{1,0:T(8,128)(2,1)}, u32[]{:S(2)}, u32[]{:S(2)}) collective-permute-start(bf16[192,3072]{1,0:T(8,128)(2,1)} %collective-permute-done.45.refs_1_.refs_5_), channel_id=1, source_target_pairs={{0,4},{1,5},{2,6},{3,7},{4,0},{5,1},{6,2},{7,3},{8,12},{9,13},{10,... | collective-permute-start | bytes 3538952 | tf_op jit(solution)/shard_map/ppermute | solution.py:408
  604.5 63.3 %collective-permute-start.47 = (bf16[192,3072]{1,0:T(8,128)(2,1)}, bf16[192,3072]{1,0:T(8,128)(2,1)}, u32[]{:S(2)}, u32[]{:S(2)}) collective-permute-start(bf16[192,3072]{1,0:T(8,128)(2,1)} %collective-permute-done.45.refs_1_.refs_5_), channel_id=1, source_target_pairs={{0,1},{1,0},{2,3},{3,2},{4,5},{5,4},{6,7},{7,6},{8,9},{9,8},{10,11... | collective-permute-start | bytes 3538952 | tf_op jit(solution)/shard_map/ppermute | solution.py:408
  628.4 38.7 %collective-permute-start.46 = (bf16[192,3072]{1,0:T(8,128)(2,1)}, bf16[192,3072]{1,0:T(8,128)(2,1)}, u32[]{:S(2)}, u32[]{:S(2)}) collective-permute-start(bf16[192,3072]{1,0:T(8,128)(2,1)} %collective-permute-done.44.refs_0_.refs_4_), channel_id=1, source_target_pairs={{0,1},{1,0},{2,3},{3,2},{4,5},{5,4},{6,7},{7,6},{8,9},{9,8},{10,11... | collective-permute-start | bytes 3538952 | tf_op jit(solution)/shard_map/ppermute | solution.py:408
  630.4 37.4 %collective-permute-start.50 = (bf16[192,3072]{1,0:T(8,128)(2,1)}, bf16[192,3072]{1,0:T(8,128)(2,1)}, u32[]{:S(2)}, u32[]{:S(2)}) collective-permute-start(bf16[192,3072]{1,0:T(8,128)(2,1)} %collective-permute-done.48.refs_4_.refs_8_), channel_id=1, source_target_pairs={{0,1},{1,0},{2,3},{3,2},{4,5},{5,4},{6,7},{7,6},{8,9},{9,8},{10,11... | collective-permute-start | bytes 3538952 | tf_op jit(solution)/shard_map/ppermute | solution.py:408
  630.5 37.4 %collective-permute-start.51 = (bf16[192,3072]{1,0:T(8,128)(2,1)}, bf16[192,3072]{1,0:T(8,128)(2,1)}, u32[]{:S(2)}, u32[]{:S(2)}) collective-permute-start(bf16[192,3072]{1,0:T(8,128)(2,1)} %collective-permute-done.49.refs_5_.refs_9_), channel_id=1, source_target_pairs={{0,1},{1,0},{2,3},{3,2},{4,5},{5,4},{6,7},{7,6},{8,9},{9,8},{10,11... | collective-permute-start | bytes 3538952 | tf_op jit(solution)/shard_map/ppermute | solution.py:408
  667.2 38.5 %collective-permute-start.52 = (bf16[192,3072]{1,0:T(8,128)(2,1)}, bf16[192,3072]{1,0:T(8,128)(2,1)S(1)}, u32[]{:S(2)}, u32[]{:S(2)}) collective-permute-start(bf16[192,3072]{1,0:T(8,128)(2,1)} %collective-permute-done.48.refs_4_.refs_8_), channel_id=1, source_target_pairs={{0,2},{1,3},{2,0},{3,1},{4,6},{5,7},{6,4},{7,5},{8,10},{9,11},{10,... | collective-permute-start | bytes 3538952 | tf_op jit(solution)/shard_map/ppermute | solution.py:408
  705.7 14.4 %collective-permute-start.54 = (bf16[192,3072]{1,0:T(8,128)(2,1)S(1)}, bf16[192,3072]{1,0:T(8,128)(2,1)S(1)}, u32[]{:S(2)}, u32[]{:S(2)}) collective-permute-start(bf16[192,3072]{1,0:T(8,128)(2,1)S(1)} %collective-permute-done.52.refs_12_.refs_0_), channel_id=1, source_target_pairs={{0,1},{1,0},{2,3},{3,2},{4,5},{5,4},{6,7},{7,6},{8,9},{9,8},{10,11... | collective-permute-start | bytes 3538952 | tf_op jit(solution)/shard_map/ppermute | solution.py:408
  706.1 14.0 %collective-permute-start.55 = (bf16[192,3072]{1,0:T(8,128)(2,1)}, bf16[192,3072]{1,0:T(8,128)(2,1)S(1)}, u32[]{:S(2)}, u32[]{:S(2)}) collective-permute-start(bf16[192,3072]{1,0:T(8,128)(2,1)} %collective-permute-done.53.refs_13_.refs_1_), channel_id=1, source_target_pairs={{0,1},{1,0},{2,3},{3,2},{4,5},{5,4},{6,7},{7,6},{8,9},{9,8},{10,11... | collective-permute-start | bytes 3538952 | tf_op jit(solution)/shard_map/ppermute | solution.py:408
  720.1 17.4 %slice-start = ((s8[6291456]{0:T(1024)(128)(4,1)}), s8[4194304]{0:T(1024)(128)(4,1)S(1)}, s32[]{:S(2)}) async-start(s8[6291456]{0:T(1024)(128)(4,1)} %bitcast.17), calls=%async_computation.1 | async-start | bytes 8388608
  (23 other events, 80.1 us)

commit v2 on v1

--- a/solution.py
+++ b/solution.py
@@ -38,14 +38,6 @@
 
 def dot_nt(lhs, rhs):
     return lax.dot_general(lhs, rhs, (((1,), (1,)), ((), ())), preferred_element_type=F32)
-
-
-def dot_tn(lhs, rhs):
-    return lax.dot_general(lhs, rhs, (((0,), (0,)), ((), ())), preferred_element_type=F32)
-
-
-def dot_tt(lhs, rhs):
-    return lax.dot_general(lhs, rhs, (((0,), (1,)), ((), ())), preferred_element_type=F32)
 
 
 def proj_kernel(group, x_ref, g_ref, wq_ref, wk_ref, wv_ref, wo_ref, cos_ref, sin_ref, out_ref):
@@ -251,64 +243,103 @@
     )(first_blk, packed, packed, packed, packed, starts, cos_t, sin_t)
 
 
-def assemble_kernel(turn, me_ref, *refs):
+def assemble_kernel(turn, half_steps, me_ref, *refs):
     out_ref = refs[-1]
-    for rel, ref in enumerate(refs[:-1]):
-        tokens = ref.shape[0]
-        place = pl.ds(pl.multiple_of((me_ref[0] ^ rel) * tokens, tokens), tokens)
-        if turn:
-            out_ref[:, place] = ref[...].T
-        else:
-            out_ref[place, :] = ref[...]
-
-
-def assemble(pieces, me, turn):
-    tokens, width = pieces[0].shape
-    seq = tokens * len(pieces)
+    n_dev = len(refs) // 2
+
+    def fill(ins):
+        for rel, ref in enumerate(ins):
+            tokens = ref.shape[0]
+            place = pl.ds(pl.multiple_of((me_ref[0] ^ rel) * tokens, tokens), tokens)
+            if turn:
+                out_ref[:, place] = ref[...].T
+            else:
+                out_ref[place, :] = ref[...]
+
+    @pl.when(pl.program_id(0) < half_steps)
+    def _():
+        fill(refs[:n_dev])
+
+    @pl.when(pl.program_id(0) >= half_steps)
+    def _():
+        fill(refs[n_dev:2 * n_dev])
+
+
+def assemble(low, high, me, turn):
+    tokens, half_width = low[0].shape
+    seq, width = tokens * len(low), 2 * half_width
     col_blk = 512
+    steps = half_width // col_blk
     if turn:
         out_spec, shape = pl.BlockSpec((col_blk, seq), lambda i, me: (i, 0)), (width, seq)
     else:
         out_spec, shape = pl.BlockSpec((seq, col_blk), lambda i, me: (0, i)), (seq, width)
+    low_specs = [pl.BlockSpec((tokens, col_blk), lambda i, me: (0, jnp.minimum(i, steps - 1))) for _ in low]
+    high_specs = [pl.BlockSpec((tokens, col_blk), lambda i, me: (0, jnp.maximum(i - steps, 0))) for _ in high]
     return pl.pallas_call(
-        functools.partial(assemble_kernel, turn),
+        functools.partial(assemble_kernel, turn, steps),
         grid_spec=pltpu.PrefetchScalarGridSpec(
             num_scalar_prefetch=1,
-            grid=(width // col_blk,),
-            in_specs=[pl.BlockSpec((tokens, col_blk), lambda i, me: (0, i)) for _ in pieces],
+            grid=(2 * steps,),
+            in_specs=low_specs + high_specs,
             out_specs=out_spec,
         ),
         out_shape=jax.ShapeDtypeStruct(shape, BF16),
-        compiler_params=pltpu.CompilerParams(dimension_semantics=("arbitrary",), vmem_limit_bytes=32 * 1024 * 1024),
+        compiler_params=pltpu.CompilerParams(dimension_semantics=("arbitrary",), vmem_limit_bytes=28 * 1024 * 1024),
         cost_estimate=pl.CostEstimate(flops=0, bytes_accessed=4 * seq * width, transcendentals=0),
-    )(me, *pieces)
-
-
-def own_kernel(rows, me_ref, *refs):
-    out_ref = refs[-1]
-    for rel in range(len(refs[:-1]) // len(rows)):
-        base = (me_ref[0] ^ rel) * sum(rows)
-        for part, height in enumerate(rows):
-            place = pl.ds(pl.multiple_of(base + sum(rows[:part]), HALF), height)
-            out_ref[place, :] = refs[rel * len(rows) + part][...]
-
-
-def own_columns(pieces, me, tokens):
-    rows = tuple(part.shape[0] for part in pieces[0])
-    flat = [part for piece in pieces for part in piece]
-    total = sum(rows) * len(pieces)
+    )(me, *low, *high)
+
+
+def own_kernel(kinds, turned, me_ref, *refs):
+    n_parts = sum(len(rows) * count for rows, count in kinds)
+    parts, weights, (out_ref, scr) = refs[:n_parts], refs[n_parts:-2], refs[-2:]
+
+    @pl.when(pl.program_id(0) == 0)
+    def _():
+        at = start = 0
+        for rows, count in kinds:
+            unit = sum(rows)
+            for rel in range(count):
+                block = jnp.concatenate([parts[at + j][...] for j in range(len(rows))], axis=0)
+                at += len(rows)
+                place = pl.ds(pl.multiple_of(start + (me_ref[0] ^ rel) * unit, HEAD_DIM), unit)
+                scr[:, place] = block.T
+            start += unit * count
+
+    total = None
+    start = 0
+    for (rows, count), weight in zip(kinds, weights):
+        width = sum(rows) * count
+        dot = dot_nt if turned else dot_nn
+        term = dot(scr[:, start:start + width], weight[...])
+        total = term if total is None else total + term
+        start += width
+    out_ref[...] = total.astype(BF16)
+
+
+def own_product(groups, weights, me, tokens, turned):
+    kinds = tuple((tuple(part.shape[0] for part in pieces[0]), len(pieces)) for pieces in groups)
+    flat = [part for pieces in groups for piece in pieces for part in piece]
+    width = weights[0].shape[0] if turned else weights[0].shape[1]
+    depth = sum(sum(rows) * count for rows, count in kinds)
+    blk = 512
+    if turned:
+        weight_specs = [pl.BlockSpec((blk, weight.shape[1]), lambda i, me: (i, 0)) for weight in weights]
+    else:
+        weight_specs = [pl.BlockSpec((weight.shape[0], blk), lambda i, me: (0, i)) for weight in weights]
     return pl.pallas_call(
-        functools.partial(own_kernel, rows),
+        functools.partial(own_kernel, kinds, turned),
         grid_spec=pltpu.PrefetchScalarGridSpec(
             num_scalar_prefetch=1,
-            grid=(1,),
-            in_specs=[pl.BlockSpec((part.shape[0], tokens), lambda i, me: (0, me[0])) for part in flat],
-            out_specs=pl.BlockSpec((total, tokens), lambda i, me: (0, 0)),
+            grid=(width // blk,),
+            in_specs=[pl.BlockSpec((part.shape[0], tokens), lambda i, me: (0, me[0]), pipeline_mode=pl.Buffered(1)) for part in flat] + weight_specs,
+            out_specs=pl.BlockSpec((tokens, blk), lambda i, me: (0, i)),
+            scratch_shapes=[pltpu.VMEM((tokens, depth), BF16)],
         ),
-        out_shape=jax.ShapeDtypeStruct((total, tokens), BF16),
-        compiler_params=pltpu.CompilerParams(dimension_semantics=("arbitrary",), vmem_limit_bytes=16 * 1024 * 1024),
-        cost_estimate=pl.CostEstimate(flops=0, bytes_accessed=4 * total * tokens, transcendentals=0),
-    )(me, *flat)
+        out_shape=jax.ShapeDtypeStruct((tokens, width), BF16),
+        compiler_params=pltpu.CompilerParams(dimension_semantics=("arbitrary",), vmem_limit_bytes=32 * 1024 * 1024),
+        cost_estimate=pl.CostEstimate(flops=2 * tokens * width * depth, bytes_accessed=2 * depth * (width + tokens), transcendentals=0),
+    )(me, *flat, *weights)
 
 
 def wgrad_kernel(by_rows, rels, n_out, me_ref, big_ref, *refs):
@@ -393,7 +424,7 @@
         ),
         out_shape=[jax.ShapeDtypeStruct(shape, F32)] * n_out,
         input_output_aliases={n_fixed + o: o for o in range(len(prev))},
-        compiler_params=pltpu.CompilerParams(dimension_semantics=("arbitrary",), vmem_limit_bytes=60 * 1024 * 1024),
+        compiler_params=pltpu.CompilerParams(dimension_semantics=("arbitrary",), vmem_limit_bytes=48 * 1024 * 1024),
         cost_estimate=pl.CostEstimate(flops=2 * rows * width * seq, bytes_accessed=4 * width * rows + 2 * seq * (width + rows), transcendentals=0),
     )(me, big, *parts, *prev)
 
@@ -438,8 +469,13 @@
         freqs = rope_freqs()
         me = lax.axis_index("sp").astype(jnp.int32)
         me_arr = me[None]
-        idx_all = lax.all_gather(jnp.stack([positions, doc_ids])[None], "sp", axis=0, tiled=True)
-        idx_all, hidden, grad_out = lax.optimization_barrier((idx_all, hidden, grad_out))
+        idx = {0: jnp.stack([positions, doc_ids])}
+        idx[SIDE_X], idx[SIDE_Y] = swap(idx[0], SIDE_X), swap(idx[0], SIDE_Y)
+        idx[SIDE_X | SIDE_Y] = swap(idx[0], SIDE_X | SIDE_Y)
+        for rel in (0, SIDE_X, SIDE_Y, SIDE_X | SIDE_Y):
+            idx[rel | CORE] = swap(idx[0], rel | CORE)
+        order = me ^ jnp.arange(n_dev, dtype=jnp.int32)
+        idx_all = jnp.take(jnp.stack([idx[rel] for rel in range(n_dev)]), order, axis=0)
         pos_all = idx_all[:, 0, :].reshape(seq)
         doc_all = idx_all[:, 1, :].reshape(seq)
         starts = jnp.sum((doc_all[None, :] < doc_all[:, None]).astype(jnp.int32), axis=1)
@@ -458,43 +494,43 @@
         def pairs(got, rels):
             return [half[r] for r in rels for half in got]
 
-        x_got = reach(hidden, grad_out)
+        half = hidden.shape[1] // 2
+        x_got = reach(hidden[:, :half], hidden[:, half:])
         packed = project(hidden, grad_out, w_q, w_k, w_v, w_o, cos_tab, sin_tab, n_dev, group)
         packed = lax.all_to_all(packed, "sp", 0, 0, tiled=True).reshape(seq, -1)
+        relay(x_got)
+        g_got = reach(grad_out[:, :half], grad_out[:, half:])
         ctx_lo, ctx_hi, dq_lo, dq_hi, dk_t, dv_t = attention(packed, first_blk, starts[None, :], cos_t, sin_t, group)
-        for rel in (SIDE_X, SIDE_Y):
-            x_got[1][rel] = after(x_got[1][rel], dk_t)
-        relay(x_got)
+        finish(x_got, dk_t)
         kv_got = reach(dk_t, dv_t)
         ctx_got = reach(ctx_lo, ctx_hi)
         dq_got = reach(dq_lo, dq_hi)
-        finish(x_got, dk_t)
-        x_turned = assemble([x_got[0][r] for r in every], me_arr, True)
-        g_all = assemble([x_got[1][r] for r in every], after(me_arr, x_turned), False)
-        hold(kv_got, x_turned)
-        relay(kv_got)
-        (g_q,) = weight_grad(x_turned, pairs(dq_got, (0,)) + [swap(dq_got[0][0], CORE), swap(dq_got[1][0], CORE)], groups[0], after(me_arr, g_all), None, False, 1, n_dev)
-        finish(kv_got, g_q)
-        g_k, g_v = weight_grad(x_turned, [kv_got[0][r] for r in every] + [kv_got[1][r] for r in every], every, after(me_arr, g_q), None, False, 2, n_dev)
-        hold(ctx_got, g_k)
+
+        x_turned = assemble([x_got[0][r] for r in every], [x_got[1][r] for r in every], after(me_arr, dk_t), True)
+        hold(g_got, x_turned)
+        relay(g_got)
+        (g_q,) = weight_grad(x_turned, pairs(dq_got, (0,)) + [swap(dq_got[0][0], CORE), swap(dq_got[1][0], CORE)], groups[0], me_arr, None, False, 1, n_dev)
+        finish(g_got, g_q)
+        g_all = assemble([g_got[0][r] for r in every], [g_got[1][r] for r in every], after(me_arr, g_q), False)
+        (g_o,) = weight_grad(g_all, pairs(ctx_got, (0,)) + [swap(ctx_got[0][0], CORE), swap(ctx_got[1][0], CORE)], groups[0], me_arr, None, True, 1, n_dev)
+        hold(ctx_got, g_o)
         relay(ctx_got)
-        (g_o,) = weight_grad(g_all, pairs(ctx_got, groups[0]), groups[0], after(me_arr, g_k), None, True, 1, n_dev)
         (g_o,) = weight_grad(g_all, pairs(ctx_got, groups[1]), groups[1], me_arr, (g_o,), True, 1, n_dev)
         finish(ctx_got, g_o)
-        hold(dq_got, g_o)
+        (g_o,) = weight_grad(g_all, pairs(ctx_got, groups[2]), groups[2], me_arr, (g_o,), True, 1, n_dev)
+        hold(kv_got, g_o)
+        relay(kv_got)
+        attn_out = own_product([[[part[r] for part in ctx_got] for r in every]], [w_o], after(me_arr, g_o), tokens, False)
+        finish(kv_got, attn_out)
+        g_k, g_v = weight_grad(x_turned, [kv_got[0][r] for r in every] + [kv_got[1][r] for r in every], every, after(me_arr, attn_out), None, False, 2, n_dev)
+        hold(dq_got, g_k)
         relay(dq_got)
-        (g_o,) = weight_grad(g_all, pairs(ctx_got, groups[2]), groups[2], me_arr, (g_o,), True, 1, n_dev)
-        own_ctx = own_columns([[half[r] for half in ctx_got] for r in every], after(me_arr, g_o), tokens)
-        attn_out = dot_tn(own_ctx, w_o).astype(BF16)
-        (g_q,) = weight_grad(x_turned, pairs(dq_got, groups[1]), groups[1], after(me_arr, attn_out), (g_q,), False, 1, n_dev)
+        (g_q,) = weight_grad(x_turned, pairs(dq_got, groups[1]), groups[1], after(me_arr, g_k), (g_q,), False, 1, n_dev)
         finish(dq_got, g_q)
         (g_q,) = weight_grad(x_turned, pairs(dq_got, groups[2]), groups[2], me_arr, (g_q,), False, 1, n_dev)
-        own_k = own_columns([[kv_got[0][r]] for r in every], after(me_arr, g_k), tokens)
-        own_v = own_columns([[kv_got[1][r]] for r in every], after(me_arr, g_k), tokens)
-        own_q = own_columns([[half[r] for half in dq_got] for r in every], me_arr, tokens)
-        grad_hidden = (dot_tt(own_q, w_q) + dot_tt(own_k, w_k) + dot_tt(own_v, w_v)).astype(BF16)
-        g_q, g_o = [g_q], [g_o]
-        return attn_out, grad_hidden, g_q[0], g_k, g_v, g_o[0]
+        sources = [[[part[r] for part in dq_got] for r in every], [[kv_got[0][r]] for r in every], [[kv_got[1][r]] for r in every]]
+        grad_hidden = own_product(sources, [w_q, w_k, w_v], after(me_arr, g_q), tokens, True)
+        return attn_out, grad_hidden, g_q, g_k, g_v, g_o
 
     tok_spec = P(("dp", "sp"), None)
     vec_spec = P(("dp", "sp"))

time: 770 us -> 705 us (0.916)
  waiting for transfers between devices: 297 us -> 223 us
  matrix products: 40.6 us -> 0 us
  local copies, waits for them, and re-layouts: 16.7 us -> 47.9 us
  Pallas kernels: 344 us -> 359 us
  blocking collectives: 10.4 us -> 0 us
  starting transfers between devices: 45.2 us -> 54.7 us
    ppermute x56 -> x77, waiting for transfers between devices: 297 us -> 223 us  [swap(): return lax.ppermute(values, 'sp', [(i, i ^ bit) for i in range(n_dev)])]
    dot_general x4 -> x0, matrix products: 40.6 us -> none  [the longest x3 27.9 us: dot_tt(): lax.dot_general(lhs, rhs, (((0,), (1,)), ((), ())), preferred_element_typ...]
    unnamed x60 -> x142, local copies, waits for them, and re-layouts: 15.2 us -> 42.7 us
    pallas_call x6 -> x4, Pallas kernels: 33.6 us -> 58 us  [the longest x2 33.6 us: own_product(): pl.pallas_call(functools.partial(own_kernel, kinds, turned), grid_spec=pl...]
    all_gather x1 -> x0, blocking collectives: 10.4 us -> none  [device_body(): lax.all_gather(jnp.stack([positions, doc_ids])[None], 'sp', axis=0, tiled...]
    pallas_call x7, Pallas kernels: 208 us -> 198 us  [weight_grad(): pl.pallas_call(body, grid_spec=pltpu.PrefetchScalarGridSpec(num_scalar_pr...]
    ppermute x56 -> x77, starting transfers between devices: 39.7 us -> 49 us  [swap(): return lax.ppermute(values, 'sp', [(i, i ^ bit) for i in range(n_dev)])]
  transfers between devices with their start and end apart: 57 -> 78, of which waited for: 10 -> 25; matrix products, arithmetic and copies ran while one was open for 4% -> 3% of each run, Pallas kernels for 37% -> 41%
where the time goes in v2:
time: 705 us; the launch traced here: 699 us
  Pallas kernels  359 us (51%)
  waiting for transfers between devices  223 us (32%)
  starting transfers between devices  54.7 us (8%)
  local copies, waits for them, and re-layouts  47.9 us (7%)
  other arithmetic  13.3 us (2%)
    ppermute x77, waiting for transfers between devices, swap(): return lax.ppermute(values, 'sp', [(i, i ^ bit) for i in range(n_dev)])  223 us
    pallas_call x7, Pallas kernels, weight_grad(): pl.pallas_call(body, grid_spec=pltpu.PrefetchScalarGridSpec(num_scalar_pr...  198 us
    pallas_call x1, Pallas kernels, attention(): pl.pallas_call(functools.partial(attn_kernel, group), grid_spec=grid_spec...  67.6 us
    ppermute x77, starting transfers between devices, swap(): return lax.ppermute(values, 'sp', [(i, i ^ bit) for i in range(n_dev)])  49 us
    unnamed x142, local copies, waits for them, and re-layouts  42.7 us
    pallas_call x1, Pallas kernels, project(): pl.pallas_call(functools.partial(proj_kernel, group), grid=(n_dev,), in_s...  35.1 us
    pallas_call x2, Pallas kernels, own_product(): pl.pallas_call(functools.partial(own_kernel, kinds, turned), grid_spec=pl...  33.6 us
    pallas_call x2, Pallas kernels, assemble(): pl.pallas_call(functools.partial(assemble_kernel, turn, steps), grid_spec...  24.4 us
  transfers between devices with their start and end apart: 78, of which 25 were waited for; matrix products, arithmetic and copies ran while one was open for 3% of the time, Pallas kernels for 41%

profile of v2, /device:TPU:1, one launch (start us, length us, event | category | flops | bytes accessed | tf_op | source)
XLA Modules:
  0.0 699.4 jit_solution(5056351956939984315)
XLA Ops:
  2.3 1.7 copy-done.12
  4.0 1.7 copy-done.13
  5.6 35.1 %project.1 = bf16[8,384,1024]{2,1,0:T(8,128)(2,1)} custom-call(bf16[384,3072]{1,0:T(8,128)(2,1)S(1)} %copy-done.12, bf16[384,3072]{1,0:T(8,128)(2,1)S(1)} %copy-done.13, bf16[3072,3072]{1,0:T(8,128)(2,1)} %refs_32_.1, bf16[3072,1024]{1,0:T(8,128)(2,1)} %refs_33_.1, bf16[3072,1024]{1,0:T(8,128)(2,1)} %refs_34_.1, bf16[3072,3072]{1,0:T(8,128)(2,1)} %refs_16_.1, ...), custom_call_target="tpu_custom_call" | custom-call | flops 19327352832 | bytes 60000000 | tf_op jit(solution)/shard_map/project/pallas_call | solution.py:64
  40.7 5.7 all-to-all-start
  46.5 2.5 collective-permute-start.5
  52.5 1.8 fusion.3
  56.6 59.7 %collective-permute-done.1 = s32[2,384]{1,0:T(2,128)S(1)} collective-permute-done((s32[2,384]{1,0:T(2,128)S(1)}, s32[2,384]{1,0:T(2,128)S(1)}, u32[]{:S(2)}, u32[]{:S(2)}) %collective-permute-start.1) | collective-permute-done | bytes 3104 | tf_op jit(solution)/shard_map/ppermute | solution.py:439
  116.3 2.2 collective-permute-start.6
  120.9 1.3 constant_dynamic-update-slice_fusion.4
  122.3 1.3 constant_dynamic-update-slice_fusion.3
  123.6 1.3 collective-permute-start.17
  127.1 1.9 gather_fusion
  129.8 17.9 %collective-permute-done.15.refs_10_ = bf16[384,1536]{1,0:T(8,128)(2,1)S(1)} collective-permute-done((bf16[384,1536]{1,0:T(8,128)(2,1)S(1)}, bf16[384,1536]{1,0:T(8,128)(2,1)S(1)}, u32[]{:S(2)}, u32[]{:S(2)}) %collective-permute-start.15) | collective-permute-done | bytes 1179680 | tf_op jit(solution)/shard_map/ppermute | solution.py:439
  147.7 2.3 collective-permute-done.10.refs_4_
  150.4 4.6 convert_reduce_fusion
  156.3 4.5 multiply_sine_fusion
  160.9 14.4 %collective-permute-done.17.refs_12_ = bf16[384,1536]{1,0:T(8,128)(2,1)} collective-permute-done((bf16[384,1536]{1,0:T(8,128)(2,1)S(1)}, bf16[384,1536]{1,0:T(8,128)(2,1)}, u32[]{:S(2)}, u32[]{:S(2)}) %collective-permute-start.17) | collective-permute-done | bytes 1179680 | tf_op jit(solution)/shard_map/ppermute | solution.py:439
  176.6 23.9 %collective-permute-done.19.refs_14_ = bf16[384,1536]{1,0:T(8,128)(2,1)} collective-permute-done((bf16[384,1536]{1,0:T(8,128)(2,1)S(1)}, bf16[384,1536]{1,0:T(8,128)(2,1)}, u32[]{:S(2)}, u32[]{:S(2)}) %collective-permute-start.19) | collective-permute-done | bytes 1179680 | tf_op jit(solution)/shard_map/ppermute | solution.py:439
  201.2 67.6 %attention.1 = (bf16[192,3072]{1,0:T(8,128)(2,1)}, bf16[192,3072]{1,0:T(8,128)(2,1)}, bf16[192,3072]{1,0:T(8,128)(2,1)}, bf16[192,3072]{1,0:T(8,128)(2,1)}, bf16...) custom-call(s32[12]{0:T(128)} %and_select_fusion.lo_ref, bf16[3072,1024]{1,0:T(8,128)(2,1)} %bitcast.11.q_ref.do_ref.k_ref.v_ref, ...), custom_call_target="tpu_custom_call" | custom-call | flops 72477573120 | bytes 12000000 | tf_op jit(solution)/shard_map/attention/pallas_call | solution.py:229
  269.9 1.5 collective-permute-start.33
  274.2 14.7 %shard_map.127.big_ref = bf16[3072,3072]{1,0:T(8,128)(2,1)} custom-call(s32[1]{0:T(128)} %bitcast.me_ref, bf16[384,1536]{1,0:T(8,128)(2,1)S(1)} %get-tuple-element.89.refs_0_, bf16[384,1536]{1,0:T(8,128)(2,1)} %collective-permute-done.7.refs_1_, bf16[384,1536]{1,0:T(8,128)(2,1)} %collective-permute-done.8.refs_2_, ...), custom_call_target="tpu_custom_call" | custom-call | bytes 37748736 | tf_op jit(solution)/shard_map/pallas_call | solution.py:279
  288.9 7.8 %collective-permute-done.31.refs_10_ = bf16[384,1536]{1,0:T(8,128)(2,1)S(1)} collective-permute-done((bf16[384,1536]{1,0:T(8,128)(2,1)S(1)}, bf16[384,1536]{1,0:T(8,128)(2,1)S(1)}, u32[]{:S(2)}, u32[]{:S(2)}) %collective-permute-start.31) | collective-permute-done | bytes 1179680 | tf_op jit(solution)/shard_map/ppermute | solution.py:439
  296.7 2.2 collective-permute-start.22
  299.2 22.9 %collective-permute-done.33.refs_12_ = bf16[384,1536]{1,0:T(8,128)(2,1)} collective-permute-done((bf16[384,1536]{1,0:T(8,128)(2,1)S(1)}, bf16[384,1536]{1,0:T(8,128)(2,1)}, u32[]{:S(2)}, u32[]{:S(2)}) %collective-permute-start.33) | collective-permute-done | bytes 1179680 | tf_op jit(solution)/shard_map/ppermute | solution.py:439
  322.1 2.1 collective-permute-start.30
  324.8 22.5 %collective-permute-done.28.refs_6_ = bf16[384,1536]{1,0:T(8,128)(2,1)S(1)} collective-permute-done((bf16[384,1536]{1,0:T(8,128)(2,1)S(1)}, bf16[384,1536]{1,0:T(8,128)(2,1)S(1)}, u32[]{:S(2)}, u32[]{:S(2)}) %collective-permute-start.28) | collective-permute-done | bytes 1179680 | tf_op jit(solution)/shard_map/ppermute | solution.py:439
  347.3 1.3 collective-permute-start.32
  348.6 1.9 collective-permute-start.25
  350.5 19.8 %shard_map.128.refs_8_ = f32[3072,3072]{1,0:T(8,128)} custom-call(s32[1]{0:T(128)} %bitcast.me_ref, bf16[3072,3072]{1,0:T(8,128)(2,1)} %shard_map.127.big_ref, bf16[192,3072]{1,0:T(8,128)(2,1)S(1)} %copy-done, bf16[192,3072]{1,0:T(8,128)(2,1)S(1)} %copy-done.1, bf16[192,3072]{1,0:T(8,128)(2,1)S(1)} %collective-permute-done.21.refs_2_, ...), custom_call_target="tpu_custom_call" | custom-call | flops 14495514624 | bytes 33030144 | tf_op jit(solution)/shard_map/pallas_call | solution.py:412
  372.4 2.0 collective-permute-done.34.refs_13_
  376.1 1.6 collective-permute-done.36.refs_15_
  377.8 1.3 copy-done.16
  379.1 1.3 copy-done.18
  380.3 9.7 %shard_map.129.big_ref = bf16[3072,3072]{1,0:T(8,128)(2,1)} custom-call(s32[1]{0:T(128)} %bitcast.me_ref, bf16[384,1536]{1,0:T(8,128)(2,1)S(1)} %get-tuple-element.87.refs_0_, bf16[384,1536]{1,0:T(8,128)(2,1)} %collective-permute-done.23.refs_1_, bf16[384,1536]{1,0:T(8,128)(2,1)S(1)} %copy-done.16, bf16[384,1536]{1,0:T(8,128)(2,1)} %collective-permute-done.25.refs_3_, ...), custom_call_target="tpu_custom_call" | custom-call | bytes 37748736 | tf_op jit(solution)/shard_map/pallas_call | solution.py:279
  390.0 1.4 collective-permute-start.41
  391.4 19.0 %shard_map.130.refs_8_ = f32[3072,3072]{1,0:T(8,128)} custom-call(s32[1]{0:T(128)} %bitcast.me_ref, bf16[3072,3072]{1,0:T(8,128)(2,1)} %shard_map.129.big_ref, bf16[192,3072]{1,0:T(8,128)(2,1)S(1)} %copy-done.6, bf16[192,3072]{1,0:T(8,128)(2,1)S(1)} %copy-done.7, bf16[192,3072]{1,0:T(8,128)(2,1)S(1)} %collective-permute-done.38.refs_2_, ...), custom_call_target="tpu_custom_call" | custom-call | flops 14495514624 | bytes 33030144 | tf_op jit(solution)/shard_map/pallas_call | solution.py:412
  410.5 18.3 %collective-permute-done.46.refs_5_.refs_9_ = bf16[192,3072]{1,0:T(8,128)(2,1)S(1)} collective-permute-done((bf16[192,3072]{1,0:T(8,128)(2,1)S(1)}, bf16[192,3072]{1,0:T(8,128)(2,1)S(1)}, u32[]{:S(2)}, u32[]{:S(2)}) %collective-permute-start.46) | collective-permute-done | bytes 1179680 | tf_op jit(solution)/shard_map/ppermute | solution.py:439
  432.8 1.4 collective-permute-done.45.refs_3_.refs_7_
  435.9 1.8 collective-permute-done.48.refs_7_.refs_11_
  437.7 1.3 copy-done.20
  438.9 1.3 copy-done.25
  440.2 36.2 %shard_map.131.refs_4_ = f32[3072,3072]{1,0:T(8,128)} custom-call(s32[1]{0:T(128)} %bitcast.me_ref, bf16[3072,3072]{1,0:T(8,128)(2,1)} %shard_map.129.big_ref, bf16[192,3072]{1,0:T(8,128)(2,1)S(1)} %copy-done.20, bf16[192,3072]{1,0:T(8,128)(2,1)S(1)} %collective-permute-done.41.refs_1_.refs_5_, ...), custom_call_target="tpu_custom_call", output_to_operand_aliasing={{}: (10, {})} | custom-call | flops 28991029248 | bytes 47185920 | tf_op jit(solution)/shard_map/pallas_call | solution.py:412
  477.1 1.4 collective-permute-start.60
  478.4 1.3 collective-permute-start.55
  481.1 19.0 %shard_map.132 = f32[3072,3072]{1,0:T(8,128)} custom-call(s32[1]{0:T(128)} %bitcast.me_ref, bf16[3072,3072]{1,0:T(8,128)(2,1)} %shard_map.129.big_ref, bf16[192,3072]{1,0:T(8,128)(2,1)S(1)} %collective-permute-done.40.refs_0_.refs_12_, bf16[192,3072]{1,0:T(8,128)(2,1)S(1)} %collective-permute-done.42.refs_1_.refs_13_, ...), custom_call_target="tpu_custom_call", output_to_operand_aliasing={{}: (6, {})} | custom-call | flops 14495514624 | bytes 33030144 | tf_op jit(solution)/shard_map/pallas_call | solution.py:412
  500.1 12.8 %collective-permute-done.55.refs_4_.refs_20_ = bf16[128,3072]{1,0:T(8,128)(2,1)} collective-permute-done((bf16[128,3072]{1,0:T(8,128)(2,1)}, bf16[128,3072]{1,0:T(8,128)(2,1)}, u32[]{:S(2)}, u32[]{:S(2)}) %collective-permute-start.55) | collective-permute-done | bytes 786464 | tf_op jit(solution)/shard_map/ppermute | solution.py:439
  514.3 1.8 collective-permute-start.59
  516.7 1.3 copy-done.26
  517.9 1.3 copy-done.28
  519.2 13.6 %shard_map.133 = bf16[384,3072]{1,0:T(8,128)(2,1)} custom-call(s32[1]{0:T(128)} %bitcast.me_ref, bf16[192,3072]{1,0:T(8,128)(2,1)S(1)} %copy-done.6, bf16[192,3072]{1,0:T(8,128)(2,1)S(1)} %copy-done.7, bf16[192,3072]{1,0:T(8,128)(2,1)S(1)} %collective-permute-done.38.refs_2_, bf16[192,3072]{1,0:T(8,128)(2,1)S(1)} %collective-permute-done.39.refs_3_, ...), custom_call_target="tpu_custom_call" | custom-call | flops 7247757312 | bytes 21233664 | tf_op jit(solution)/shard_map/pallas_call | solution.py:330
  546.1 48.3 %shard_map.134 = (f32[3072,1024]{1,0:T(8,128)}, f32[3072,1024]{1,0:T(8,128)}) custom-call(s32[1]{0:T(128)} %bitcast.me_ref, bf16[3072,3072]{1,0:T(8,128)(2,1)} %shard_map.127.big_ref, bf16[128,3072]{1,0:T(8,128)(2,1)S(1)} %copy-done.36, bf16[128,3072]{1,0:T(8,128)(2,1)S(1)} %copy-done.47, bf16[128,3072]{1,0:T(8,128)(2,1)} %collective-permute-done.53.refs_2_.refs_18_, ...), custom_call_target="tpu_custom_call" | custom-call | flops 38654705664 | bytes 56623104 | tf_op jit(solution)/shard_map/pallas_call | solution.py:412
  594.5 1.6 collective-permute-start.73
  597.2 1.3 collective-permute-done.73.refs_6_.refs_10_
  598.8 1.5 collective-permute-done.71.refs_3_.refs_7_
  600.2 1.7 collective-permute-done.70.refs_2_.refs_6_
  601.9 1.7 collective-permute-done.74.refs_7_.refs_11_
  604.7 36.1 %shard_map.135.refs_4_ = f32[3072,3072]{1,0:T(8,128)} custom-call(s32[1]{0:T(128)} %bitcast.me_ref, bf16[3072,3072]{1,0:T(8,128)(2,1)} %shard_map.127.big_ref, bf16[192,3072]{1,0:T(8,128)(2,1)S(1)} %collective-permute-done.69.refs_0_.refs_4_, bf16[192,3072]{1,0:T(8,128)(2,1)S(1)} %collective-permute-done.67.refs_1_.refs_5_, ...), custom_call_target="tpu_custom_call", output_to_operand_aliasing={{}: (10, {})} | custom-call | flops 28991029248 | bytes 47185920 | tf_op jit(solution)/shard_map/pallas_call | solution.py:412
  642.4 2.3 collective-permute-done.75.refs_2_.refs_14_
  644.8 1.7 collective-permute-done.76.refs_3_.refs_15_
  646.5 19.7 %shard_map.136 = f32[3072,3072]{1,0:T(8,128)} custom-call(s32[1]{0:T(128)} %bitcast.me_ref, bf16[3072,3072]{1,0:T(8,128)(2,1)} %shard_map.127.big_ref, bf16[192,3072]{1,0:T(8,128)(2,1)S(1)} %collective-permute-done.66.refs_0_.refs_12_, bf16[192,3072]{1,0:T(8,128)(2,1)S(1)} %collective-permute-done.68.refs_1_.refs_13_, ...), custom_call_target="tpu_custom_call", output_to_operand_aliasing={{}: (6, {})} | custom-call | flops 14495514624 | bytes 33030144 | tf_op jit(solution)/shard_map/pallas_call | solution.py:412
  666.3 1.3 copy-done.30
  667.6 1.3 copy-done.32
  668.8 1.3 copy-done.34
  679.2 20.0 %shard_map.137 = bf16[384,3072]{1,0:T(8,128)(2,1)} custom-call(s32[1]{0:T(128)} %bitcast.me_ref, bf16[192,3072]{1,0:T(8,128)(2,1)S(1)} %copy-done, bf16[192,3072]{1,0:T(8,128)(2,1)S(1)} %copy-done.1, bf16[192,3072]{1,0:T(8,128)(2,1)S(1)} %copy-done.3, bf16[192,3072]{1,0:T(8,128)(2,1)S(1)} %copy-done.5, ...), custom_call_target="tpu_custom_call" | custom-call | flops 12079595520 | bytes 35389440 | tf_op jit(solution)/shard_map/pallas_call | solution.py:330
  (268 shorter events, 61.4 us)
Async XLA Ops:
  40.7 160.5 %all-to-all-start = ((bf16[8,384,1024]{2,1,0:T(8,128)(2,1)}), bf16[8,384,1024]{2,1,0:T(8,128)(2,1)}, u32[]{:S(2)}, u32[]{:S(2)}) async-start(bf16[8,384,1024]{2,1,0:T(8,128)(2,1)} %project.1), calls=%async_computation | async-start | bytes 12582912 | tf_op jit(solution)/shard_map/all_to_all | solution.py:500
  46.5 79.0 %collective-permute-start.5 = (s32[2,384]{1,0:T(2,128)S(1)}, s32[2,384]{1,0:T(2,128)S(1)}, u32[]{:S(2)}, u32[]{:S(2)}) collective-permute-start(s32[2,384]{1,0:T(2,128)S(1)} %pad_add_fusion), channel_id=1, source_target_pairs={{0,6},{1,7},{2,4},{3,5},{4,2},{5,3},{6,0},{7,1},{8,14},{9,15},{10,... | collective-permute-start | bytes 9224 | tf_op jit(solution)/shard_map/ppermute | solution.py:439
  49.0 74.6 %collective-permute-start.4 = (s32[2,384]{1,0:T(2,128)S(1)}, s32[2,384]{1,0:T(2,128)S(1)}, u32[]{:S(2)}, u32[]{:S(2)}) collective-permute-start(s32[2,384]{1,0:T(2,128)S(1)} %pad_add_fusion), channel_id=1, source_target_pairs={{0,5},{1,4},{2,7},{3,6},{4,1},{5,0},{6,3},{7,2},{8,13},{9,12},{10,... | collective-permute-start | bytes 9224 | tf_op jit(solution)/shard_map/ppermute | solution.py:439
  50.0 72.1 %collective-permute-start.3 = (s32[2,384]{1,0:T(2,128)S(1)}, s32[2,384]{1,0:T(2,128)}, u32[]{:S(2)}, u32[]{:S(2)}) collective-permute-start(s32[2,384]{1,0:T(2,128)S(1)} %pad_add_fusion), channel_id=1, source_target_pairs={{0,4},{1,5},{2,6},{3,7},{4,0},{5,1},{6,2},{7,3},{8,12},{9,13},{10,... | collective-permute-start | bytes 9224 | tf_op jit(solution)/shard_map/ppermute | solution.py:439
  51.2 67.8 %collective-permute-start.2 = (s32[2,384]{1,0:T(2,128)S(1)}, s32[2,384]{1,0:T(2,128)S(1)}, u32[]{:S(2)}, u32[]{:S(2)}) collective-permute-start(s32[2,384]{1,0:T(2,128)S(1)} %pad_add_fusion), channel_id=1, source_target_pairs={{0,3},{1,2},{2,1},{3,0},{4,7},{5,6},{6,5},{7,4},{8,11},{9,10},{10,... | collective-permute-start | bytes 9224 | tf_op jit(solution)/shard_map/ppermute | solution.py:439
  54.8 61.5 %collective-permute-start.1 = (s32[2,384]{1,0:T(2,128)S(1)}, s32[2,384]{1,0:T(2,128)S(1)}, u32[]{:S(2)}, u32[]{:S(2)}) collective-permute-start(s32[2,384]{1,0:T(2,128)S(1)} %pad_add_fusion), channel_id=1, source_target_pairs={{0,2},{1,3},{2,0},{3,1},{4,6},{5,7},{6,4},{7,5},{8,10},{9,11},{10,... | collective-permute-start | bytes 9224 | tf_op jit(solution)/shard_map/ppermute | solution.py:439
  116.3 10.1 %collective-permute-start.6 = (s32[2,384]{1,0:T(2,128)S(1)}, s32[2,384]{1,0:T(2,128)S(1)}, u32[]{:S(2)}, u32[]{:S(2)}) collective-permute-start(s32[2,384]{1,0:T(2,128)S(1)} %pad_add_fusion), channel_id=1, source_target_pairs={{0,7},{1,6},{2,5},{3,4},{4,3},{5,2},{6,1},{7,0},{8,15},{9,14},{10,... | collective-permute-start | bytes 9224 | tf_op jit(solution)/shard_map/ppermute | solution.py:439
  119.7 28.1 %collective-permute-start.15 = (bf16[384,1536]{1,0:T(8,128)(2,1)S(1)}, bf16[384,1536]{1,0:T(8,128)(2,1)S(1)}, u32[]{:S(2)}, u32[]{:S(2)}) collective-permute-start(bf16[384,1536]{1,0:T(8,128)(2,1)S(1)} %get-tuple-element.88.refs_8_), channel_id=1, source_target_pairs={{0,2},{1,3},{2,0},{3,1},{4,6},{5,7},{6,4},{7,5},{8,10},{9,11},{10,... | collective-permute-start | bytes 3538952 | tf_op jit(solution)/shard_map/ppermute | solution.py:439
  122.1 27.9 %collective-permute-start.10 = (bf16[384,1536]{1,0:T(8,128)(2,1)S(1)}, bf16[384,1536]{1,0:T(8,128)(2,1)}, u32[]{:S(2)}, u32[]{:S(2)}) collective-permute-start(bf16[384,1536]{1,0:T(8,128)(2,1)S(1)} %get-tuple-element.89.refs_0_), channel_id=1, source_target_pairs={{0,4},{1,5},{2,6},{3,7},{4,0},{5,1},{6,2},{7,3},{8,12},{9,13},{10,... | collective-permute-start | bytes 3538952 | tf_op jit(solution)/shard_map/ppermute | solution.py:439
  123.6 51.7 %collective-permute-start.17 = (bf16[384,1536]{1,0:T(8,128)(2,1)S(1)}, bf16[384,1536]{1,0:T(8,128)(2,1)}, u32[]{:S(2)}, u32[]{:S(2)}) collective-permute-start(bf16[384,1536]{1,0:T(8,128)(2,1)S(1)} %get-tuple-element.88.refs_8_), channel_id=1, source_target_pairs={{0,4},{1,5},{2,6},{3,7},{4,0},{5,1},{6,2},{7,3},{8,12},{9,13},{10,... | collective-permute-start | bytes 3538952 | tf_op jit(solution)/shard_map/ppermute | solution.py:439
  125.5 50.7 %collective-permute-start.14 = (bf16[384,1536]{1,0:T(8,128)(2,1)S(1)}, bf16[384,1536]{1,0:T(8,128)(2,1)}, u32[]{:S(2)}, u32[]{:S(2)}) collective-permute-start(bf16[384,1536]{1,0:T(8,128)(2,1)S(1)} %get-tuple-element.88.refs_8_), channel_id=1, source_target_pairs={{0,1},{1,0},{2,3},{3,2},{4,5},{5,4},{6,7},{7,6},{8,9},{9,8},{10,11... | collective-permute-start | bytes 3538952 | tf_op jit(solution)/shard_map/ppermute | solution.py:439
  126.4 49.8 %collective-permute-start.8 = (bf16[384,1536]{1,0:T(8,128)(2,1)S(1)}, bf16[384,1536]{1,0:T(8,128)(2,1)}, u32[]{:S(2)}, u32[]{:S(2)}) collective-permute-start(bf16[384,1536]{1,0:T(8,128)(2,1)S(1)} %get-tuple-element.89.refs_0_), channel_id=1, source_target_pairs={{0,2},{1,3},{2,0},{3,1},{4,6},{5,7},{6,4},{7,5},{8,10},{9,11},{10,... | collective-permute-start | bytes 3538952 | tf_op jit(solution)/shard_map/ppermute | solution.py:439
  147.7 52.8 %collective-permute-start.19 = (bf16[384,1536]{1,0:T(8,128)(2,1)S(1)}, bf16[384,1536]{1,0:T(8,128)(2,1)}, u32[]{:S(2)}, u32[]{:S(2)}) collective-permute-start(bf16[384,1536]{1,0:T(8,128)(2,1)S(1)} %collective-permute-done.15.refs_10_), channel_id=1, source_target_pairs={{0,4},{1,5},{2,6},{3,7},{4,0},{5,1},{6,2},{7,3},{8,12},{9,13},{10,... | collective-permute-start | bytes 3538952 | tf_op jit(solution)/shard_map/ppermute | solution.py:439
  150.0 51.2 %collective-permute-start.12 = (bf16[384,1536]{1,0:T(8,128)(2,1)}, bf16[384,1536]{1,0:T(8,128)(2,1)}, u32[]{:S(2)}, u32[]{:S(2)}) collective-permute-start(bf16[384,1536]{1,0:T(8,128)(2,1)} %collective-permute-done.10.refs_4_), channel_id=1, source_target_pairs={{0,2},{1,3},{2,0},{3,1},{4,6},{5,7},{6,4},{7,5},{8,10},{9,11},{10,... | collective-permute-start | bytes 3538952 | tf_op jit(solution)/shard_map/ppermute | solution.py:439
  175.3 93.6 %collective-permute-start.7 = (bf16[384,1536]{1,0:T(8,128)(2,1)S(1)}, bf16[384,1536]{1,0:T(8,128)(2,1)}, u32[]{:S(2)}, u32[]{:S(2)}) collective-permute-start(bf16[384,1536]{1,0:T(8,128)(2,1)S(1)} %get-tuple-element.89.refs_0_), channel_id=1, source_target_pairs={{0,1},{1,0},{2,3},{3,2},{4,5},{5,4},{6,7},{7,6},{8,9},{9,8},{10,11... | collective-permute-start | bytes 3538952 | tf_op jit(solution)/shard_map/ppermute | solution.py:439
  176.1 93.5 %collective-permute-start.16 = (bf16[384,1536]{1,0:T(8,128)(2,1)S(1)}, bf16[384,1536]{1,0:T(8,128)(2,1)}, u32[]{:S(2)}, u32[]{:S(2)}) collective-permute-start(bf16[384,1536]{1,0:T(8,128)(2,1)S(1)} %collective-permute-done.15.refs_10_), channel_id=1, source_target_pairs={{0,1},{1,0},{2,3},{3,2},{4,5},{5,4},{6,7},{7,6},{8,9},{9,8},{10,11... | collective-permute-start | bytes 3538952 | tf_op jit(solution)/shard_map/ppermute | solution.py:439
  176.1 93.8 %collective-permute-start.11 = (bf16[384,1536]{1,0:T(8,128)(2,1)}, bf16[384,1536]{1,0:T(8,128)(2,1)}, u32[]{:S(2)}, u32[]{:S(2)}) collective-permute-start(bf16[384,1536]{1,0:T(8,128)(2,1)} %collective-permute-done.10.refs_4_), channel_id=1, source_target_pairs={{0,1},{1,0},{2,3},{3,2},{4,5},{5,4},{6,7},{7,6},{8,9},{9,8},{10,11... | collective-permute-start | bytes 3538952 | tf_op jit(solution)/shard_map/ppermute | solution.py:439
  200.6 68.8 %collective-permute-start.18 = (bf16[384,1536]{1,0:T(8,128)(2,1)}, bf16[384,1536]{1,0:T(8,128)(2,1)}, u32[]{:S(2)}, u32[]{:S(2)}) collective-permute-start(bf16[384,1536]{1,0:T(8,128)(2,1)} %collective-permute-done.17.refs_12_), channel_id=1, source_target_pairs={{0,1},{1,0},{2,3},{3,2},{4,5},{5,4},{6,7},{7,6},{8,9},{9,8},{10,11... | collective-permute-start | bytes 3538952 | tf_op jit(solution)/shard_map/ppermute | solution.py:439
  201.2 68.7 %collective-permute-start.9 = (bf16[384,1536]{1,0:T(8,128)(2,1)}, bf16[384,1536]{1,0:T(8,128)(2,1)}, u32[]{:S(2)}, u32[]{:S(2)}) collective-permute-start(bf16[384,1536]{1,0:T(8,128)(2,1)} %collective-permute-done.8.refs_2_), channel_id=1, source_target_pairs={{0,1},{1,0},{2,3},{3,2},{4,5},{5,4},{6,7},{7,6},{8,9},{9,8},{10,11... | collective-permute-start | bytes 3538952 | tf_op jit(solution)/shard_map/ppermute | solution.py:439
  269.6 27.1 %collective-permute-start.31 = (bf16[384,1536]{1,0:T(8,128)(2,1)S(1)}, bf16[384,1536]{1,0:T(8,128)(2,1)S(1)}, u32[]{:S(2)}, u32[]{:S(2)}) collective-permute-start(bf16[384,1536]{1,0:T(8,128)(2,1)S(1)} %get-tuple-element.86.refs_8_), channel_id=1, source_target_pairs={{0,2},{1,3},{2,0},{3,1},{4,6},{5,7},{6,4},{7,5},{8,10},{9,11},{10,... | collective-permute-start | bytes 3538952 | tf_op jit(solution)/shard_map/ppermute | solution.py:439
  269.9 29.1 %collective-permute-start.26 = (bf16[384,1536]{1,0:T(8,128)(2,1)S(1)}, bf16[384,1536]{1,0:T(8,128)(2,1)S(1)}, u32[]{:S(2)}, u32[]{:S(2)}) collective-permute-start(bf16[384,1536]{1,0:T(8,128)(2,1)S(1)} %get-tuple-element.87.refs_0_), channel_id=1, source_target_pairs={{0,4},{1,5},{2,6},{3,7},{4,0},{5,1},{6,2},{7,3},{8,12},{9,13},{10,... | collective-permute-start | bytes 3538952 | tf_op jit(solution)/shard_map/ppermute | solution.py:439
  269.9 52.2 %collective-permute-start.33 = (bf16[384,1536]{1,0:T(8,128)(2,1)S(1)}, bf16[384,1536]{1,0:T(8,128)(2,1)}, u32[]{:S(2)}, u32[]{:S(2)}) collective-permute-start(bf16[384,1536]{1,0:T(8,128)(2,1)S(1)} %get-tuple-element.86.refs_8_), channel_id=1, source_target_pairs={{0,4},{1,5},{2,6},{3,7},{4,0},{5,1},{6,2},{7,3},{8,12},{9,13},{10,... | collective-permute-start | bytes 3538952 | tf_op jit(solution)/shard_map/ppermute | solution.py:439
  272.1 50.0 %collective-permute-start.24 = (bf16[384,1536]{1,0:T(8,128)(2,1)S(1)}, bf16[384,1536]{1,0:T(8,128)(2,1)S(1)}, u32[]{:S(2)}, u32[]{:S(2)}) collective-permute-start(bf16[384,1536]{1,0:T(8,128)(2,1)S(1)} %get-tuple-element.87.refs_0_), channel_id=1, source_target_pairs={{0,2},{1,3},{2,0},{3,1},{4,6},{5,7},{6,4},{7,5},{8,10},{9,11},{10,... | collective-permute-start | bytes 3538952 | tf_op jit(solution)/shard_map/ppermute | solution.py:439
  273.8 50.5 %collective-permute-start.21 = (bf16[192,3072]{1,0:T(8,128)(2,1)S(1)}, bf16[192,3072]{1,0:T(8,128)(2,1)S(1)}, u32[]{:S(2)}, u32[]{:S(2)}) collective-permute-start(bf16[192,3072]{1,0:T(8,128)(2,1)S(1)} %copy-done), channel_id=1, source_target_pairs={{0,1},{1,0},{2,3},{3,2},{4,5},{5,4},{6,7},{7,6},{8,9},{9,8},{10,11... | collective-permute-start | bytes 3538952 | tf_op jit(solution)/shard_map/ppermute | solution.py:439
  296.7 27.6 %collective-permute-start.22 = (bf16[192,3072]{1,0:T(8,128)(2,1)S(1)}, bf16[192,3072]{1,0:T(8,128)(2,1)S(1)}, u32[]{:S(2)}, u32[]{:S(2)}) collective-permute-start(bf16[192,3072]{1,0:T(8,128)(2,1)S(1)} %copy-done.1), channel_id=1, source_target_pairs={{0,1},{1,0},{2,3},{3,2},{4,5},{5,4},{6,7},{7,6},{8,9},{9,8},{10,11... | collective-permute-start | bytes 3538952 | tf_op jit(solution)/shard_map/ppermute | solution.py:439
  299.0 48.3 %collective-permute-start.28 = (bf16[384,1536]{1,0:T(8,128)(2,1)S(1)}, bf16[384,1536]{1,0:T(8,128)(2,1)S(1)}, u32[]{:S(2)}, u32[]{:S(2)}) collective-permute-start(bf16[384,1536]{1,0:T(8,128)(2,1)S(1)} %collective-permute-done.26.refs_4_), channel_id=1, source_target_pairs={{0,2},{1,3},{2,0},{3,1},{4,6},{5,7},{6,4},{7,5},{8,10},{9,11},{10,... | collective-permute-start | bytes 3538952 | tf_op jit(solution)/shard_map/ppermute | solution.py:439
  322.1 26.5 %collective-permute-start.35 = (bf16[384,1536]{1,0:T(8,128)(2,1)S(1)}, bf16[384,1536]{1,0:T(8,128)(2,1)S(1)}, u32[]{:S(2)}, u32[]{:S(2)}) collective-permute-start(bf16[384,1536]{1,0:T(8,128)(2,1)S(1)} %collective-permute-done.31.refs_10_), channel_id=1, source_target_pairs={{0,4},{1,5},{2,6},{3,7},{4,0},{5,1},{6,2},{7,3},{8,12},{9,13},{10,... | collective-permute-start | bytes 3538952 | tf_op jit(solution)/shard_map/ppermute | solution.py:439
  322.1 48.2 %collective-permute-start.30 = (bf16[384,1536]{1,0:T(8,128)(2,1)S(1)}, bf16[384,1536]{1,0:T(8,128)(2,1)S(1)}, u32[]{:S(2)}, u32[]{:S(2)}) collective-permute-start(bf16[384,1536]{1,0:T(8,128)(2,1)S(1)} %get-tuple-element.86.refs_8_), channel_id=1, source_target_pairs={{0,1},{1,0},{2,3},{3,2},{4,5},{5,4},{6,7},{7,6},{8,9},{9,8},{10,11... | collective-permute-start | bytes 3538952 | tf_op jit(solution)/shard_map/ppermute | solution.py:439
  324.2 47.1 %collective-permute-start.23 = (bf16[384,1536]{1,0:T(8,128)(2,1)S(1)}, bf16[384,1536]{1,0:T(8,128)(2,1)}, u32[]{:S(2)}, u32[]{:S(2)}) collective-permute-start(bf16[384,1536]{1,0:T(8,128)(2,1)S(1)} %get-tuple-element.87.refs_0_), channel_id=1, source_target_pairs={{0,1},{1,0},{2,3},{3,2},{4,5},{5,4},{6,7},{7,6},{8,9},{9,8},{10,11... | collective-permute-start | bytes 3538952 | tf_op jit(solution)/shard_map/ppermute | solution.py:439
  324.3 47.6 %collective-permute-start.27 = (bf16[384,1536]{1,0:T(8,128)(2,1)S(1)}, bf16[384,1536]{1,0:T(8,128)(2,1)}, u32[]{:S(2)}, u32[]{:S(2)}) collective-permute-start(bf16[384,1536]{1,0:T(8,128)(2,1)S(1)} %collective-permute-done.26.refs_4_), channel_id=1, source_target_pairs={{0,1},{1,0},{2,3},{3,2},{4,5},{5,4},{6,7},{7,6},{8,9},{9,8},{10,11... | collective-permute-start | bytes 3538952 | tf_op jit(solution)/shard_map/ppermute | solution.py:439
  347.3 25.1 %collective-permute-start.32 = (bf16[384,1536]{1,0:T(8,128)(2,1)S(1)}, bf16[384,1536]{1,0:T(8,128)(2,1)}, u32[]{:S(2)}, u32[]{:S(2)}) collective-permute-start(bf16[384,1536]{1,0:T(8,128)(2,1)S(1)} %collective-permute-done.31.refs_10_), channel_id=1, source_target_pairs={{0,1},{1,0},{2,3},{3,2},{4,5},{5,4},{6,7},{7,6},{8,9},{9,8},{10,11... | collective-permute-start | bytes 3538952 | tf_op jit(solution)/shard_map/ppermute | solution.py:439
  348.6 23.2 %collective-permute-start.25 = (bf16[384,1536]{1,0:T(8,128)(2,1)S(1)}, bf16[384,1536]{1,0:T(8,128)(2,1)}, u32[]{:S(2)}, u32[]{:S(2)}) collective-permute-start(bf16[384,1536]{1,0:T(8,128)(2,1)S(1)} %collective-permute-done.24.refs_2_), channel_id=1, source_target_pairs={{0,1},{1,0},{2,3},{3,2},{4,5},{5,4},{6,7},{7,6},{8,9},{9,8},{10,11... | collective-permute-start | bytes 3538952 | tf_op jit(solution)/shard_map/ppermute | solution.py:439
  371.3 4.7 collective-permute-start.29
  371.8 5.9 collective-permute-start.36
  371.9 18.2 %collective-permute-start.38 = (bf16[192,3072]{1,0:T(8,128)(2,1)S(1)}, bf16[192,3072]{1,0:T(8,128)(2,1)S(1)}, u32[]{:S(2)}, u32[]{:S(2)}) collective-permute-start(bf16[192,3072]{1,0:T(8,128)(2,1)S(1)} %copy-done.6), channel_id=1, source_target_pairs={{0,1},{1,0},{2,3},{3,2},{4,5},{5,4},{6,7},{7,6},{8,9},{9,8},{10,11... | collective-permute-start | bytes 3538952 | tf_op jit(solution)/shard_map/ppermute | solution.py:439
  372.4 19.1 %collective-permute-start.39 = (bf16[192,3072]{1,0:T(8,128)(2,1)S(1)}, bf16[192,3072]{1,0:T(8,128)(2,1)S(1)}, u32[]{:S(2)}, u32[]{:S(2)}) collective-permute-start(bf16[192,3072]{1,0:T(8,128)(2,1)S(1)} %copy-done.7), channel_id=1, source_target_pairs={{0,1},{1,0},{2,3},{3,2},{4,5},{5,4},{6,7},{7,6},{8,9},{9,8},{10,11... | collective-permute-start | bytes 3538952 | tf_op jit(solution)/shard_map/ppermute | solution.py:439
  374.4 54.4 %collective-permute-start.43 = (bf16[192,3072]{1,0:T(8,128)(2,1)S(1)}, bf16[192,3072]{1,0:T(8,128)(2,1)S(1)}, u32[]{:S(2)}, u32[]{:S(2)}) collective-permute-start(bf16[192,3072]{1,0:T(8,128)(2,1)S(1)} %copy-done.6), channel_id=1, source_target_pairs={{0,2},{1,3},{2,0},{3,1},{4,6},{5,7},{6,4},{7,5},{8,10},{9,11},{10,... | collective-permute-start | bytes 3538952 | tf_op jit(solution)/shard_map/ppermute | solution.py:439
  376.1 52.7 %collective-permute-start.37 = (bf16[192,3072]{1,0:T(8,128)(2,1)S(1)}, bf16[192,3072]{1,0:T(8,128)(2,1)}, u32[]{:S(2)}, u32[]{:S(2)}) collective-permute-start(bf16[192,3072]{1,0:T(8,128)(2,1)S(1)} %copy-done.6), channel_id=1, source_target_pairs={{0,4},{1,5},{2,6},{3,7},{4,0},{5,1},{6,2},{7,3},{8,12},{9,13},{10,... | collective-permute-start | bytes 3538952 | tf_op jit(solution)/shard_map/ppermute | solution.py:439
  377.8 51.0 %collective-permute-start.46 = (bf16[192,3072]{1,0:T(8,128)(2,1)S(1)}, bf16[192,3072]{1,0:T(8,128)(2,1)S(1)}, u32[]{:S(2)}, u32[]{:S(2)}) collective-permute-start(bf16[192,3072]{1,0:T(8,128)(2,1)S(1)} %copy-done.7), channel_id=1, source_target_pairs={{0,4},{1,5},{2,6},{3,7},{4,0},{5,1},{6,2},{7,3},{8,12},{9,13},{10,... | collective-permute-start | bytes 3538952 | tf_op jit(solution)/shard_map/ppermute | solution.py:439
  390.0 38.7 %collective-permute-start.41 = (bf16[192,3072]{1,0:T(8,128)(2,1)S(1)}, bf16[192,3072]{1,0:T(8,128)(2,1)S(1)}, u32[]{:S(2)}, u32[]{:S(2)}) collective-permute-start(bf16[192,3072]{1,0:T(8,128)(2,1)S(1)} %copy-done.7), channel_id=1, source_target_pairs={{0,2},{1,3},{2,0},{3,1},{4,6},{5,7},{6,4},{7,5},{8,10},{9,11},{10,... | collective-permute-start | bytes 3538952 | tf_op jit(solution)/shard_map/ppermute | solution.py:439
  429.8 4.4 collective-permute-start.45
  429.8 6.0 collective-permute-start.44
  431.3 6.4 collective-permute-start.48
  431.4 45.1 %collective-permute-start.40 = (bf16[192,3072]{1,0:T(8,128)(2,1)}, bf16[192,3072]{1,0:T(8,128)(2,1)S(1)}, u32[]{:S(2)}, u32[]{:S(2)}) collective-permute-start(bf16[192,3072]{1,0:T(8,128)(2,1)} %collective-permute-done.37.refs_4_.refs_8_), channel_id=1, source_target_pairs={{0,2},{1,3},{2,0},{3,1},{4,6},{5,7},{6,4},{7,5},{8,10},{9,11},{10,... | collective-permute-start | bytes 3538952 | tf_op jit(solution)/shard_map/ppermute | solution.py:439
  432.6 43.9 %collective-permute-start.42 = (bf16[192,3072]{1,0:T(8,128)(2,1)S(1)}, bf16[192,3072]{1,0:T(8,128)(2,1)S(1)}, u32[]{:S(2)}, u32[]{:S(2)}) collective-permute-start(bf16[192,3072]{1,0:T(8,128)(2,1)S(1)} %collective-permute-done.41.refs_1_.refs_5_), channel_id=1, source_target_pairs={{0,4},{1,5},{2,6},{3,7},{4,0},{5,1},{6,2},{7,3},{8,12},{9,13},{10,... | collective-permute-start | bytes 3538952 | tf_op jit(solution)/shard_map/ppermute | solution.py:439
  477.0 39.1 %collective-permute-start.62 = (bf16[128,3072]{1,0:T(8,128)(2,1)}, bf16[128,3072]{1,0:T(8,128)(2,1)}, u32[]{:S(2)}, u32[]{:S(2)}) collective-permute-start(bf16[128,3072]{1,0:T(8,128)(2,1)} %get-tuple-element.72.refs_8_.refs_24_), channel_id=1, source_target_pairs={{0,4},{1,5},{2,6},{3,7},{4,0},{5,1},{6,2},{7,3},{8,12},{9,13},{10,... | collective-permute-start | bytes 2359304 | tf_op jit(solution)/shard_map/ppermute | solution.py:439
  477.1 37.1 %collective-permute-start.60 = (bf16[128,3072]{1,0:T(8,128)(2,1)}, bf16[128,3072]{1,0:T(8,128)(2,1)}, u32[]{:S(2)}, u32[]{:S(2)}) collective-permute-start(bf16[128,3072]{1,0:T(8,128)(2,1)} %get-tuple-element.72.refs_8_.refs_24_), channel_id=1, source_target_pairs={{0,2},{1,3},{2,0},{3,1},{4,6},{5,7},{6,4},{7,5},{8,10},{9,11},{10,... | collective-permute-start | bytes 2359304 | tf_op jit(solution)/shard_map/ppermute | solution.py:439
  478.4 34.5 %collective-permute-start.55 = (bf16[128,3072]{1,0:T(8,128)(2,1)}, bf16[128,3072]{1,0:T(8,128)(2,1)}, u32[]{:S(2)}, u32[]{:S(2)}) collective-permute-start(bf16[128,3072]{1,0:T(8,128)(2,1)} %get-tuple-element.46.refs_0_.refs_16_), channel_id=1, source_target_pairs={{0,4},{1,5},{2,6},{3,7},{4,0},{5,1},{6,2},{7,3},{8,12},{9,13},{10,... | collective-permute-start | bytes 2359304 | tf_op jit(solution)/shard_map/ppermute | solution.py:439
  479.7 36.4 %collective-permute-start.53 = (bf16[128,3072]{1,0:T(8,128)(2,1)}, bf16[128,3072]{1,0:T(8,128)(2,1)}, u32[]{:S(2)}, u32[]{:S(2)}) collective-permute-start(bf16[128,3072]{1,0:T(8,128)(2,1)} %get-tuple-element.46.refs_0_.refs_16_), channel_id=1, source_target_pairs={{0,2},{1,3},{2,0},{3,1},{4,6},{5,7},{6,4},{7,5},{8,10},{9,11},{10,... | collective-permute-start | bytes 2359304 | tf_op jit(solution)/shard_map/ppermute | solution.py:439
  512.9 19.8 %collective-permute-start.57 = (bf16[128,3072]{1,0:T(8,128)(2,1)}, bf16[128,3072]{1,0:T(8,128)(2,1)S(1)}, u32[]{:S(2)}, u32[]{:S(2)}) collective-permute-start(bf16[128,3072]{1,0:T(8,128)(2,1)} %collective-permute-done.55.refs_4_.refs_20_), channel_id=1, source_target_pairs={{0,2},{1,3},{2,0},{3,1},{4,6},{5,7},{6,4},{7,5},{8,10},{9,11},{10,... | collective-permute-start | bytes 2359304 | tf_op jit(solution)/shard_map/ppermute | solution.py:439
  514.2 18.9 %collective-permute-start.64 = (bf16[128,3072]{1,0:T(8,128)(2,1)}, bf16[128,3072]{1,0:T(8,128)(2,1)S(1)}, u32[]{:S(2)}, u32[]{:S(2)}) collective-permute-start(bf16[128,3072]{1,0:T(8,128)(2,1)} %collective-permute-done.60.refs_10_.refs_26_), channel_id=1, source_target_pairs={{0,4},{1,5},{2,6},{3,7},{4,0},{5,1},{6,2},{7,3},{8,12},{9,13},{10,... | collective-permute-start | bytes 2359304 | tf_op jit(solution)/shard_map/ppermute | solution.py:439
  514.3 20.0 %collective-permute-start.59 = (bf16[128,3072]{1,0:T(8,128)(2,1)}, bf16[128,3072]{1,0:T(8,128)(2,1)S(1)}, u32[]{:S(2)}, u32[]{:S(2)}) collective-permute-start(bf16[128,3072]{1,0:T(8,128)(2,1)} %get-tuple-element.72.refs_8_.refs_24_), channel_id=1, source_target_pairs={{0,1},{1,0},{2,3},{3,2},{4,5},{5,4},{6,7},{7,6},{8,9},{9,8},{10,11... | collective-permute-start | bytes 2359304 | tf_op jit(solution)/shard_map/ppermute | solution.py:439
  516.1 18.3 %collective-permute-start.52 = (bf16[128,3072]{1,0:T(8,128)(2,1)S(1)}, bf16[128,3072]{1,0:T(8,128)(2,1)S(1)}, u32[]{:S(2)}, u32[]{:S(2)}) collective-permute-start(bf16[128,3072]{1,0:T(8,128)(2,1)S(1)} %copy-done.35), channel_id=1, source_target_pairs={{0,1},{1,0},{2,3},{3,2},{4,5},{5,4},{6,7},{7,6},{8,9},{9,8},{10,11... | collective-permute-start | bytes 2359304 | tf_op jit(solution)/shard_map/ppermute | solution.py:439
  516.2 20.5 %collective-permute-start.54 = (bf16[128,3072]{1,0:T(8,128)(2,1)}, bf16[128,3072]{1,0:T(8,128)(2,1)S(1)}, u32[]{:S(2)}, u32[]{:S(2)}) collective-permute-start(bf16[128,3072]{1,0:T(8,128)(2,1)} %collective-permute-done.53.refs_2_.refs_18_), channel_id=1, source_target_pairs={{0,1},{1,0},{2,3},{3,2},{4,5},{5,4},{6,7},{7,6},{8,9},{9,8},{10,11... | collective-permute-start | bytes 2359304 | tf_op jit(solution)/shard_map/ppermute | solution.py:439
  532.8 4.9 collective-permute-start.56
  533.1 5.0 collective-permute-start.61
  537.6 56.8 %collective-permute-start.69 = (bf16[192,3072]{1,0:T(8,128)(2,1)S(1)}, bf16[192,3072]{1,0:T(8,128)(2,1)S(1)}, u32[]{:S(2)}, u32[]{:S(2)}) collective-permute-start(bf16[192,3072]{1,0:T(8,128)(2,1)S(1)} %copy-done), channel_id=1, source_target_pairs={{0,2},{1,3},{2,0},{3,1},{4,6},{5,7},{6,4},{7,5},{8,10},{9,11},{10,... | collective-permute-start | bytes 3538952 | tf_op jit(solution)/shard_map/ppermute | solution.py:439
  538.1 56.4 %collective-permute-start.51 = (bf16[192,3072]{1,0:T(8,128)(2,1)S(1)}, bf16[192,3072]{1,0:T(8,128)(2,1)S(1)}, u32[]{:S(2)}, u32[]{:S(2)}) collective-permute-start(bf16[192,3072]{1,0:T(8,128)(2,1)S(1)} %copy-done), channel_id=1, source_target_pairs={{0,4},{1,5},{2,6},{3,7},{4,0},{5,1},{6,2},{7,3},{8,12},{9,13},{10,... | collective-permute-start | bytes 3538952 | tf_op jit(solution)/shard_map/ppermute | solution.py:439
  538.3 56.1 %collective-permute-start.72 = (bf16[192,3072]{1,0:T(8,128)(2,1)S(1)}, bf16[192,3072]{1,0:T(8,128)(2,1)}, u32[]{:S(2)}, u32[]{:S(2)}) collective-permute-start(bf16[192,3072]{1,0:T(8,128)(2,1)S(1)} %copy-done.1), channel_id=1, source_target_pairs={{0,4},{1,5},{2,6},{3,7},{4,0},{5,1},{6,2},{7,3},{8,12},{9,13},{10,... | collective-permute-start | bytes 3538952 | tf_op jit(solution)/shard_map/ppermute | solution.py:439
  539.6 54.9 %collective-permute-start.67 = (bf16[192,3072]{1,0:T(8,128)(2,1)S(1)}, bf16[192,3072]{1,0:T(8,128)(2,1)S(1)}, u32[]{:S(2)}, u32[]{:S(2)}) collective-permute-start(bf16[192,3072]{1,0:T(8,128)(2,1)S(1)} %copy-done.1), channel_id=1, source_target_pairs={{0,2},{1,3},{2,0},{3,1},{4,6},{5,7},{6,4},{7,5},{8,10},{9,11},{10,... | collective-permute-start | bytes 3538952 | tf_op jit(solution)/shard_map/ppermute | solution.py:439
  596.1 5.8 collective-permute-start.70
  596.6 7.0 %collective-permute-start.74 = (bf16[192,3072]{1,0:T(8,128)(2,1)}, bf16[192,3072]{1,0:T(8,128)(2,1)S(1)}, u32[]{:S(2)}, u32[]{:S(2)}) collective-permute-start(bf16[192,3072]{1,0:T(8,128)(2,1)} %collective-permute-done.72.refs_5_.refs_9_), channel_id=1, source_target_pairs={{0,1},{1,0},{2,3},{3,2},{4,5},{5,4},{6,7},{7,6},{8,9},{9,8},{10,11... | collective-permute-start | bytes 3538952 | tf_op jit(solution)/shard_map/ppermute | solution.py:439
  596.6 45.3 %collective-permute-start.66 = (bf16[192,3072]{1,0:T(8,128)(2,1)S(1)}, bf16[192,3072]{1,0:T(8,128)(2,1)S(1)}, u32[]{:S(2)}, u32[]{:S(2)}) collective-permute-start(bf16[192,3072]{1,0:T(8,128)(2,1)S(1)} %collective-permute-done.51.refs_4_.refs_8_), channel_id=1, source_target_pairs={{0,2},{1,3},{2,0},{3,1},{4,6},{5,7},{6,4},{7,5},{8,10},{9,11},{10,... | collective-permute-start | bytes 3538952 | tf_op jit(solution)/shard_map/ppermute | solution.py:439
  598.5 43.3 %collective-permute-start.68 = (bf16[192,3072]{1,0:T(8,128)(2,1)S(1)}, bf16[192,3072]{1,0:T(8,128)(2,1)S(1)}, u32[]{:S(2)}, u32[]{:S(2)}) collective-permute-start(bf16[192,3072]{1,0:T(8,128)(2,1)S(1)} %collective-permute-done.67.refs_1_.refs_5_), channel_id=1, source_target_pairs={{0,4},{1,5},{2,6},{3,7},{4,0},{5,1},{6,2},{7,3},{8,12},{9,13},{10,... | collective-permute-start | bytes 3538952 | tf_op jit(solution)/shard_map/ppermute | solution.py:439
  (82 other events, 1065.6 us)

commit v3 on v2

--- a/solution.py
+++ b/solution.py
@@ -76,7 +76,7 @@
         ],
         out_specs=pl.BlockSpec((1, tokens, total), lambda i: (i, 0, 0)),
         out_shape=jax.ShapeDtypeStruct((n_dev, tokens, total), BF16),
-        compiler_params=pltpu.CompilerParams(dimension_semantics=("arbitrary",), vmem_limit_bytes=48 * 1024 * 1024),
+        compiler_params=pltpu.CompilerParams(dimension_semantics=("arbitrary",), vmem_limit_bytes=60 * 1024 * 1024),
         cost_estimate=pl.CostEstimate(flops=flops, bytes_accessed=60_000_000, transcendentals=0),
         name="project",
     )(hidden, grad_out, w_q, w_k, w_v, w_o, cos_tab, sin_tab)
@@ -243,14 +243,17 @@
     )(first_blk, packed, packed, packed, packed, starts, cos_t, sin_t)
 
 
-def assemble_kernel(turn, half_steps, me_ref, *refs):
+def assemble_kernel(turn, half_steps, rels, me_ref, *refs):
     out_ref = refs[-1]
-    n_dev = len(refs) // 2
+    count = len(rels)
 
     def fill(ins):
-        for rel, ref in enumerate(ins):
+        for rel, ref in zip(rels, ins):
             tokens = ref.shape[0]
-            place = pl.ds(pl.multiple_of((me_ref[0] ^ rel) * tokens, tokens), tokens)
+            slot = me_ref[0] ^ rel
+            if count == 2:
+                slot = slot % 2
+            place = pl.ds(pl.multiple_of(slot * tokens, tokens), tokens)
             if turn:
                 out_ref[:, place] = ref[...].T
             else:
@@ -258,36 +261,45 @@
 
     @pl.when(pl.program_id(0) < half_steps)
     def _():
-        fill(refs[:n_dev])
+        fill(refs[:count])
 
     @pl.when(pl.program_id(0) >= half_steps)
     def _():
-        fill(refs[n_dev:2 * n_dev])
-
-
-def assemble(low, high, me, turn):
+        fill(refs[count:2 * count])
+
+
+def assemble(got, rels, n_dev, prev, me, turn):
+    low, high = [got[0][rel] for rel in rels], [got[1][rel] for rel in rels]
     tokens, half_width = low[0].shape
-    seq, width = tokens * len(low), 2 * half_width
+    seq, width = tokens * n_dev, 2 * half_width
     col_blk = 512
     steps = half_width // col_blk
+    span = seq if prev is None else 2 * tokens
+    pair = rels[0] // 2
+    place = (lambda me: 0) if prev is None else (lambda me: (me[0] // 2) ^ pair)
     if turn:
-        out_spec, shape = pl.BlockSpec((col_blk, seq), lambda i, me: (i, 0)), (width, seq)
+        out_spec, shape = pl.BlockSpec((col_blk, span), lambda i, me: (i, place(me))), (width, seq)
     else:
-        out_spec, shape = pl.BlockSpec((seq, col_blk), lambda i, me: (0, i)), (seq, width)
+        out_spec, shape = pl.BlockSpec((span, col_blk), lambda i, me: (place(me), i)), (seq, width)
     low_specs = [pl.BlockSpec((tokens, col_blk), lambda i, me: (0, jnp.minimum(i, steps - 1))) for _ in low]
     high_specs = [pl.BlockSpec((tokens, col_blk), lambda i, me: (0, jnp.maximum(i - steps, 0))) for _ in high]
+    body = functools.partial(assemble_kernel, turn, steps, rels)
+    extra, extra_specs, alias = [], [], {}
+    if prev is not None:
+        extra, extra_specs, alias = [prev], [pl.BlockSpec(memory_space=pl.ANY)], {1 + 2 * len(rels): 0}
     return pl.pallas_call(
-        functools.partial(assemble_kernel, turn, steps),
+        body,
         grid_spec=pltpu.PrefetchScalarGridSpec(
             num_scalar_prefetch=1,
             grid=(2 * steps,),
-            in_specs=low_specs + high_specs,
+            in_specs=low_specs + high_specs + extra_specs,
             out_specs=out_spec,
         ),
         out_shape=jax.ShapeDtypeStruct(shape, BF16),
-        compiler_params=pltpu.CompilerParams(dimension_semantics=("arbitrary",), vmem_limit_bytes=28 * 1024 * 1024),
-        cost_estimate=pl.CostEstimate(flops=0, bytes_accessed=4 * seq * width, transcendentals=0),
-    )(me, *low, *high)
+        input_output_aliases=alias,
+        compiler_params=pltpu.CompilerParams(dimension_semantics=("arbitrary",), vmem_limit_bytes=60 * 1024 * 1024),
+        cost_estimate=pl.CostEstimate(flops=0, bytes_accessed=4 * len(rels) * tokens * width, transcendentals=0),
+    )(me, *low, *high, *extra)
 
 
 def own_kernel(kinds, turned, me_ref, *refs):
@@ -337,7 +349,7 @@
             scratch_shapes=[pltpu.VMEM((tokens, depth), BF16)],
         ),
         out_shape=jax.ShapeDtypeStruct((tokens, width), BF16),
-        compiler_params=pltpu.CompilerParams(dimension_semantics=("arbitrary",), vmem_limit_bytes=32 * 1024 * 1024),
+        compiler_params=pltpu.CompilerParams(dimension_semantics=("arbitrary",), vmem_limit_bytes=60 * 1024 * 1024),
         cost_estimate=pl.CostEstimate(flops=2 * tokens * width * depth, bytes_accessed=2 * depth * (width + tokens), transcendentals=0),
     )(me, *flat, *weights)
 
@@ -424,7 +436,7 @@
         ),
         out_shape=[jax.ShapeDtypeStruct(shape, F32)] * n_out,
         input_output_aliases={n_fixed + o: o for o in range(len(prev))},
-        compiler_params=pltpu.CompilerParams(dimension_semantics=("arbitrary",), vmem_limit_bytes=48 * 1024 * 1024),
+        compiler_params=pltpu.CompilerParams(dimension_semantics=("arbitrary",), vmem_limit_bytes=60 * 1024 * 1024),
         cost_estimate=pl.CostEstimate(flops=2 * rows * width * seq, bytes_accessed=4 * width * rows + 2 * seq * (width + rows), transcendentals=0),
     )(me, big, *parts, *prev)
 
@@ -469,13 +481,8 @@
         freqs = rope_freqs()
         me = lax.axis_index("sp").astype(jnp.int32)
         me_arr = me[None]
-        idx = {0: jnp.stack([positions, doc_ids])}
-        idx[SIDE_X], idx[SIDE_Y] = swap(idx[0], SIDE_X), swap(idx[0], SIDE_Y)
-        idx[SIDE_X | SIDE_Y] = swap(idx[0], SIDE_X | SIDE_Y)
-        for rel in (0, SIDE_X, SIDE_Y, SIDE_X | SIDE_Y):
-            idx[rel | CORE] = swap(idx[0], rel | CORE)
-        order = me ^ jnp.arange(n_dev, dtype=jnp.int32)
-        idx_all = jnp.take(jnp.stack([idx[rel] for rel in range(n_dev)]), order, axis=0)
+        idx_all = lax.all_gather(jnp.stack([positions, doc_ids])[None], "sp", axis=0, tiled=True)
+        idx_all, hidden, grad_out = lax.optimization_barrier((idx_all, hidden, grad_out))
         pos_all = idx_all[:, 0, :].reshape(seq)
         doc_all = idx_all[:, 1, :].reshape(seq)
         starts = jnp.sum((doc_all[None, :] < doc_all[:, None]).astype(jnp.int32), axis=1)
@@ -499,6 +506,8 @@
         packed = project(hidden, grad_out, w_q, w_k, w_v, w_o, cos_tab, sin_tab, n_dev, group)
         packed = lax.all_to_all(packed, "sp", 0, 0, tiled=True).reshape(seq, -1)
         relay(x_got)
+        near, far = tuple(range(6)), (6, 7)
+        x_turned = assemble(x_got, near, n_dev, None, me_arr, True)
         g_got = reach(grad_out[:, :half], grad_out[:, half:])
         ctx_lo, ctx_hi, dq_lo, dq_hi, dk_t, dv_t = attention(packed, first_blk, starts[None, :], cos_t, sin_t, group)
         finish(x_got, dk_t)
@@ -506,12 +515,13 @@
         ctx_got = reach(ctx_lo, ctx_hi)
         dq_got = reach(dq_lo, dq_hi)
 
-        x_turned = assemble([x_got[0][r] for r in every], [x_got[1][r] for r in every], after(me_arr, dk_t), True)
+        x_turned = assemble(x_got, far, n_dev, x_turned, after(me_arr, dk_t), True)
         hold(g_got, x_turned)
         relay(g_got)
         (g_q,) = weight_grad(x_turned, pairs(dq_got, (0,)) + [swap(dq_got[0][0], CORE), swap(dq_got[1][0], CORE)], groups[0], me_arr, None, False, 1, n_dev)
-        finish(g_got, g_q)
-        g_all = assemble([g_got[0][r] for r in every], [g_got[1][r] for r in every], after(me_arr, g_q), False)
+        g_all = assemble(g_got, near, n_dev, None, after(me_arr, g_q), False)
+        finish(g_got, g_all)
+        g_all = assemble(g_got, far, n_dev, g_all, me_arr, False)
         (g_o,) = weight_grad(g_all, pairs(ctx_got, (0,)) + [swap(ctx_got[0][0], CORE), swap(ctx_got[1][0], CORE)], groups[0], me_arr, None, True, 1, n_dev)
         hold(ctx_got, g_o)
         relay(ctx_got)

time: 705 us -> 659 us (0.935)
  waiting for transfers between devices: 223 us -> 186 us
  local copies, waits for them, and re-layouts: 47.9 us -> 11.5 us
  Pallas kernels: 359 us -> 388 us
  blocking collectives: 0 us -> 11.4 us
  starting transfers between devices: 54.7 us -> 43.8 us
    ppermute x77 -> x70, waiting for transfers between devices: 223 us -> 186 us  [swap(): return lax.ppermute(values, 'sp', [(i, i ^ bit) for i in range(n_dev)])]
    unnamed x142 -> x74, local copies, waits for them, and re-layouts: 42.7 us -> 6.9 us
    pallas_call x2 -> x4, Pallas kernels: 24.4 us -> 40.9 us  [assemble(): pl.pallas_call(body, grid_spec=pltpu.PrefetchScalarGridSpec(num_scalar_pr...]
    all_gather x0 -> x1, blocking collectives: none -> 11.4 us  [device_body(): lax.all_gather(jnp.stack([positions, doc_ids])[None], 'sp', axis=0, tiled...]
    ppermute x77 -> x70, starting transfers between devices: 49 us -> 38.5 us  [swap(): return lax.ppermute(values, 'sp', [(i, i ^ bit) for i in range(n_dev)])]
    pallas_call x7, Pallas kernels: 198 us -> 208 us  [weight_grad(): pl.pallas_call(body, grid_spec=pltpu.PrefetchScalarGridSpec(num_scalar_pr...]
  transfers between devices with their start and end apart: 78 -> 71, of which waited for: 25 -> 29; matrix products, arithmetic and copies ran while one was open for 3% -> 2% of each run, Pallas kernels for 41% -> 47%
where the time goes in v3:
time: 659 us; the launch traced here: 655 us
  Pallas kernels  388 us (59%)
  waiting for transfers between devices  186 us (28%)
  starting transfers between devices  43.8 us (7%)
  other arithmetic  12.1 us (2%)
  local copies, waits for them, and re-layouts  11.5 us (2%)
  blocking collectives  11.4 us (2%)
    pallas_call x7, Pallas kernels, weight_grad(): pl.pallas_call(body, grid_spec=pltpu.PrefetchScalarGridSpec(num_scalar_pr...  208 us
    ppermute x70, waiting for transfers between devices, swap(): return lax.ppermute(values, 'sp', [(i, i ^ bit) for i in range(n_dev)])  186 us
    pallas_call x1, Pallas kernels, attention(): pl.pallas_call(functools.partial(attn_kernel, group), grid_spec=grid_spec...  67.7 us
    pallas_call x4, Pallas kernels, assemble(): pl.pallas_call(body, grid_spec=pltpu.PrefetchScalarGridSpec(num_scalar_pr...  40.9 us
    ppermute x70, starting transfers between devices, swap(): return lax.ppermute(values, 'sp', [(i, i ^ bit) for i in range(n_dev)])  38.5 us
    pallas_call x1, Pallas kernels, project(): pl.pallas_call(functools.partial(proj_kernel, group), grid=(n_dev,), in_s...  36.9 us
    pallas_call x2, Pallas kernels, own_product(): pl.pallas_call(functools.partial(own_kernel, kinds, turned), grid_spec=pl...  35 us
  transfers between devices with their start and end apart: 71, of which 29 were waited for; matrix products, arithmetic and copies ran while one was open for 2% of the time, Pallas kernels for 47%

profile of v3, /device:TPU:1, one launch (start us, length us, event | category | flops | bytes accessed | tf_op | source)
XLA Modules:
  0.0 654.6 jit_solution(7725917343211756542)
XLA Ops:
  2.7 11.4 %all-gather.1 = s32[8,2,384]{2,1,0:T(2,128)} all-gather(s32[1,2,384]{2,1,0:T(2,128)S(1)} %add_bitcast_fusion), channel_id=2, replica_groups=mesh['dp'=2,'sp'=8] {'sp'}, dimensions={0}, use_global_device_ids=true | all-gather | bytes 27648 | tf_op jit(solution)/shard_map/all_gather | solution.py:484
  14.9 0.9 pad_maximum_fusion
  15.8 36.9 %project.1 = bf16[8,384,1024]{2,1,0:T(8,128)(2,1)} custom-call(bf16[384,3072]{1,0:T(8,128)(2,1)} %x_ref, bf16[384,3072]{1,0:T(8,128)(2,1)} %g_ref, bf16[3072,3072]{1,0:T(8,128)(2,1)} %refs_32_.1, bf16[3072,1024]{1,0:T(8,128)(2,1)} %refs_33_.1, bf16[3072,1024]{1,0:T(8,128)(2,1)} %refs_34_.1, bf16[3072,3072]{1,0:T(8,128)(2,1)} %refs_16_.1, ...), custom_call_target="tpu_custom_call" | custom-call | flops 19327352832 | bytes 60000000 | tf_op jit(solution)/shard_map/project/pallas_call | solution.py:64
  52.7 5.4 all-to-all-start
  58.1 1.8 fusion.2
  59.9 1.4 collective-permute-start.13
  62.0 1.2 collective-permute-start.4
  63.5 4.6 convert_reduce_fusion
  68.0 1.3 slice.23
  69.3 1.2 and_select_fusion.lo_ref
  70.6 3.8 multiply_sine_fusion
  74.4 78.6 %collective-permute-done.13.refs_10_ = bf16[384,1536]{1,0:T(8,128)(2,1)S(1)} collective-permute-done((bf16[384,1536]{1,0:T(8,128)(2,1)S(1)}, bf16[384,1536]{1,0:T(8,128)(2,1)S(1)}, u32[]{:S(2)}, u32[]{:S(2)}) %collective-permute-start.13) | collective-permute-done | bytes 1179680 | tf_op jit(solution)/shard_map/ppermute | solution.py:451
  153.0 1.5 collective-permute-start.7
  154.7 1.2 collective-permute-start.5
  155.9 22.6 %collective-permute-done.8.refs_2_ = bf16[384,1536]{1,0:T(8,128)(2,1)} collective-permute-done((bf16[384,1536]{1,0:T(8,128)(2,1)S(1)}, bf16[384,1536]{1,0:T(8,128)(2,1)}, u32[]{:S(2)}, u32[]{:S(2)}) %collective-permute-start.8) | collective-permute-done | bytes 1179680 | tf_op jit(solution)/shard_map/ppermute | solution.py:451
  178.4 0.9 collective-permute-start.14
  180.1 67.7 %attention.1 = (bf16[192,3072]{1,0:T(8,128)(2,1)}, bf16[192,3072]{1,0:T(8,128)(2,1)}, bf16[192,3072]{1,0:T(8,128)(2,1)}, bf16[192,3072]{1,0:T(8,128)(2,1)}, bf16...) custom-call(s32[12]{0:T(128)} %and_select_fusion.lo_ref, bf16[3072,1024]{1,0:T(8,128)(2,1)} %bitcast.3.q_ref.do_ref.k_ref.v_ref, ...), custom_call_target="tpu_custom_call" | custom-call | flops 72477573120 | bytes 12000000 | tf_op jit(solution)/shard_map/attention/pallas_call | solution.py:229
  249.9 1.4 collective-permute-done.9.refs_3_
  251.7 1.3 collective-permute-done.10.refs_5_
  252.9 0.9 collective-permute-start.23
  253.8 0.8 collective-permute-done.3.refs_1_
  254.6 1.0 copy-done.21
  255.6 0.9 collective-permute-start.19
  256.5 14.3 %shard_map.127.refs_4_ = bf16[3072,3072]{1,0:T(8,128)(2,1)} custom-call(s32[1]{0:T(128)} %bitcast.me_ref, bf16[384,1536]{1,0:T(8,128)(2,1)} %copy-done.1, bf16[384,1536]{1,0:T(8,128)(2,1)} %collective-permute-done.7.refs_1_, bf16[384,1536]{1,0:T(8,128)(2,1)} %collective-permute-done.8.refs_2_, bf16[384,1536]{1,0:T(8,128)(2,1)} %copy-done.20, ...), custom_call_target="tpu_custom_call" | custom-call | bytes 28311552 | tf_op jit(solution)/shard_map/pallas_call | solution.py:290
  271.5 6.9 %shard_map.128.big_ref = bf16[3072,3072]{1,0:T(8,128)(2,1)} custom-call(s32[1]{0:T(128)} %bitcast.me_ref, bf16[384,1536]{1,0:T(8,128)(2,1)} %collective-permute-done.2.refs_0_, bf16[384,1536]{1,0:T(8,128)(2,1)} %copy-done.21, bf16[384,1536]{1,0:T(8,128)(2,1)} %collective-permute-done.5.refs_2_, ...), custom_call_target="tpu_custom_call", output_to_operand_aliasing={{}: (5, {})} | custom-call | bytes 9437184 | tf_op jit(solution)/shard_map/pallas_call | solution.py:290
  278.8 23.1 %collective-permute-done.25.refs_10_ = bf16[384,1536]{1,0:T(8,128)(2,1)} collective-permute-done((bf16[384,1536]{1,0:T(8,128)(2,1)S(1)}, bf16[384,1536]{1,0:T(8,128)(2,1)}, u32[]{:S(2)}, u32[]{:S(2)}) %collective-permute-start.25) | collective-permute-done | bytes 1179680 | tf_op jit(solution)/shard_map/ppermute | solution.py:451
  301.9 1.3 collective-permute-start.16
  303.2 2.3 collective-permute-done.19.refs_2_
  305.5 1.2 collective-permute-start.21
  306.7 0.9 collective-permute-start.15
  307.6 0.8 collective-permute-start.28
  308.4 1.1 copy-done.7
  310.6 20.7 %shard_map.129.refs_8_ = f32[3072,3072]{1,0:T(8,128)} custom-call(s32[1]{0:T(128)} %bitcast.me_ref, bf16[3072,3072]{1,0:T(8,128)(2,1)} %shard_map.128.big_ref, bf16[192,3072]{1,0:T(8,128)(2,1)} %get-tuple-element.57.refs_0_, bf16[192,3072]{1,0:T(8,128)(2,1)} %get-tuple-element.58.refs_1_, bf16[192,3072]{1,0:T(8,128)(2,1)} %copy-done.7, ...), custom_call_target="tpu_custom_call" | custom-call | flops 14495514624 | bytes 33030144 | tf_op jit(solution)/shard_map/pallas_call | solution.py:424
  331.3 1.0 copy-done.24
  332.3 13.3 %shard_map.130.refs_4_ = bf16[3072,3072]{1,0:T(8,128)(2,1)} custom-call(s32[1]{0:T(128)} %bitcast.me_ref, bf16[384,1536]{1,0:T(8,128)(2,1)} %copy-done.3, bf16[384,1536]{1,0:T(8,128)(2,1)} %copy-done.19, bf16[384,1536]{1,0:T(8,128)(2,1)} %collective-permute-done.19.refs_2_, bf16[384,1536]{1,0:T(8,128)(2,1)} %collective-permute-done.20.refs_3_, ...), custom_call_target="tpu_custom_call" | custom-call | bytes 28311552 | tf_op jit(solution)/shard_map/pallas_call | solution.py:290
  346.9 1.8 collective-permute-done.27.refs_1_
  350.4 1.0 copy-done.25
  352.1 6.4 shard_map.131.big_ref
  359.5 20.5 %shard_map.132.refs_8_ = f32[3072,3072]{1,0:T(8,128)} custom-call(s32[1]{0:T(128)} %bitcast.me_ref, bf16[3072,3072]{1,0:T(8,128)(2,1)} %shard_map.131.big_ref, bf16[192,3072]{1,0:T(8,128)(2,1)} %get-tuple-element.65.refs_0_, bf16[192,3072]{1,0:T(8,128)(2,1)} %get-tuple-element.66.refs_1_, bf16[192,3072]{1,0:T(8,128)(2,1)} %copy-done.10, ...), custom_call_target="tpu_custom_call" | custom-call | flops 14495514624 | bytes 33030144 | tf_op jit(solution)/shard_map/pallas_call | solution.py:424
  380.0 21.5 %collective-permute-done.39.refs_5_.refs_9_ = bf16[192,3072]{1,0:T(8,128)(2,1)} collective-permute-done((bf16[192,3072]{1,0:T(8,128)(2,1)S(1)}, bf16[192,3072]{1,0:T(8,128)(2,1)}, u32[]{:S(2)}, u32[]{:S(2)}) %collective-permute-start.39) | collective-permute-done | bytes 1179680 | tf_op jit(solution)/shard_map/ppermute | solution.py:451
  401.5 1.0 collective-permute-start.40
  403.3 1.9 collective-permute-done.40.refs_6_.refs_10_
  405.9 1.2 collective-permute-done.38.refs_3_.refs_7_
  407.1 1.7 collective-permute-done.37.refs_2_.refs_6_
  408.8 1.7 collective-permute-done.41.refs_7_.refs_11_
  410.4 37.6 %shard_map.133.refs_4_ = f32[3072,3072]{1,0:T(8,128)} custom-call(s32[1]{0:T(128)} %bitcast.me_ref, bf16[3072,3072]{1,0:T(8,128)(2,1)} %shard_map.131.big_ref, bf16[192,3072]{1,0:T(8,128)(2,1)} %collective-permute-done.36.refs_0_.refs_4_, bf16[192,3072]{1,0:T(8,128)(2,1)} %collective-permute-done.34.refs_1_.refs_5_, ...), custom_call_target="tpu_custom_call", output_to_operand_aliasing={{}: (10, {})} | custom-call | flops 28991029248 | bytes 47185920 | tf_op jit(solution)/shard_map/pallas_call | solution.py:424
  451.6 1.2 collective-permute-done.43.refs_3_.refs_15_
  452.8 20.5 %shard_map.134 = f32[3072,3072]{1,0:T(8,128)} custom-call(s32[1]{0:T(128)} %bitcast.me_ref, bf16[3072,3072]{1,0:T(8,128)(2,1)} %shard_map.131.big_ref, bf16[192,3072]{1,0:T(8,128)(2,1)} %copy-done.11, bf16[192,3072]{1,0:T(8,128)(2,1)} %copy-done.12, bf16[192,3072]{1,0:T(8,128)(2,1)} %copy-done.13, ...), custom_call_target="tpu_custom_call", output_to_operand_aliasing={{}: (6, {})} | custom-call | flops 14495514624 | bytes 33030144 | tf_op jit(solution)/shard_map/pallas_call | solution.py:424
  473.3 11.2 %collective-permute-done.48.refs_4_.refs_20_ = bf16[128,3072]{1,0:T(8,128)(2,1)} collective-permute-done((bf16[128,3072]{1,0:T(8,128)(2,1)}, bf16[128,3072]{1,0:T(8,128)(2,1)}, u32[]{:S(2)}, u32[]{:S(2)}) %collective-permute-start.48) | collective-permute-done | bytes 786464 | tf_op jit(solution)/shard_map/ppermute | solution.py:451
  484.8 1.0 collective-permute-start.57
  485.8 1.8 collective-permute-start.52
  488.1 14.0 %shard_map.135 = bf16[384,3072]{1,0:T(8,128)(2,1)} custom-call(s32[1]{0:T(128)} %bitcast.me_ref, bf16[192,3072]{1,0:T(8,128)(2,1)} %get-tuple-element.65.refs_0_, bf16[192,3072]{1,0:T(8,128)(2,1)} %get-tuple-element.66.refs_1_, bf16[192,3072]{1,0:T(8,128)(2,1)} %copy-done.10, bf16[192,3072]{1,0:T(8,128)(2,1)} %collective-permute-done.32.refs_3_, ...), custom_call_target="tpu_custom_call" | custom-call | flops 7247757312 | bytes 21233664 | tf_op jit(solution)/shard_map/pallas_call | solution.py:342
  502.7 2.1 collective-permute-start.49
  511.6 49.7 %shard_map.136 = (f32[3072,1024]{1,0:T(8,128)}, f32[3072,1024]{1,0:T(8,128)}) custom-call(s32[1]{0:T(128)} %bitcast.me_ref, bf16[3072,3072]{1,0:T(8,128)(2,1)} %shard_map.128.big_ref, bf16[128,3072]{1,0:T(8,128)(2,1)} %get-tuple-element.52.refs_0_.refs_16_, bf16[128,3072]{1,0:T(8,128)(2,1)} %copy-done.31, ...), custom_call_target="tpu_custom_call" | custom-call | flops 38654705664 | bytes 56623104 | tf_op jit(solution)/shard_map/pallas_call | solution.py:424
  562.9 1.8 collective-permute-done.66.refs_6_.refs_10_
  565.4 0.9 collective-permute-done.64.refs_3_.refs_7_
  566.3 1.7 collective-permute-done.63.refs_2_.refs_6_
  568.0 1.0 copy-done.29
  569.0 0.8 collective-permute-done.67.refs_7_.refs_11_
  569.8 37.7 %shard_map.137.refs_4_ = f32[3072,3072]{1,0:T(8,128)} custom-call(s32[1]{0:T(128)} %bitcast.me_ref, bf16[3072,3072]{1,0:T(8,128)(2,1)} %shard_map.128.big_ref, bf16[192,3072]{1,0:T(8,128)(2,1)} %copy-done.26, bf16[192,3072]{1,0:T(8,128)(2,1)} %collective-permute-done.60.refs_1_.refs_5_, ...), custom_call_target="tpu_custom_call", output_to_operand_aliasing={{}: (10, {})} | custom-call | flops 28991029248 | bytes 47185920 | tf_op jit(solution)/shard_map/pallas_call | solution.py:424
  608.1 2.3 collective-permute-done.68.refs_2_.refs_14_
  610.5 1.8 collective-permute-done.69.refs_3_.refs_15_
  612.3 21.0 %shard_map.138 = f32[3072,3072]{1,0:T(8,128)} custom-call(s32[1]{0:T(128)} %bitcast.me_ref, bf16[3072,3072]{1,0:T(8,128)(2,1)} %shard_map.128.big_ref, bf16[192,3072]{1,0:T(8,128)(2,1)} %copy-done.14, bf16[192,3072]{1,0:T(8,128)(2,1)} %copy-done.15, bf16[192,3072]{1,0:T(8,128)(2,1)} %copy-done.16, ...), custom_call_target="tpu_custom_call", output_to_operand_aliasing={{}: (6, {})} | custom-call | flops 14495514624 | bytes 33030144 | tf_op jit(solution)/shard_map/pallas_call | solution.py:424
  633.3 21.0 %shard_map.139 = bf16[384,3072]{1,0:T(8,128)(2,1)} custom-call(s32[1]{0:T(128)} %bitcast.me_ref, bf16[192,3072]{1,0:T(8,128)(2,1)} %get-tuple-element.57.refs_0_, bf16[192,3072]{1,0:T(8,128)(2,1)} %get-tuple-element.58.refs_1_, bf16[192,3072]{1,0:T(8,128)(2,1)} %copy-done.7, bf16[192,3072]{1,0:T(8,128)(2,1)} %collective-permute-done.17.refs_3_, ...), custom_call_target="tpu_custom_call" | custom-call | flops 12079595520 | bytes 35389440 | tf_op jit(solution)/shard_map/pallas_call | solution.py:342
  (182 shorter events, 29.9 us)
Async XLA Ops:
  52.7 127.4 %all-to-all-start = ((bf16[8,384,1024]{2,1,0:T(8,128)(2,1)}), bf16[8,384,1024]{2,1,0:T(8,128)(2,1)}, u32[]{:S(2)}, u32[]{:S(2)}) async-start(bf16[8,384,1024]{2,1,0:T(8,128)(2,1)} %project.1), calls=%async_computation | async-start | bytes 12582912 | tf_op jit(solution)/shard_map/all_to_all | solution.py:507
  59.9 93.1 %collective-permute-start.13 = (bf16[384,1536]{1,0:T(8,128)(2,1)S(1)}, bf16[384,1536]{1,0:T(8,128)(2,1)S(1)}, u32[]{:S(2)}, u32[]{:S(2)}) collective-permute-start(bf16[384,1536]{1,0:T(8,128)(2,1)S(1)} %get-tuple-element.94.refs_6_), channel_id=1, source_target_pairs={{0,4},{1,5},{2,6},{3,7},{4,0},{5,1},{6,2},{7,3},{8,12},{9,13},{10,... | collective-permute-start | bytes 3538952 | tf_op jit(solution)/shard_map/ppermute | solution.py:451
  61.3 93.4 %collective-permute-start.11 = (bf16[384,1536]{1,0:T(8,128)(2,1)S(1)}, bf16[384,1536]{1,0:T(8,128)(2,1)}, u32[]{:S(2)}, u32[]{:S(2)}) collective-permute-start(bf16[384,1536]{1,0:T(8,128)(2,1)S(1)} %get-tuple-element.94.refs_6_), channel_id=1, source_target_pairs={{0,1},{1,0},{2,3},{3,2},{4,5},{5,4},{6,7},{7,6},{8,9},{9,8},{10,11... | collective-permute-start | bytes 3538952 | tf_op jit(solution)/shard_map/ppermute | solution.py:451
  62.0 92.6 %collective-permute-start.4 = (bf16[384,1536]{1,0:T(8,128)(2,1)S(1)}, bf16[384,1536]{1,0:T(8,128)(2,1)}, u32[]{:S(2)}, u32[]{:S(2)}) collective-permute-start(bf16[384,1536]{1,0:T(8,128)(2,1)S(1)} %get-tuple-element.94.refs_6_), channel_id=1, source_target_pairs={{0,2},{1,3},{2,0},{3,1},{4,6},{5,7},{6,4},{7,5},{8,10},{9,11},{10,... | collective-permute-start | bytes 3538952 | tf_op jit(solution)/shard_map/ppermute | solution.py:451
  63.2 115.3 %collective-permute-start.8 = (bf16[384,1536]{1,0:T(8,128)(2,1)S(1)}, bf16[384,1536]{1,0:T(8,128)(2,1)}, u32[]{:S(2)}, u32[]{:S(2)}) collective-permute-start(bf16[384,1536]{1,0:T(8,128)(2,1)S(1)} %get-tuple-element.95.refs_0_), channel_id=1, source_target_pairs={{0,2},{1,3},{2,0},{3,1},{4,6},{5,7},{6,4},{7,5},{8,10},{9,11},{10,... | collective-permute-start | bytes 3538952 | tf_op jit(solution)/shard_map/ppermute | solution.py:451
  63.4 116.0 %collective-permute-start.1 = (bf16[384,1536]{1,0:T(8,128)(2,1)S(1)}, bf16[384,1536]{1,0:T(8,128)(2,1)}, u32[]{:S(2)}, u32[]{:S(2)}) collective-permute-start(bf16[384,1536]{1,0:T(8,128)(2,1)S(1)} %get-tuple-element.95.refs_0_), channel_id=1, source_target_pairs={{0,4},{1,5},{2,6},{3,7},{4,0},{5,1},{6,2},{7,3},{8,12},{9,13},{10,... | collective-permute-start | bytes 3538952 | tf_op jit(solution)/shard_map/ppermute | solution.py:451
  153.0 95.5 %collective-permute-start.7 = (bf16[384,1536]{1,0:T(8,128)(2,1)S(1)}, bf16[384,1536]{1,0:T(8,128)(2,1)}, u32[]{:S(2)}, u32[]{:S(2)}) collective-permute-start(bf16[384,1536]{1,0:T(8,128)(2,1)S(1)} %get-tuple-element.95.refs_0_), channel_id=1, source_target_pairs={{0,1},{1,0},{2,3},{3,2},{4,5},{5,4},{6,7},{7,6},{8,9},{9,8},{10,11... | collective-permute-start | bytes 3538952 | tf_op jit(solution)/shard_map/ppermute | solution.py:451
  154.5 94.8 %collective-permute-start.12 = (bf16[384,1536]{1,0:T(8,128)(2,1)}, bf16[384,1536]{1,0:T(8,128)(2,1)}, u32[]{:S(2)}, u32[]{:S(2)}) collective-permute-start(bf16[384,1536]{1,0:T(8,128)(2,1)} %collective-permute-done.4.refs_8_), channel_id=1, source_target_pairs={{0,1},{1,0},{2,3},{3,2},{4,5},{5,4},{6,7},{7,6},{8,9},{9,8},{10,11... | collective-permute-start | bytes 3538952 | tf_op jit(solution)/shard_map/ppermute | solution.py:451
  154.7 94.0 %collective-permute-start.5 = (bf16[384,1536]{1,0:T(8,128)(2,1)}, bf16[384,1536]{1,0:T(8,128)(2,1)}, u32[]{:S(2)}, u32[]{:S(2)}) collective-permute-start(bf16[384,1536]{1,0:T(8,128)(2,1)} %collective-permute-done.4.refs_8_), channel_id=1, source_target_pairs={{0,4},{1,5},{2,6},{3,7},{4,0},{5,1},{6,2},{7,3},{8,12},{9,13},{10,... | collective-permute-start | bytes 3538952 | tf_op jit(solution)/shard_map/ppermute | solution.py:451
  178.4 70.6 %collective-permute-start.14 = (bf16[384,1536]{1,0:T(8,128)(2,1)S(1)}, bf16[384,1536]{1,0:T(8,128)(2,1)}, u32[]{:S(2)}, u32[]{:S(2)}) collective-permute-start(bf16[384,1536]{1,0:T(8,128)(2,1)S(1)} %collective-permute-done.13.refs_10_), channel_id=1, source_target_pairs={{0,1},{1,0},{2,3},{3,2},{4,5},{5,4},{6,7},{7,6},{8,9},{9,8},{10,11... | collective-permute-start | bytes 3538952 | tf_op jit(solution)/shard_map/ppermute | solution.py:451
  179.4 68.4 %collective-permute-start.2 = (bf16[384,1536]{1,0:T(8,128)(2,1)}, bf16[384,1536]{1,0:T(8,128)(2,1)}, u32[]{:S(2)}, u32[]{:S(2)}) collective-permute-start(bf16[384,1536]{1,0:T(8,128)(2,1)} %collective-permute-done.1.refs_4_), channel_id=1, source_target_pairs={{0,2},{1,3},{2,0},{3,1},{4,6},{5,7},{6,4},{7,5},{8,10},{9,11},{10,... | collective-permute-start | bytes 3538952 | tf_op jit(solution)/shard_map/ppermute | solution.py:451
  248.6 4.4 collective-permute-start.10
  248.6 6.0 collective-permute-start.3
  249.1 21.7 %collective-permute-start.6 = (bf16[384,1536]{1,0:T(8,128)(2,1)}, bf16[384,1536]{1,0:T(8,128)(2,1)}, u32[]{:S(2)}, u32[]{:S(2)}) collective-permute-start(bf16[384,1536]{1,0:T(8,128)(2,1)} %collective-permute-done.5.refs_2_), channel_id=1, source_target_pairs={{0,1},{1,0},{2,3},{3,2},{4,5},{5,4},{6,7},{7,6},{8,9},{9,8},{10,11... | collective-permute-start | bytes 3538952 | tf_op jit(solution)/shard_map/ppermute | solution.py:451
  249.4 29.1 %collective-permute-start = (bf16[384,1536]{1,0:T(8,128)(2,1)S(1)}, bf16[384,1536]{1,0:T(8,128)(2,1)}, u32[]{:S(2)}, u32[]{:S(2)}) collective-permute-start(bf16[384,1536]{1,0:T(8,128)(2,1)S(1)} %get-tuple-element.93.refs_0_), channel_id=1, source_target_pairs={{0,4},{1,5},{2,6},{3,7},{4,0},{5,1},{6,2},{7,3},{8,12},{9,13},{10,... | collective-permute-start | bytes 3538952 | tf_op jit(solution)/shard_map/ppermute | solution.py:451
  251.3 50.6 %collective-permute-start.25 = (bf16[384,1536]{1,0:T(8,128)(2,1)S(1)}, bf16[384,1536]{1,0:T(8,128)(2,1)}, u32[]{:S(2)}, u32[]{:S(2)}) collective-permute-start(bf16[384,1536]{1,0:T(8,128)(2,1)S(1)} %get-tuple-element.92.refs_6_), channel_id=1, source_target_pairs={{0,4},{1,5},{2,6},{3,7},{4,0},{5,1},{6,2},{7,3},{8,12},{9,13},{10,... | collective-permute-start | bytes 3538952 | tf_op jit(solution)/shard_map/ppermute | solution.py:451
  252.9 50.2 %collective-permute-start.23 = (bf16[384,1536]{1,0:T(8,128)(2,1)S(1)}, bf16[384,1536]{1,0:T(8,128)(2,1)}, u32[]{:S(2)}, u32[]{:S(2)}) collective-permute-start(bf16[384,1536]{1,0:T(8,128)(2,1)S(1)} %get-tuple-element.92.refs_6_), channel_id=1, source_target_pairs={{0,2},{1,3},{2,0},{3,1},{4,6},{5,7},{6,4},{7,5},{8,10},{9,11},{10,... | collective-permute-start | bytes 3538952 | tf_op jit(solution)/shard_map/ppermute | solution.py:451
  255.6 49.8 %collective-permute-start.19 = (bf16[384,1536]{1,0:T(8,128)(2,1)S(1)}, bf16[384,1536]{1,0:T(8,128)(2,1)}, u32[]{:S(2)}, u32[]{:S(2)}) collective-permute-start(bf16[384,1536]{1,0:T(8,128)(2,1)S(1)} %get-tuple-element.93.refs_0_), channel_id=1, source_target_pairs={{0,2},{1,3},{2,0},{3,1},{4,6},{5,7},{6,4},{7,5},{8,10},{9,11},{10,... | collective-permute-start | bytes 3538952 | tf_op jit(solution)/shard_map/ppermute | solution.py:451
  270.8 35.9 %collective-permute-start.22 = (bf16[384,1536]{1,0:T(8,128)(2,1)S(1)}, bf16[384,1536]{1,0:T(8,128)(2,1)}, u32[]{:S(2)}, u32[]{:S(2)}) collective-permute-start(bf16[384,1536]{1,0:T(8,128)(2,1)S(1)} %get-tuple-element.92.refs_6_), channel_id=1, source_target_pairs={{0,1},{1,0},{2,3},{3,2},{4,5},{5,4},{6,7},{7,6},{8,9},{9,8},{10,11... | collective-permute-start | bytes 3538952 | tf_op jit(solution)/shard_map/ppermute | solution.py:451
  278.4 29.2 %collective-permute-start.18 = (bf16[384,1536]{1,0:T(8,128)(2,1)S(1)}, bf16[384,1536]{1,0:T(8,128)(2,1)S(1)}, u32[]{:S(2)}, u32[]{:S(2)}) collective-permute-start(bf16[384,1536]{1,0:T(8,128)(2,1)S(1)} %get-tuple-element.93.refs_0_), channel_id=1, source_target_pairs={{0,1},{1,0},{2,3},{3,2},{4,5},{5,4},{6,7},{7,6},{8,9},{9,8},{10,11... | collective-permute-start | bytes 3538952 | tf_op jit(solution)/shard_map/ppermute | solution.py:451
  301.9 6.5 collective-permute-start.16
  303.2 6.9 %collective-permute-start.17 = (bf16[192,3072]{1,0:T(8,128)(2,1)}, bf16[192,3072]{1,0:T(8,128)(2,1)}, u32[]{:S(2)}, u32[]{:S(2)}) collective-permute-start(bf16[192,3072]{1,0:T(8,128)(2,1)} %get-tuple-element.58.refs_1_), channel_id=1, source_target_pairs={{0,1},{1,0},{2,3},{3,2},{4,5},{5,4},{6,7},{7,6},{8,9},{9,8},{10,11... | collective-permute-start | bytes 3538952 | tf_op jit(solution)/shard_map/ppermute | solution.py:451
  305.5 4.6 collective-permute-start.21
  306.7 38.9 %collective-permute-start.15 = (bf16[384,1536]{1,0:T(8,128)(2,1)}, bf16[384,1536]{1,0:T(8,128)(2,1)}, u32[]{:S(2)}, u32[]{:S(2)}) collective-permute-start(bf16[384,1536]{1,0:T(8,128)(2,1)} %collective-permute-done.refs_4_), channel_id=1, source_target_pairs={{0,2},{1,3},{2,0},{3,1},{4,6},{5,7},{6,4},{7,5},{8,10},{9,11},{10,... | collective-permute-start | bytes 3538952 | tf_op jit(solution)/shard_map/ppermute | solution.py:451
  307.6 38.0 %collective-permute-start.28 = (bf16[384,1536]{1,0:T(8,128)(2,1)}, bf16[384,1536]{1,0:T(8,128)(2,1)}, u32[]{:S(2)}, u32[]{:S(2)}) collective-permute-start(bf16[384,1536]{1,0:T(8,128)(2,1)} %collective-permute-done.23.refs_8_), channel_id=1, source_target_pairs={{0,4},{1,5},{2,6},{3,7},{4,0},{5,1},{6,2},{7,3},{8,12},{9,13},{10,... | collective-permute-start | bytes 3538952 | tf_op jit(solution)/shard_map/ppermute | solution.py:451
  309.5 21.8 %collective-permute-start.24 = (bf16[384,1536]{1,0:T(8,128)(2,1)}, bf16[384,1536]{1,0:T(8,128)(2,1)S(1)}, u32[]{:S(2)}, u32[]{:S(2)}) collective-permute-start(bf16[384,1536]{1,0:T(8,128)(2,1)} %collective-permute-done.23.refs_8_), channel_id=1, source_target_pairs={{0,1},{1,0},{2,3},{3,2},{4,5},{5,4},{6,7},{7,6},{8,9},{9,8},{10,11... | collective-permute-start | bytes 3538952 | tf_op jit(solution)/shard_map/ppermute | solution.py:451
  310.1 21.2 %collective-permute-start.20 = (bf16[384,1536]{1,0:T(8,128)(2,1)}, bf16[384,1536]{1,0:T(8,128)(2,1)}, u32[]{:S(2)}, u32[]{:S(2)}) collective-permute-start(bf16[384,1536]{1,0:T(8,128)(2,1)} %collective-permute-done.19.refs_2_), channel_id=1, source_target_pairs={{0,1},{1,0},{2,3},{3,2},{4,5},{5,4},{6,7},{7,6},{8,9},{9,8},{10,11... | collective-permute-start | bytes 3538952 | tf_op jit(solution)/shard_map/ppermute | solution.py:451
  310.1 21.2 %collective-permute-start.26 = (bf16[384,1536]{1,0:T(8,128)(2,1)}, bf16[384,1536]{1,0:T(8,128)(2,1)}, u32[]{:S(2)}, u32[]{:S(2)}) collective-permute-start(bf16[384,1536]{1,0:T(8,128)(2,1)} %collective-permute-done.25.refs_10_), channel_id=1, source_target_pairs={{0,1},{1,0},{2,3},{3,2},{4,5},{5,4},{6,7},{7,6},{8,9},{9,8},{10,11... | collective-permute-start | bytes 3538952 | tf_op jit(solution)/shard_map/ppermute | solution.py:451
  345.7 4.7 collective-permute-start.29
  346.2 12.3 %collective-permute-start.31 = (bf16[192,3072]{1,0:T(8,128)(2,1)S(1)}, bf16[192,3072]{1,0:T(8,128)(2,1)S(1)}, u32[]{:S(2)}, u32[]{:S(2)}) collective-permute-start(bf16[192,3072]{1,0:T(8,128)(2,1)S(1)} %copy-done.8), channel_id=1, source_target_pairs={{0,1},{1,0},{2,3},{3,2},{4,5},{5,4},{6,7},{7,6},{8,9},{9,8},{10,11... | collective-permute-start | bytes 3538952 | tf_op jit(solution)/shard_map/ppermute | solution.py:451
  346.2 12.9 %collective-permute-start.32 = (bf16[192,3072]{1,0:T(8,128)(2,1)S(1)}, bf16[192,3072]{1,0:T(8,128)(2,1)}, u32[]{:S(2)}, u32[]{:S(2)}) collective-permute-start(bf16[192,3072]{1,0:T(8,128)(2,1)S(1)} %copy-done.9), channel_id=1, source_target_pairs={{0,1},{1,0},{2,3},{3,2},{4,5},{5,4},{6,7},{7,6},{8,9},{9,8},{10,11... | collective-permute-start | bytes 3538952 | tf_op jit(solution)/shard_map/ppermute | solution.py:451
  346.7 54.8 %collective-permute-start.36 = (bf16[192,3072]{1,0:T(8,128)(2,1)S(1)}, bf16[192,3072]{1,0:T(8,128)(2,1)}, u32[]{:S(2)}, u32[]{:S(2)}) collective-permute-start(bf16[192,3072]{1,0:T(8,128)(2,1)S(1)} %copy-done.8), channel_id=1, source_target_pairs={{0,2},{1,3},{2,0},{3,1},{4,6},{5,7},{6,4},{7,5},{8,10},{9,11},{10,... | collective-permute-start | bytes 3538952 | tf_op jit(solution)/shard_map/ppermute | solution.py:451
  348.7 52.8 %collective-permute-start.30 = (bf16[192,3072]{1,0:T(8,128)(2,1)S(1)}, bf16[192,3072]{1,0:T(8,128)(2,1)}, u32[]{:S(2)}, u32[]{:S(2)}) collective-permute-start(bf16[192,3072]{1,0:T(8,128)(2,1)S(1)} %copy-done.8), channel_id=1, source_target_pairs={{0,4},{1,5},{2,6},{3,7},{4,0},{5,1},{6,2},{7,3},{8,12},{9,13},{10,... | collective-permute-start | bytes 3538952 | tf_op jit(solution)/shard_map/ppermute | solution.py:451
  351.4 50.1 %collective-permute-start.39 = (bf16[192,3072]{1,0:T(8,128)(2,1)S(1)}, bf16[192,3072]{1,0:T(8,128)(2,1)}, u32[]{:S(2)}, u32[]{:S(2)}) collective-permute-start(bf16[192,3072]{1,0:T(8,128)(2,1)S(1)} %copy-done.9), channel_id=1, source_target_pairs={{0,4},{1,5},{2,6},{3,7},{4,0},{5,1},{6,2},{7,3},{8,12},{9,13},{10,... | collective-permute-start | bytes 3538952 | tf_op jit(solution)/shard_map/ppermute | solution.py:451
  358.5 43.0 %collective-permute-start.34 = (bf16[192,3072]{1,0:T(8,128)(2,1)S(1)}, bf16[192,3072]{1,0:T(8,128)(2,1)}, u32[]{:S(2)}, u32[]{:S(2)}) collective-permute-start(bf16[192,3072]{1,0:T(8,128)(2,1)S(1)} %copy-done.9), channel_id=1, source_target_pairs={{0,2},{1,3},{2,0},{3,1},{4,6},{5,7},{6,4},{7,5},{8,10},{9,11},{10,... | collective-permute-start | bytes 3538952 | tf_op jit(solution)/shard_map/ppermute | solution.py:451
  402.6 4.5 collective-permute-start.38
  402.6 6.1 collective-permute-start.37
  403.1 7.4 %collective-permute-start.41 = (bf16[192,3072]{1,0:T(8,128)(2,1)}, bf16[192,3072]{1,0:T(8,128)(2,1)}, u32[]{:S(2)}, u32[]{:S(2)}) collective-permute-start(bf16[192,3072]{1,0:T(8,128)(2,1)} %collective-permute-done.39.refs_5_.refs_9_), channel_id=1, source_target_pairs={{0,1},{1,0},{2,3},{3,2},{4,5},{5,4},{6,7},{7,6},{8,9},{9,8},{10,11... | collective-permute-start | bytes 3538952 | tf_op jit(solution)/shard_map/ppermute | solution.py:451
  403.1 45.0 %collective-permute-start.33 = (bf16[192,3072]{1,0:T(8,128)(2,1)}, bf16[192,3072]{1,0:T(8,128)(2,1)S(1)}, u32[]{:S(2)}, u32[]{:S(2)}) collective-permute-start(bf16[192,3072]{1,0:T(8,128)(2,1)} %collective-permute-done.30.refs_4_.refs_8_), channel_id=1, source_target_pairs={{0,2},{1,3},{2,0},{3,1},{4,6},{5,7},{6,4},{7,5},{8,10},{9,11},{10,... | collective-permute-start | bytes 3538952 | tf_op jit(solution)/shard_map/ppermute | solution.py:451
  405.2 42.8 %collective-permute-start.35 = (bf16[192,3072]{1,0:T(8,128)(2,1)}, bf16[192,3072]{1,0:T(8,128)(2,1)S(1)}, u32[]{:S(2)}, u32[]{:S(2)}) collective-permute-start(bf16[192,3072]{1,0:T(8,128)(2,1)} %collective-permute-done.34.refs_1_.refs_5_), channel_id=1, source_target_pairs={{0,4},{1,5},{2,6},{3,7},{4,0},{5,1},{6,2},{7,3},{8,12},{9,13},{10,... | collective-permute-start | bytes 3538952 | tf_op jit(solution)/shard_map/ppermute | solution.py:451
  448.5 4.3 collective-permute-start.43
  448.7 39.0 %collective-permute-start.55 = (bf16[128,3072]{1,0:T(8,128)(2,1)}, bf16[128,3072]{1,0:T(8,128)(2,1)}, u32[]{:S(2)}, u32[]{:S(2)}) collective-permute-start(bf16[128,3072]{1,0:T(8,128)(2,1)} %get-tuple-element.78.refs_8_.refs_24_), channel_id=1, source_target_pairs={{0,4},{1,5},{2,6},{3,7},{4,0},{5,1},{6,2},{7,3},{8,12},{9,13},{10,... | collective-permute-start | bytes 2359304 | tf_op jit(solution)/shard_map/ppermute | solution.py:451
  449.3 35.5 %collective-permute-start.53 = (bf16[128,3072]{1,0:T(8,128)(2,1)}, bf16[128,3072]{1,0:T(8,128)(2,1)}, u32[]{:S(2)}, u32[]{:S(2)}) collective-permute-start(bf16[128,3072]{1,0:T(8,128)(2,1)} %get-tuple-element.78.refs_8_.refs_24_), channel_id=1, source_target_pairs={{0,2},{1,3},{2,0},{3,1},{4,6},{5,7},{6,4},{7,5},{8,10},{9,11},{10,... | collective-permute-start | bytes 2359304 | tf_op jit(solution)/shard_map/ppermute | solution.py:451
  449.9 34.6 %collective-permute-start.48 = (bf16[128,3072]{1,0:T(8,128)(2,1)}, bf16[128,3072]{1,0:T(8,128)(2,1)}, u32[]{:S(2)}, u32[]{:S(2)}) collective-permute-start(bf16[128,3072]{1,0:T(8,128)(2,1)} %get-tuple-element.52.refs_0_.refs_16_), channel_id=1, source_target_pairs={{0,4},{1,5},{2,6},{3,7},{4,0},{5,1},{6,2},{7,3},{8,12},{9,13},{10,... | collective-permute-start | bytes 2359304 | tf_op jit(solution)/shard_map/ppermute | solution.py:451
  451.0 36.6 %collective-permute-start.46 = (bf16[128,3072]{1,0:T(8,128)(2,1)}, bf16[128,3072]{1,0:T(8,128)(2,1)}, u32[]{:S(2)}, u32[]{:S(2)}) collective-permute-start(bf16[128,3072]{1,0:T(8,128)(2,1)} %get-tuple-element.52.refs_0_.refs_16_), channel_id=1, source_target_pairs={{0,2},{1,3},{2,0},{3,1},{4,6},{5,7},{6,4},{7,5},{8,10},{9,11},{10,... | collective-permute-start | bytes 2359304 | tf_op jit(solution)/shard_map/ppermute | solution.py:451
  484.5 18.2 %collective-permute-start.50 = (bf16[128,3072]{1,0:T(8,128)(2,1)}, bf16[128,3072]{1,0:T(8,128)(2,1)}, u32[]{:S(2)}, u32[]{:S(2)}) collective-permute-start(bf16[128,3072]{1,0:T(8,128)(2,1)} %collective-permute-done.48.refs_4_.refs_20_), channel_id=1, source_target_pairs={{0,2},{1,3},{2,0},{3,1},{4,6},{5,7},{6,4},{7,5},{8,10},{9,11},{10,... | collective-permute-start | bytes 2359304 | tf_op jit(solution)/shard_map/ppermute | solution.py:451
  484.8 20.1 %collective-permute-start.57 = (bf16[128,3072]{1,0:T(8,128)(2,1)}, bf16[128,3072]{1,0:T(8,128)(2,1)}, u32[]{:S(2)}, u32[]{:S(2)}) collective-permute-start(bf16[128,3072]{1,0:T(8,128)(2,1)} %collective-permute-done.53.refs_10_.refs_26_), channel_id=1, source_target_pairs={{0,4},{1,5},{2,6},{3,7},{4,0},{5,1},{6,2},{7,3},{8,12},{9,13},{10,... | collective-permute-start | bytes 2359304 | tf_op jit(solution)/shard_map/ppermute | solution.py:451
  485.8 19.2 %collective-permute-start.52 = (bf16[128,3072]{1,0:T(8,128)(2,1)}, bf16[128,3072]{1,0:T(8,128)(2,1)S(1)}, u32[]{:S(2)}, u32[]{:S(2)}) collective-permute-start(bf16[128,3072]{1,0:T(8,128)(2,1)} %get-tuple-element.78.refs_8_.refs_24_), channel_id=1, source_target_pairs={{0,1},{1,0},{2,3},{3,2},{4,5},{5,4},{6,7},{7,6},{8,9},{9,8},{10,11... | collective-permute-start | bytes 2359304 | tf_op jit(solution)/shard_map/ppermute | solution.py:451
  487.6 17.7 %collective-permute-start.45 = (bf16[128,3072]{1,0:T(8,128)(2,1)}, bf16[128,3072]{1,0:T(8,128)(2,1)S(1)}, u32[]{:S(2)}, u32[]{:S(2)}) collective-permute-start(bf16[128,3072]{1,0:T(8,128)(2,1)} %get-tuple-element.52.refs_0_.refs_16_), channel_id=1, source_target_pairs={{0,1},{1,0},{2,3},{3,2},{4,5},{5,4},{6,7},{7,6},{8,9},{9,8},{10,11... | collective-permute-start | bytes 2359304 | tf_op jit(solution)/shard_map/ppermute | solution.py:451
  487.6 18.0 %collective-permute-start.47 = (bf16[128,3072]{1,0:T(8,128)(2,1)}, bf16[128,3072]{1,0:T(8,128)(2,1)}, u32[]{:S(2)}, u32[]{:S(2)}) collective-permute-start(bf16[128,3072]{1,0:T(8,128)(2,1)} %collective-permute-done.46.refs_2_.refs_18_), channel_id=1, source_target_pairs={{0,1},{1,0},{2,3},{3,2},{4,5},{5,4},{6,7},{7,6},{8,9},{9,8},{10,11... | collective-permute-start | bytes 2359304 | tf_op jit(solution)/shard_map/ppermute | solution.py:451
  502.7 4.2 collective-permute-start.49
  505.0 4.1 collective-permute-start.56
  505.3 5.0 collective-permute-start.51
  505.6 6.0 collective-permute-start.58
  507.0 54.4 %collective-permute-start.62 = (bf16[192,3072]{1,0:T(8,128)(2,1)S(1)}, bf16[192,3072]{1,0:T(8,128)(2,1)S(1)}, u32[]{:S(2)}, u32[]{:S(2)}) collective-permute-start(bf16[192,3072]{1,0:T(8,128)(2,1)S(1)} %copy-done.5), channel_id=1, source_target_pairs={{0,2},{1,3},{2,0},{3,1},{4,6},{5,7},{6,4},{7,5},{8,10},{9,11},{10,... | collective-permute-start | bytes 3538952 | tf_op jit(solution)/shard_map/ppermute | solution.py:451
  508.1 53.3 %collective-permute-start.44 = (bf16[192,3072]{1,0:T(8,128)(2,1)S(1)}, bf16[192,3072]{1,0:T(8,128)(2,1)}, u32[]{:S(2)}, u32[]{:S(2)}) collective-permute-start(bf16[192,3072]{1,0:T(8,128)(2,1)S(1)} %copy-done.5), channel_id=1, source_target_pairs={{0,4},{1,5},{2,6},{3,7},{4,0},{5,1},{6,2},{7,3},{8,12},{9,13},{10,... | collective-permute-start | bytes 3538952 | tf_op jit(solution)/shard_map/ppermute | solution.py:451
  509.2 52.1 %collective-permute-start.65 = (bf16[192,3072]{1,0:T(8,128)(2,1)S(1)}, bf16[192,3072]{1,0:T(8,128)(2,1)}, u32[]{:S(2)}, u32[]{:S(2)}) collective-permute-start(bf16[192,3072]{1,0:T(8,128)(2,1)S(1)} %copy-done.6), channel_id=1, source_target_pairs={{0,4},{1,5},{2,6},{3,7},{4,0},{5,1},{6,2},{7,3},{8,12},{9,13},{10,... | collective-permute-start | bytes 3538952 | tf_op jit(solution)/shard_map/ppermute | solution.py:451
  510.3 51.0 %collective-permute-start.60 = (bf16[192,3072]{1,0:T(8,128)(2,1)S(1)}, bf16[192,3072]{1,0:T(8,128)(2,1)}, u32[]{:S(2)}, u32[]{:S(2)}) collective-permute-start(bf16[192,3072]{1,0:T(8,128)(2,1)S(1)} %copy-done.6), channel_id=1, source_target_pairs={{0,2},{1,3},{2,0},{3,1},{4,6},{5,7},{6,4},{7,5},{8,10},{9,11},{10,... | collective-permute-start | bytes 3538952 | tf_op jit(solution)/shard_map/ppermute | solution.py:451
  561.9 4.4 collective-permute-start.64
  561.9 6.0 collective-permute-start.63
  562.4 7.4 %collective-permute-start.67 = (bf16[192,3072]{1,0:T(8,128)(2,1)}, bf16[192,3072]{1,0:T(8,128)(2,1)}, u32[]{:S(2)}, u32[]{:S(2)}) collective-permute-start(bf16[192,3072]{1,0:T(8,128)(2,1)} %collective-permute-done.65.refs_5_.refs_9_), channel_id=1, source_target_pairs={{0,1},{1,0},{2,3},{3,2},{4,5},{5,4},{6,7},{7,6},{8,9},{9,8},{10,11... | collective-permute-start | bytes 3538952 | tf_op jit(solution)/shard_map/ppermute | solution.py:451
  562.5 45.1 %collective-permute-start.59 = (bf16[192,3072]{1,0:T(8,128)(2,1)}, bf16[192,3072]{1,0:T(8,128)(2,1)S(1)}, u32[]{:S(2)}, u32[]{:S(2)}) collective-permute-start(bf16[192,3072]{1,0:T(8,128)(2,1)} %collective-permute-done.44.refs_4_.refs_8_), channel_id=1, source_target_pairs={{0,2},{1,3},{2,0},{3,1},{4,6},{5,7},{6,4},{7,5},{8,10},{9,11},{10,... | collective-permute-start | bytes 3538952 | tf_op jit(solution)/shard_map/ppermute | solution.py:451
  564.7 42.8 %collective-permute-start.61 = (bf16[192,3072]{1,0:T(8,128)(2,1)}, bf16[192,3072]{1,0:T(8,128)(2,1)S(1)}, u32[]{:S(2)}, u32[]{:S(2)}) collective-permute-start(bf16[192,3072]{1,0:T(8,128)(2,1)} %collective-permute-done.60.refs_1_.refs_5_), channel_id=1, source_target_pairs={{0,4},{1,5},{2,6},{3,7},{4,0},{5,1},{6,2},{7,3},{8,12},{9,13},{10,... | collective-permute-start | bytes 3538952 | tf_op jit(solution)/shard_map/ppermute | solution.py:451
  608.0 4.3 collective-permute-start.69
  (44 other events, 812.8 us)

commit v4 on v3

--- a/solution.py
+++ b/solution.py
@@ -354,91 +354,141 @@
     )(me, *flat, *weights)
 
 
-def wgrad_kernel(by_rows, rels, n_out, me_ref, big_ref, *refs):
-    n_in = len(refs) - 3 - n_out
-    in_refs, out_refs = refs[:n_in - n_out], refs[n_in:n_in + n_out]
-    cat, acc, sems = refs[-3:]
+def wgrad_kernel(by_rows, spots, unit, n_out, n_big, half_steps, me_ref, *refs):
+    n_part = len(spots)
+    parts, bigs = refs[:n_part], refs[n_part:n_part + n_big]
+    first_scratch = len(refs) - (4 if n_big == 1 else 6)
+    scratch, out_refs = refs[first_scratch:], refs[first_scratch - n_out:first_scratch]
+    cat, acc, part_sems, out_sems = scratch[:4]
     step, n_steps = pl.program_id(0), pl.num_programs(0)
     slot = lax.rem(step, 2)
-    blk = 512
-    unit = cat.shape[0] // (len(rels) * n_out)
-
-    def copies(at_step, at_slot):
+    blk = acc.shape[1] if not by_rows else acc.shape[2]
+
+    def out_copies(at_step, at_slot):
         out = []
         wide = pl.ds(pl.multiple_of(at_step * blk, blk), blk)
-        for o in range(n_out):
-            for j, rel in enumerate(rels):
-                part = pl.ds((o * len(rels) + j) * unit, unit)
-                place = pl.ds(pl.multiple_of((me_ref[0] ^ rel) * unit, unit), unit)
-                if by_rows:
-                    src, dst = acc.at[at_slot, part, :], out_refs[o].at[place, wide]
-                else:
-                    src, dst = acc.at[at_slot, :, part], out_refs[o].at[wide, place]
-                out.append(pltpu.make_async_copy(src, dst, sems.at[at_slot, o * len(rels) + j]))
+        row = 0
+        for j, ((o, rel, off), part) in enumerate(zip(spots, parts)):
+            height = part.shape[0]
+            base = (me_ref[0] ^ rel) * unit
+            if by_rows:
+                place = pl.ds(pl.multiple_of(base + off, HALF), height)
+                out.append(pltpu.make_async_copy(acc.at[at_slot, row:row + height, :], out_refs[o].at[place, wide], out_sems.at[at_slot, j]))
+            elif off == 0:
+                place = pl.ds(pl.multiple_of(base, HEAD_DIM), unit)
+                out.append(pltpu.make_async_copy(acc.at[at_slot, :, row:row + unit], out_refs[o].at[wide, place], out_sems.at[at_slot, j]))
+            row += height
         return out
 
+    def part_copies():
+        row, out = 0, []
+        for j, part in enumerate(parts):
+            out.append(pltpu.make_async_copy(part, cat.at[row:row + part.shape[0], :], part_sems.at[j]))
+            row += part.shape[0]
+        return out
+
     @pl.when(step == 0)
     def _():
-        row = 0
-        for ref in in_refs:
-            cat[row:row + ref.shape[0], :] = ref[...]
-            row += ref.shape[0]
+        for copy in part_copies():
+            copy.start()
+
+    if n_big > 1:
+        big_scr, big_sems = scratch[4:]
+        n_dev = n_big // 2
+        tokens = bigs[0].shape[0]
+
+        def big_copies(ins, at_step, at_slot):
+            wide = pl.ds(pl.multiple_of(lax.rem(at_step, half_steps) * blk, blk), blk)
+            out = []
+            for rel, ref in enumerate(ins):
+                place = pl.ds(pl.multiple_of((me_ref[0] ^ rel) * tokens, tokens), tokens)
+                out.append(pltpu.make_async_copy(ref.at[:, wide], big_scr.at[at_slot, place, :], big_sems.at[at_slot, rel]))
+            return out
+
+        def fetch(at_step, at_slot):
+            @pl.when(at_step < half_steps)
+            def _():
+                for copy in big_copies(bigs[:n_dev], at_step, at_slot):
+                    copy.start()
+
+            @pl.when(at_step >= half_steps)
+            def _():
+                for copy in big_copies(bigs[n_dev:], at_step, at_slot):
+                    copy.start()
+
+        @pl.when(step == 0)
+        def _():
+            fetch(step, slot)
+
+        @pl.when(step + 1 < n_steps)
+        def _():
+            fetch(step + 1, 1 - slot)
+
+    @pl.when(step == 0)
+    def _():
+        for copy in part_copies():
+            copy.wait()
+
+    if n_big > 1:
+        for copy in big_copies(bigs[:n_dev], step, slot):
+            copy.wait()
+        big = big_scr[slot]
+    else:
+        big = bigs[0][...]
 
     @pl.when(step >= 2)
     def _():
-        for copy in copies(step - 2, slot):
+        for copy in out_copies(step - 2, slot):
             copy.wait()
 
-    if by_rows:
-        acc[slot] = dot_nn(cat[...], big_ref[...])
-    else:
-        acc[slot] = dot_nt(big_ref[...], cat[...])
-    for copy in copies(step, slot):
+    acc[slot] = dot_nn(cat[...], big) if by_rows else dot_nt(big, cat[...])
+    for copy in out_copies(step, slot):
         copy.start()
 
     @pl.when(step == n_steps - 1)
     def _():
-        for copy in copies(step - 1, 1 - slot):
+        for copy in out_copies(step - 1, 1 - slot):
             copy.wait()
-        for copy in copies(step, slot):
+        for copy in out_copies(step, slot):
             copy.wait()
 
 
-def weight_grad(big, parts, rels, me, prev, by_rows, n_out, n_dev):
-    seq = big.shape[0] if by_rows else big.shape[1]
-    width = big.shape[1] if by_rows else big.shape[0]
+def weight_grad(bigs, parts, spots, unit, me, prev, by_rows, n_out, n_dev):
+    n_big = len(bigs)
+    seq = parts[0].shape[1]
     rows = sum(part.shape[0] for part in parts)
-    unit = rows // (len(rels) * n_out)
+    blk = 512
+    any_spec = pl.BlockSpec(memory_space=pl.ANY)
+    width = bigs[0].shape[0] if n_big == 1 else 2 * bigs[0].shape[1]
     cols = unit * n_dev
-    blk = 512
     shape = (cols, width) if by_rows else (width, cols)
-    big_spec = pl.BlockSpec((seq, blk), lambda i, me: (0, i)) if by_rows else pl.BlockSpec((blk, seq), lambda i, me: (i, 0))
-    acc_shape = (2, rows, blk) if by_rows else (2, blk, rows)
+    big_specs = [pl.BlockSpec((blk, seq), lambda i, me: (i, 0))] if n_big == 1 else [any_spec] * n_big
     prev = [] if prev is None else list(prev)
-    any_spec = pl.BlockSpec(memory_space=pl.ANY)
-    n_fixed = 2 + len(parts)
-    body = functools.partial(wgrad_kernel, by_rows, rels, n_out)
-    if not prev:
-        inner = body
-        body = lambda me_ref, big_ref, *refs: inner(me_ref, big_ref, *refs[:len(parts)], *([None] * n_out), *refs[len(parts):])
+    scratch = [
+        pltpu.VMEM((rows, seq), BF16),
+        pltpu.VMEM((2, rows, blk) if by_rows else (2, blk, rows), F32),
+        pltpu.SemaphoreType.DMA((len(parts),)),
+        pltpu.SemaphoreType.DMA((2, len(parts))),
+    ]
+    if n_big > 1:
+        scratch += [pltpu.VMEM((2, seq, blk), BF16), pltpu.SemaphoreType.DMA((2, n_dev))]
+    body = functools.partial(wgrad_kernel, by_rows, spots, unit, n_out, n_big, width // blk // 2)
+    n_lead = 1 + len(parts) + n_big
+
     return pl.pallas_call(
         body,
         grid_spec=pltpu.PrefetchScalarGridSpec(
             num_scalar_prefetch=1,
             grid=(width // blk,),
-            in_specs=[big_spec] + [pl.BlockSpec(part.shape, lambda i, me: (0, 0), pipeline_mode=pl.Buffered(1)) for part in parts] + [any_spec] * len(prev),
+            in_specs=[any_spec] * len(parts) + big_specs + [any_spec] * len(prev),
             out_specs=[any_spec] * n_out,
-            scratch_shapes=[
-                pltpu.VMEM((rows, seq), BF16),
-                pltpu.VMEM(acc_shape, F32),
-                pltpu.SemaphoreType.DMA((2, len(rels) * n_out)),
-            ],
+            scratch_shapes=scratch,
         ),
         out_shape=[jax.ShapeDtypeStruct(shape, F32)] * n_out,
-        input_output_aliases={n_fixed + o: o for o in range(len(prev))},
+        input_output_aliases={n_lead + o: o for o in range(len(prev))},
         compiler_params=pltpu.CompilerParams(dimension_semantics=("arbitrary",), vmem_limit_bytes=60 * 1024 * 1024),
         cost_estimate=pl.CostEstimate(flops=2 * rows * width * seq, bytes_accessed=4 * width * rows + 2 * seq * (width + rows), transcendentals=0),
-    )(me, big, *parts, *prev)
+    )(me, *parts, *bigs, *prev)
 
 
 CORE, SIDE_X, SIDE_Y = 1, 2, 4
@@ -459,7 +509,8 @@
         two[SIDE_X | SIDE_Y] = swap(two[SIDE_X], SIDE_Y)
         for part in got:
             for rel in (0, SIDE_X, SIDE_Y):
-                part[rel | CORE] = swap(part[rel], CORE)
+                if rel | CORE not in part:
+                    part[rel | CORE] = swap(part[rel], CORE)
 
     def finish(got, dep=None):
         for part in got:
@@ -498,8 +549,13 @@
         every = tuple(range(n_dev))
         groups = ((0, 1), (2, 3, 4, 5), (6, 7))
 
+        feats = group * HEAD_DIM
+
         def pairs(got, rels):
-            return [half[r] for r in rels for half in got]
+            return [part[r] for r in rels for part in got]
+
+        def places(rels, parts=(0, 1)):
+            return tuple((0, r, part * (feats // 2)) for r in rels for part in parts)
 
         half = hidden.shape[1] // 2
         x_got = reach(hidden[:, :half], hidden[:, half:])
@@ -518,26 +574,31 @@
         x_turned = assemble(x_got, far, n_dev, x_turned, after(me_arr, dk_t), True)
         hold(g_got, x_turned)
         relay(g_got)
-        (g_q,) = weight_grad(x_turned, pairs(dq_got, (0,)) + [swap(dq_got[0][0], CORE), swap(dq_got[1][0], CORE)], groups[0], me_arr, None, False, 1, n_dev)
-        g_all = assemble(g_got, near, n_dev, None, after(me_arr, g_q), False)
-        finish(g_got, g_all)
-        g_all = assemble(g_got, far, n_dev, g_all, me_arr, False)
-        (g_o,) = weight_grad(g_all, pairs(ctx_got, (0,)) + [swap(ctx_got[0][0], CORE), swap(ctx_got[1][0], CORE)], groups[0], me_arr, None, True, 1, n_dev)
-        hold(ctx_got, g_o)
+        (g_q,) = weight_grad([x_turned], pairs(dq_got, (0,)) + [swap(dq_got[0][0], CORE), swap(dq_got[1][0], CORE)], places(groups[0]), feats, me_arr, None, False, 1, n_dev)
+        finish(g_got, g_q)
+        g_all = [part[r] for part in g_got for r in every]
+        (g_o,) = weight_grad(g_all, pairs(ctx_got, (0,)) + [swap(ctx_got[0][0], CORE), swap(ctx_got[1][0], CORE)], places(groups[0]), feats, after(me_arr, g_q), None, True, 1, n_dev)
+        for rel in (SIDE_X, SIDE_Y):
+            ctx_got[0][rel] = after(ctx_got[0][rel], g_o)
+            ctx_got[0][rel | CORE] = swap(ctx_got[0][rel], CORE)
+        (g_o,) = weight_grad(g_all, [ctx_got[0][r] for r in groups[1]], places(groups[1], (0,)), feats, me_arr, (g_o,), True, 1, n_dev)
+        for rel in (SIDE_X, SIDE_Y):
+            ctx_got[1][rel] = after(ctx_got[1][rel], g_o)
         relay(ctx_got)
-        (g_o,) = weight_grad(g_all, pairs(ctx_got, groups[1]), groups[1], me_arr, (g_o,), True, 1, n_dev)
+        (g_o,) = weight_grad(g_all, [ctx_got[1][r] for r in groups[1]], places(groups[1], (1,)), feats, me_arr, (g_o,), True, 1, n_dev)
         finish(ctx_got, g_o)
-        (g_o,) = weight_grad(g_all, pairs(ctx_got, groups[2]), groups[2], me_arr, (g_o,), True, 1, n_dev)
+        (g_o,) = weight_grad(g_all, pairs(ctx_got, groups[2]), places(groups[2]), feats, me_arr, (g_o,), True, 1, n_dev)
         hold(kv_got, g_o)
         relay(kv_got)
         attn_out = own_product([[[part[r] for part in ctx_got] for r in every]], [w_o], after(me_arr, g_o), tokens, False)
         finish(kv_got, attn_out)
-        g_k, g_v = weight_grad(x_turned, [kv_got[0][r] for r in every] + [kv_got[1][r] for r in every], every, after(me_arr, attn_out), None, False, 2, n_dev)
+        kv_places = tuple((o, r, 0) for o in range(2) for r in every)
+        g_k, g_v = weight_grad([x_turned], [kv_got[0][r] for r in every] + [kv_got[1][r] for r in every], kv_places, HEAD_DIM, after(me_arr, attn_out), None, False, 2, n_dev)
         hold(dq_got, g_k)
         relay(dq_got)
-        (g_q,) = weight_grad(x_turned, pairs(dq_got, groups[1]), groups[1], after(me_arr, g_k), (g_q,), False, 1, n_dev)
+        (g_q,) = weight_grad([x_turned], pairs(dq_got, groups[1]), places(groups[1]), feats, after(me_arr, g_k), (g_q,), False, 1, n_dev)
         finish(dq_got, g_q)
-        (g_q,) = weight_grad(x_turned, pairs(dq_got, groups[2]), groups[2], me_arr, (g_q,), False, 1, n_dev)
+        (g_q,) = weight_grad([x_turned], pairs(dq_got, groups[2]), places(groups[2]), feats, me_arr, (g_q,), False, 1, n_dev)
         sources = [[[part[r] for part in dq_got] for r in every], [[kv_got[0][r]] for r in every], [[kv_got[1][r]] for r in every]]
         grad_hidden = own_product(sources, [w_q, w_k, w_v], after(me_arr, g_q), tokens, True)
         return attn_out, grad_hidden, g_q, g_k, g_v, g_o

time: 659 us -> 687 us (1.042)
  waiting for transfers between devices: 186 us -> 211 us
  starting transfers between devices: 43.8 us -> 51 us
    ppermute x70, waiting for transfers between devices: 186 us -> 211 us  [swap(): return lax.ppermute(values, 'sp', [(i, i ^ bit) for i in range(n_dev)])]
    pallas_call x4 -> x2, Pallas kernels: 40.9 us -> 21.4 us  [assemble(): pl.pallas_call(body, grid_spec=pltpu.PrefetchScalarGridSpec(num_scalar_pr...]
    pallas_call x7 -> x8, Pallas kernels: 208 us -> 224 us  [weight_grad(): pl.pallas_call(body, grid_spec=pltpu.PrefetchScalarGridSpec(num_scalar_pr...]
    ppermute x70, starting transfers between devices: 38.5 us -> 45.6 us  [swap(): return lax.ppermute(values, 'sp', [(i, i ^ bit) for i in range(n_dev)])]
  transfers between devices with their start and end apart: 71 -> 71, of which waited for: 29 -> 34; matrix products, arithmetic and copies ran while one was open for 2% -> 2% of each run, Pallas kernels for 47% -> 45%
where the time goes in v4:
time: 687 us; the launch traced here: 683 us
  Pallas kernels  385 us (56%)
  waiting for transfers between devices  211 us (31%)
  starting transfers between devices  51 us (7%)
  other arithmetic  12.1 us (2%)
  blocking collectives  11.4 us (2%)
  local copies, waits for them, and re-layouts  10.8 us (2%)
    pallas_call x8, Pallas kernels, weight_grad(): pl.pallas_call(body, grid_spec=pltpu.PrefetchScalarGridSpec(num_scalar_pr...  224 us
    ppermute x70, waiting for transfers between devices, swap(): return lax.ppermute(values, 'sp', [(i, i ^ bit) for i in range(n_dev)])  211 us
    pallas_call x1, Pallas kernels, attention(): pl.pallas_call(functools.partial(attn_kernel, group), grid_spec=grid_spec...  67.6 us
    ppermute x70, starting transfers between devices, swap(): return lax.ppermute(values, 'sp', [(i, i ^ bit) for i in range(n_dev)])  45.6 us
    pallas_call x1, Pallas kernels, project(): pl.pallas_call(functools.partial(proj_kernel, group), grid=(n_dev,), in_s...  36.9 us
    pallas_call x2, Pallas kernels, own_product(): pl.pallas_call(functools.partial(own_kernel, kinds, turned), grid_spec=pl...  35.5 us
    pallas_call x2, Pallas kernels, assemble(): pl.pallas_call(body, grid_spec=pltpu.PrefetchScalarGridSpec(num_scalar_pr...  21.4 us
  transfers between devices with their start and end apart: 71, of which 34 were waited for; matrix products, arithmetic and copies ran while one was open for 2% of the time, Pallas kernels for 45%

profile of v4, /device:TPU:1, one launch (start us, length us, event | category | flops | bytes accessed | tf_op | source)
XLA Modules:
  0.0 682.8 jit_solution(10800229849550397174)
XLA Ops:
  2.7 11.4 %all-gather.1 = s32[8,2,384]{2,1,0:T(2,128)} all-gather(s32[1,2,384]{2,1,0:T(2,128)S(1)} %add_bitcast_fusion), channel_id=2, replica_groups=mesh['dp'=2,'sp'=8] {'sp'}, dimensions={0}, use_global_device_ids=true | all-gather | bytes 27648 | tf_op jit(solution)/shard_map/all_gather | solution.py:535
  15.8 36.9 %project.1 = bf16[8,384,1024]{2,1,0:T(8,128)(2,1)} custom-call(bf16[384,3072]{1,0:T(8,128)(2,1)} %x_ref, bf16[384,3072]{1,0:T(8,128)(2,1)} %g_ref, bf16[3072,3072]{1,0:T(8,128)(2,1)} %refs_32_.1, bf16[3072,1024]{1,0:T(8,128)(2,1)} %refs_33_.1, bf16[3072,1024]{1,0:T(8,128)(2,1)} %refs_34_.1, bf16[3072,3072]{1,0:T(8,128)(2,1)} %refs_16_.1, ...), custom_call_target="tpu_custom_call" | custom-call | flops 19327352832 | bytes 60000000 | tf_op jit(solution)/shard_map/project/pallas_call | solution.py:64
  52.7 5.4 all-to-all-start
  58.1 1.8 fusion.2
  59.9 1.4 collective-permute-start.6
  61.3 1.2 collective-permute-start.3
  62.8 1.2 collective-permute-start.13
  64.1 89.2 %collective-permute-done.6.refs_8_ = bf16[384,1536]{1,0:T(8,128)(2,1)} collective-permute-done((bf16[384,1536]{1,0:T(8,128)(2,1)S(1)}, bf16[384,1536]{1,0:T(8,128)(2,1)}, u32[]{:S(2)}, u32[]{:S(2)}) %collective-permute-start.6) | collective-permute-done | bytes 1179680 | tf_op jit(solution)/shard_map/ppermute | solution.py:501
  153.2 1.2 collective-permute-start.7
  154.8 4.6 convert_reduce_fusion
  159.4 1.3 slice.22
  160.7 1.3 and_select_fusion.lo_ref
  161.9 3.8 multiply_sine_fusion
  165.8 12.6 %collective-permute-done.15.refs_10_ = bf16[384,1536]{1,0:T(8,128)(2,1)S(1)} collective-permute-done((bf16[384,1536]{1,0:T(8,128)(2,1)S(1)}, bf16[384,1536]{1,0:T(8,128)(2,1)S(1)}, u32[]{:S(2)}, u32[]{:S(2)}) %collective-permute-start.15) | collective-permute-done | bytes 1179680 | tf_op jit(solution)/shard_map/ppermute | solution.py:501
  178.4 1.5 collective-permute-start.9
  180.4 23.3 %collective-permute-done.7.refs_2_ = bf16[384,1536]{1,0:T(8,128)(2,1)} collective-permute-done((bf16[384,1536]{1,0:T(8,128)(2,1)}, bf16[384,1536]{1,0:T(8,128)(2,1)}, u32[]{:S(2)}, u32[]{:S(2)}) %collective-permute-start.7) | collective-permute-done | bytes 1179680 | tf_op jit(solution)/shard_map/ppermute | solution.py:501
  204.7 67.6 %attention.1 = (bf16[192,3072]{1,0:T(8,128)(2,1)}, bf16[192,3072]{1,0:T(8,128)(2,1)}, bf16[192,3072]{1,0:T(8,128)(2,1)}, bf16[192,3072]{1,0:T(8,128)(2,1)}, bf16...) custom-call(s32[12]{0:T(128)} %and_select_fusion.lo_ref, bf16[3072,1024]{1,0:T(8,128)(2,1)} %bitcast.3.q_ref.do_ref.k_ref.v_ref, ...), custom_call_target="tpu_custom_call" | custom-call | flops 72477573120 | bytes 12000000 | tf_op jit(solution)/shard_map/attention/pallas_call | solution.py:229
  273.2 1.2 collective-permute-start.27
  274.7 1.2 collective-permute-start.29
  275.9 14.3 %shard_map.127.refs_4_ = bf16[3072,3072]{1,0:T(8,128)(2,1)} custom-call(s32[1]{0:T(128)} %bitcast.me_ref, bf16[384,1536]{1,0:T(8,128)(2,1)} %copy-done.8, bf16[384,1536]{1,0:T(8,128)(2,1)} %collective-permute-done.9.refs_1_, bf16[384,1536]{1,0:T(8,128)(2,1)} %collective-permute-done.10.refs_2_, bf16[384,1536]{1,0:T(8,128)(2,1)} %collective-permute-done.11.refs_3_, ...), custom_call_target="tpu_custom_call" | custom-call | bytes 28311552 | tf_op jit(solution)/shard_map/pallas_call | solution.py:290
  290.5 1.6 collective-permute-start.1
  292.1 7.0 %shard_map.128.refs_4_.refs_16_.refs_8_ = bf16[3072,3072]{1,0:T(8,128)(2,1)} custom-call(s32[1]{0:T(128)} %bitcast.me_ref, bf16[384,1536]{1,0:T(8,128)(2,1)} %collective-permute-done.4.refs_0_, bf16[384,1536]{1,0:T(8,128)(2,1)} %collective-permute-done.5.refs_1_, bf16[384,1536]{1,0:T(8,128)(2,1)} %collective-permute-done.7.refs_2_, ...), custom_call_target="tpu_custom_call", output_to_operand_aliasing={{}: (5, {})} | custom-call | bytes 9437184 | tf_op jit(solution)/shard_map/pallas_call | solution.py:290
  299.2 1.3 collective-permute-done.27.refs_14_
  300.4 2.1 collective-permute-start.2
  302.5 1.2 collective-permute-start.24
  303.7 22.9 %collective-permute-done.29.refs_16_ = bf16[384,1536]{1,0:T(8,128)(2,1)} collective-permute-done((bf16[384,1536]{1,0:T(8,128)(2,1)S(1)}, bf16[384,1536]{1,0:T(8,128)(2,1)}, u32[]{:S(2)}, u32[]{:S(2)}) %collective-permute-start.29) | collective-permute-done | bytes 1179680 | tf_op jit(solution)/shard_map/ppermute | solution.py:501
  327.1 1.7 collective-permute-start.26
  329.3 21.6 %collective-permute-done.24.refs_10_ = bf16[384,1536]{1,0:T(8,128)(2,1)S(1)} collective-permute-done((bf16[384,1536]{1,0:T(8,128)(2,1)}, bf16[384,1536]{1,0:T(8,128)(2,1)S(1)}, u32[]{:S(2)}, u32[]{:S(2)}) %collective-permute-start.24) | collective-permute-done | bytes 1179680 | tf_op jit(solution)/shard_map/ppermute | solution.py:501
  350.9 1.3 collective-permute-start.18
  353.6 2.4 collective-permute-start.21
  356.0 22.9 %shard_map.129.refs_9_ = f32[3072,3072]{1,0:T(8,128)} custom-call(s32[1]{0:T(128)} %bitcast.me_ref, bf16[192,3072]{1,0:T(8,128)(2,1)} %get-tuple-element.53.refs_0_, bf16[192,3072]{1,0:T(8,128)(2,1)} %get-tuple-element.54.refs_1_, bf16[192,3072]{1,0:T(8,128)(2,1)} %collective-permute-done.1.refs_2_, bf16[192,3072]{1,0:T(8,128)(2,1)} %copy-done.11, ...), custom_call_target="tpu_custom_call" | custom-call | flops 14495514624 | bytes 33030144 | tf_op jit(solution)/shard_map/pallas_call | solution.py:478
  380.1 2.0 collective-permute-done.23.refs_9_
  382.5 1.2 collective-permute-done.28.refs_15_
  384.2 1.4 collective-permute-done.30.refs_17_
  385.6 1.7 collective-permute-done.25.refs_11_
  387.3 1.7 collective-permute-done.32.refs_19_
  389.0 21.8 %shard_map.130.refs_20_ = f32[3072,3072]{1,0:T(8,128)} custom-call(s32[1]{0:T(128)} %bitcast.me_ref, bf16[192,3072]{1,0:T(8,128)(2,1)} %get-tuple-element.52.refs_0_, bf16[192,3072]{1,0:T(8,128)(2,1)} %get-tuple-element.60.refs_1_, bf16[192,3072]{1,0:T(8,128)(2,1)} %collective-permute-done.17.refs_2_, bf16[192,3072]{1,0:T(8,128)(2,1)} %collective-permute-done.18.refs_3_, ...), custom_call_target="tpu_custom_call" | custom-call | flops 14495514624 | bytes 33030144 | tf_op jit(solution)/shard_map/pallas_call | solution.py:478
  412.9 1.4 collective-permute-start.34
  415.2 1.7 collective-permute-done.36.refs_1_.refs_6_
  417.9 21.8 %shard_map.131.refs_20_ = f32[3072,3072]{1,0:T(8,128)} custom-call(s32[1]{0:T(128)} %bitcast.me_ref, bf16[192,3072]{1,0:T(8,128)(2,1)} %collective-permute-done.35.refs_0_.refs_4_, bf16[192,3072]{1,0:T(8,128)(2,1)} %copy-done.14, bf16[192,3072]{1,0:T(8,128)(2,1)} %collective-permute-done.refs_2_.refs_8_, ...), custom_call_target="tpu_custom_call", output_to_operand_aliasing={{}: (21, {})} | custom-call | flops 14495514624 | bytes 33030144 | tf_op jit(solution)/shard_map/pallas_call | solution.py:478
  439.8 1.6 collective-permute-start.39
  441.4 1.4 collective-permute-start.33
  442.9 1.2 collective-permute-done.39.refs_1_.refs_7_
  444.1 1.7 collective-permute-done.41.refs_3_.refs_11_
  446.8 21.8 %shard_map.132.refs_20_ = f32[3072,3072]{1,0:T(8,128)} custom-call(s32[1]{0:T(128)} %bitcast.me_ref, bf16[192,3072]{1,0:T(8,128)(2,1)} %collective-permute-done.34.refs_0_.refs_5_, bf16[192,3072]{1,0:T(8,128)(2,1)} %copy-done.15, bf16[192,3072]{1,0:T(8,128)(2,1)} %collective-permute-done.40.refs_2_.refs_9_, ...), custom_call_target="tpu_custom_call", output_to_operand_aliasing={{}: (21, {})} | custom-call | flops 14495514624 | bytes 33030144 | tf_op jit(solution)/shard_map/pallas_call | solution.py:478
  468.7 1.3 collective-permute-done.38.refs_1_.refs_13_
  469.9 1.6 collective-permute-start.42
  474.6 1.2 collective-permute-done.43.refs_3_.refs_15_
  475.7 1.0 copy-done.19
  476.8 21.8 %shard_map.133 = f32[3072,3072]{1,0:T(8,128)} custom-call(s32[1]{0:T(128)} %bitcast.me_ref, bf16[192,3072]{1,0:T(8,128)(2,1)} %copy-done.17, bf16[192,3072]{1,0:T(8,128)(2,1)} %collective-permute-done.38.refs_1_.refs_13_, bf16[192,3072]{1,0:T(8,128)(2,1)} %copy-done.18, bf16[192,3072]{1,0:T(8,128)(2,1)} %copy-done.19, ...), custom_call_target="tpu_custom_call", output_to_operand_aliasing={{}: (21, {})} | custom-call | flops 14495514624 | bytes 33030144 | tf_op jit(solution)/shard_map/pallas_call | solution.py:478
  498.7 8.8 %collective-permute-done.48.refs_4_.refs_20_ = bf16[128,3072]{1,0:T(8,128)(2,1)} collective-permute-done((bf16[128,3072]{1,0:T(8,128)(2,1)}, bf16[128,3072]{1,0:T(8,128)(2,1)}, u32[]{:S(2)}, u32[]{:S(2)}) %collective-permute-start.48) | collective-permute-done | bytes 786464 | tf_op jit(solution)/shard_map/ppermute | solution.py:501
  508.5 1.9 collective-permute-start.52
  510.9 14.0 %shard_map.134 = bf16[384,3072]{1,0:T(8,128)(2,1)} custom-call(s32[1]{0:T(128)} %bitcast.me_ref, bf16[192,3072]{1,0:T(8,128)(2,1)} %get-tuple-element.52.refs_0_, bf16[192,3072]{1,0:T(8,128)(2,1)} %get-tuple-element.60.refs_1_, bf16[192,3072]{1,0:T(8,128)(2,1)} %collective-permute-done.17.refs_2_, bf16[192,3072]{1,0:T(8,128)(2,1)} %collective-permute-done.18.refs_3_, ...), custom_call_target="tpu_custom_call" | custom-call | flops 7247757312 | bytes 21233664 | tf_op jit(solution)/shard_map/pallas_call | solution.py:342
  525.5 2.2 collective-permute-start.49
  531.0 1.1 collective-permute-done.56.refs_13_.refs_29_
  534.4 51.3 %shard_map.135 = (f32[3072,1024]{1,0:T(8,128)}, f32[3072,1024]{1,0:T(8,128)}) custom-call(s32[1]{0:T(128)} %bitcast.me_ref, bf16[128,3072]{1,0:T(8,128)(2,1)} %get-tuple-element.55.refs_0_.refs_16_, bf16[128,3072]{1,0:T(8,128)(2,1)} %copy-done.29, bf16[128,3072]{1,0:T(8,128)(2,1)} %collective-permute-done.46.refs_2_.refs_18_, ...), custom_call_target="tpu_custom_call" | custom-call | flops 38654705664 | bytes 56623104 | tf_op jit(solution)/shard_map/pallas_call | solution.py:478
  587.3 1.7 collective-permute-done.66.refs_6_.refs_10_
  589.3 1.3 collective-permute-done.64.refs_3_.refs_7_
  590.5 1.7 collective-permute-done.63.refs_2_.refs_6_
  594.1 39.4 %shard_map.136.refs_5_ = f32[3072,3072]{1,0:T(8,128)} custom-call(s32[1]{0:T(128)} %bitcast.me_ref, bf16[192,3072]{1,0:T(8,128)(2,1)} %copy-done.25, bf16[192,3072]{1,0:T(8,128)(2,1)} %collective-permute-done.60.refs_1_.refs_5_, bf16[192,3072]{1,0:T(8,128)(2,1)} %copy-done.27, bf16[192,3072]{1,0:T(8,128)(2,1)} %copy-done.26, ...), custom_call_target="tpu_custom_call", output_to_operand_aliasing={{}: (10, {})} | custom-call | flops 28991029248 | bytes 47185920 | tf_op jit(solution)/shard_map/pallas_call | solution.py:478
  634.1 2.3 collective-permute-done.68.refs_2_.refs_14_
  636.4 1.8 collective-permute-done.69.refs_3_.refs_15_
  638.2 22.8 %shard_map.137 = f32[3072,3072]{1,0:T(8,128)} custom-call(s32[1]{0:T(128)} %bitcast.me_ref, bf16[192,3072]{1,0:T(8,128)(2,1)} %copy-done.20, bf16[192,3072]{1,0:T(8,128)(2,1)} %copy-done.21, bf16[192,3072]{1,0:T(8,128)(2,1)} %copy-done.22, bf16[192,3072]{1,0:T(8,128)(2,1)} %collective-permute-done.69.refs_3_.refs_15_, ...), custom_call_target="tpu_custom_call", output_to_operand_aliasing={{}: (6, {})} | custom-call | flops 14495514624 | bytes 33030144 | tf_op jit(solution)/shard_map/pallas_call | solution.py:478
  661.0 21.5 %shard_map.138 = bf16[384,3072]{1,0:T(8,128)(2,1)} custom-call(s32[1]{0:T(128)} %bitcast.me_ref, bf16[192,3072]{1,0:T(8,128)(2,1)} %get-tuple-element.53.refs_0_, bf16[192,3072]{1,0:T(8,128)(2,1)} %get-tuple-element.54.refs_1_, bf16[192,3072]{1,0:T(8,128)(2,1)} %collective-permute-done.1.refs_2_, bf16[192,3072]{1,0:T(8,128)(2,1)} %copy-done.11, ...), custom_call_target="tpu_custom_call" | custom-call | flops 12079595520 | bytes 35389440 | tf_op jit(solution)/shard_map/pallas_call | solution.py:342
  (177 shorter events, 31.9 us)
Async XLA Ops:
  52.7 152.0 %all-to-all-start = ((bf16[8,384,1024]{2,1,0:T(8,128)(2,1)}), bf16[8,384,1024]{2,1,0:T(8,128)(2,1)}, u32[]{:S(2)}, u32[]{:S(2)}) async-start(bf16[8,384,1024]{2,1,0:T(8,128)(2,1)} %project.1), calls=%async_computation | async-start | bytes 12582912 | tf_op jit(solution)/shard_map/all_to_all | solution.py:563
  59.9 93.3 %collective-permute-start.6 = (bf16[384,1536]{1,0:T(8,128)(2,1)S(1)}, bf16[384,1536]{1,0:T(8,128)(2,1)}, u32[]{:S(2)}, u32[]{:S(2)}) collective-permute-start(bf16[384,1536]{1,0:T(8,128)(2,1)S(1)} %get-tuple-element.94.refs_6_), channel_id=1, source_target_pairs={{0,2},{1,3},{2,0},{3,1},{4,6},{5,7},{6,4},{7,5},{8,10},{9,11},{10,... | collective-permute-start | bytes 3538952 | tf_op jit(solution)/shard_map/ppermute | solution.py:501
  61.3 93.1 %collective-permute-start.3 = (bf16[384,1536]{1,0:T(8,128)(2,1)S(1)}, bf16[384,1536]{1,0:T(8,128)(2,1)}, u32[]{:S(2)}, u32[]{:S(2)}) collective-permute-start(bf16[384,1536]{1,0:T(8,128)(2,1)S(1)} %get-tuple-element.95.refs_0_), channel_id=1, source_target_pairs={{0,4},{1,5},{2,6},{3,7},{4,0},{5,1},{6,2},{7,3},{8,12},{9,13},{10,... | collective-permute-start | bytes 3538952 | tf_op jit(solution)/shard_map/ppermute | solution.py:501
  62.5 115.8 %collective-permute-start.15 = (bf16[384,1536]{1,0:T(8,128)(2,1)S(1)}, bf16[384,1536]{1,0:T(8,128)(2,1)S(1)}, u32[]{:S(2)}, u32[]{:S(2)}) collective-permute-start(bf16[384,1536]{1,0:T(8,128)(2,1)S(1)} %get-tuple-element.94.refs_6_), channel_id=1, source_target_pairs={{0,4},{1,5},{2,6},{3,7},{4,0},{5,1},{6,2},{7,3},{8,12},{9,13},{10,... | collective-permute-start | bytes 3538952 | tf_op jit(solution)/shard_map/ppermute | solution.py:501
  62.8 117.0 %collective-permute-start.13 = (bf16[384,1536]{1,0:T(8,128)(2,1)S(1)}, bf16[384,1536]{1,0:T(8,128)(2,1)}, u32[]{:S(2)}, u32[]{:S(2)}) collective-permute-start(bf16[384,1536]{1,0:T(8,128)(2,1)S(1)} %get-tuple-element.94.refs_6_), channel_id=1, source_target_pairs={{0,1},{1,0},{2,3},{3,2},{4,5},{5,4},{6,7},{7,6},{8,9},{9,8},{10,11... | collective-permute-start | bytes 3538952 | tf_op jit(solution)/shard_map/ppermute | solution.py:501
  64.0 115.9 %collective-permute-start.10 = (bf16[384,1536]{1,0:T(8,128)(2,1)S(1)}, bf16[384,1536]{1,0:T(8,128)(2,1)}, u32[]{:S(2)}, u32[]{:S(2)}) collective-permute-start(bf16[384,1536]{1,0:T(8,128)(2,1)S(1)} %get-tuple-element.95.refs_0_), channel_id=1, source_target_pairs={{0,2},{1,3},{2,0},{3,1},{4,6},{5,7},{6,4},{7,5},{8,10},{9,11},{10,... | collective-permute-start | bytes 3538952 | tf_op jit(solution)/shard_map/ppermute | solution.py:501
  153.2 50.4 %collective-permute-start.7 = (bf16[384,1536]{1,0:T(8,128)(2,1)}, bf16[384,1536]{1,0:T(8,128)(2,1)}, u32[]{:S(2)}, u32[]{:S(2)}) collective-permute-start(bf16[384,1536]{1,0:T(8,128)(2,1)} %collective-permute-done.6.refs_8_), channel_id=1, source_target_pairs={{0,4},{1,5},{2,6},{3,7},{4,0},{5,1},{6,2},{7,3},{8,12},{9,13},{10,... | collective-permute-start | bytes 3538952 | tf_op jit(solution)/shard_map/ppermute | solution.py:501
  154.4 50.2 %collective-permute-start.4 = (bf16[384,1536]{1,0:T(8,128)(2,1)}, bf16[384,1536]{1,0:T(8,128)(2,1)}, u32[]{:S(2)}, u32[]{:S(2)}) collective-permute-start(bf16[384,1536]{1,0:T(8,128)(2,1)} %collective-permute-done.3.refs_4_), channel_id=1, source_target_pairs={{0,2},{1,3},{2,0},{3,1},{4,6},{5,7},{6,4},{7,5},{8,10},{9,11},{10,... | collective-permute-start | bytes 3538952 | tf_op jit(solution)/shard_map/ppermute | solution.py:501
  178.4 94.1 %collective-permute-start.9 = (bf16[384,1536]{1,0:T(8,128)(2,1)S(1)}, bf16[384,1536]{1,0:T(8,128)(2,1)}, u32[]{:S(2)}, u32[]{:S(2)}) collective-permute-start(bf16[384,1536]{1,0:T(8,128)(2,1)S(1)} %get-tuple-element.95.refs_0_), channel_id=1, source_target_pairs={{0,1},{1,0},{2,3},{3,2},{4,5},{5,4},{6,7},{7,6},{8,9},{9,8},{10,11... | collective-permute-start | bytes 3538952 | tf_op jit(solution)/shard_map/ppermute | solution.py:501
  179.9 93.3 %collective-permute-start.14 = (bf16[384,1536]{1,0:T(8,128)(2,1)}, bf16[384,1536]{1,0:T(8,128)(2,1)}, u32[]{:S(2)}, u32[]{:S(2)}) collective-permute-start(bf16[384,1536]{1,0:T(8,128)(2,1)} %collective-permute-done.6.refs_8_), channel_id=1, source_target_pairs={{0,1},{1,0},{2,3},{3,2},{4,5},{5,4},{6,7},{7,6},{8,9},{9,8},{10,11... | collective-permute-start | bytes 3538952 | tf_op jit(solution)/shard_map/ppermute | solution.py:501
  179.9 94.8 %collective-permute-start.12 = (bf16[384,1536]{1,0:T(8,128)(2,1)}, bf16[384,1536]{1,0:T(8,128)(2,1)}, u32[]{:S(2)}, u32[]{:S(2)}) collective-permute-start(bf16[384,1536]{1,0:T(8,128)(2,1)} %collective-permute-done.3.refs_4_), channel_id=1, source_target_pairs={{0,1},{1,0},{2,3},{3,2},{4,5},{5,4},{6,7},{7,6},{8,9},{9,8},{10,11... | collective-permute-start | bytes 3538952 | tf_op jit(solution)/shard_map/ppermute | solution.py:501
  203.6 69.3 %collective-permute-start.16 = (bf16[384,1536]{1,0:T(8,128)(2,1)S(1)}, bf16[384,1536]{1,0:T(8,128)(2,1)}, u32[]{:S(2)}, u32[]{:S(2)}) collective-permute-start(bf16[384,1536]{1,0:T(8,128)(2,1)S(1)} %collective-permute-done.15.refs_10_), channel_id=1, source_target_pairs={{0,1},{1,0},{2,3},{3,2},{4,5},{5,4},{6,7},{7,6},{8,9},{9,8},{10,11... | collective-permute-start | bytes 3538952 | tf_op jit(solution)/shard_map/ppermute | solution.py:501
  204.6 69.8 %collective-permute-start.11 = (bf16[384,1536]{1,0:T(8,128)(2,1)}, bf16[384,1536]{1,0:T(8,128)(2,1)}, u32[]{:S(2)}, u32[]{:S(2)}) collective-permute-start(bf16[384,1536]{1,0:T(8,128)(2,1)} %collective-permute-done.10.refs_2_), channel_id=1, source_target_pairs={{0,1},{1,0},{2,3},{3,2},{4,5},{5,4},{6,7},{7,6},{8,9},{9,8},{10,11... | collective-permute-start | bytes 3538952 | tf_op jit(solution)/shard_map/ppermute | solution.py:501
  272.4 17.8 %collective-permute-start.5 = (bf16[384,1536]{1,0:T(8,128)(2,1)}, bf16[384,1536]{1,0:T(8,128)(2,1)}, u32[]{:S(2)}, u32[]{:S(2)}) collective-permute-start(bf16[384,1536]{1,0:T(8,128)(2,1)} %collective-permute-done.4.refs_0_), channel_id=1, source_target_pairs={{0,1},{1,0},{2,3},{3,2},{4,5},{5,4},{6,7},{7,6},{8,9},{9,8},{10,11... | collective-permute-start | bytes 3538952 | tf_op jit(solution)/shard_map/ppermute | solution.py:501
  272.9 17.6 %collective-permute-start.8 = (bf16[384,1536]{1,0:T(8,128)(2,1)}, bf16[384,1536]{1,0:T(8,128)(2,1)}, u32[]{:S(2)}, u32[]{:S(2)}) collective-permute-start(bf16[384,1536]{1,0:T(8,128)(2,1)} %collective-permute-done.7.refs_2_), channel_id=1, source_target_pairs={{0,1},{1,0},{2,3},{3,2},{4,5},{5,4},{6,7},{7,6},{8,9},{9,8},{10,11... | collective-permute-start | bytes 3538952 | tf_op jit(solution)/shard_map/ppermute | solution.py:501
  273.2 27.2 %collective-permute-start.27 = (bf16[384,1536]{1,0:T(8,128)(2,1)S(1)}, bf16[384,1536]{1,0:T(8,128)(2,1)S(1)}, u32[]{:S(2)}, u32[]{:S(2)}) collective-permute-start(bf16[384,1536]{1,0:T(8,128)(2,1)S(1)} %get-tuple-element.92.refs_12_), channel_id=1, source_target_pairs={{0,2},{1,3},{2,0},{3,1},{4,6},{5,7},{6,4},{7,5},{8,10},{9,11},{10,... | collective-permute-start | bytes 3538952 | tf_op jit(solution)/shard_map/ppermute | solution.py:501
  274.4 28.1 %collective-permute-start.22 = (bf16[384,1536]{1,0:T(8,128)(2,1)S(1)}, bf16[384,1536]{1,0:T(8,128)(2,1)}, u32[]{:S(2)}, u32[]{:S(2)}) collective-permute-start(bf16[384,1536]{1,0:T(8,128)(2,1)S(1)} %get-tuple-element.93.refs_4_), channel_id=1, source_target_pairs={{0,4},{1,5},{2,6},{3,7},{4,0},{5,1},{6,2},{7,3},{8,12},{9,13},{10,... | collective-permute-start | bytes 3538952 | tf_op jit(solution)/shard_map/ppermute | solution.py:501
  274.7 51.9 %collective-permute-start.29 = (bf16[384,1536]{1,0:T(8,128)(2,1)S(1)}, bf16[384,1536]{1,0:T(8,128)(2,1)}, u32[]{:S(2)}, u32[]{:S(2)}) collective-permute-start(bf16[384,1536]{1,0:T(8,128)(2,1)S(1)} %get-tuple-element.92.refs_12_), channel_id=1, source_target_pairs={{0,4},{1,5},{2,6},{3,7},{4,0},{5,1},{6,2},{7,3},{8,12},{9,13},{10,... | collective-permute-start | bytes 3538952 | tf_op jit(solution)/shard_map/ppermute | solution.py:501
  290.2 36.8 %collective-permute-start.20 = (bf16[384,1536]{1,0:T(8,128)(2,1)S(1)}, bf16[384,1536]{1,0:T(8,128)(2,1)}, u32[]{:S(2)}, u32[]{:S(2)}) collective-permute-start(bf16[384,1536]{1,0:T(8,128)(2,1)S(1)} %get-tuple-element.93.refs_4_), channel_id=1, source_target_pairs={{0,2},{1,3},{2,0},{3,1},{4,6},{5,7},{6,4},{7,5},{8,10},{9,11},{10,... | collective-permute-start | bytes 3538952 | tf_op jit(solution)/shard_map/ppermute | solution.py:501
  290.5 38.2 %collective-permute-start.1 = (bf16[192,3072]{1,0:T(8,128)(2,1)}, bf16[192,3072]{1,0:T(8,128)(2,1)}, u32[]{:S(2)}, u32[]{:S(2)}) collective-permute-start(bf16[192,3072]{1,0:T(8,128)(2,1)} %get-tuple-element.53.refs_0_), channel_id=1, source_target_pairs={{0,1},{1,0},{2,3},{3,2},{4,5},{5,4},{6,7},{7,6},{8,9},{9,8},{10,11... | collective-permute-start | bytes 3538952 | tf_op jit(solution)/shard_map/ppermute | solution.py:501
  300.4 28.4 %collective-permute-start.2 = (bf16[192,3072]{1,0:T(8,128)(2,1)}, bf16[192,3072]{1,0:T(8,128)(2,1)S(1)}, u32[]{:S(2)}, u32[]{:S(2)}) collective-permute-start(bf16[192,3072]{1,0:T(8,128)(2,1)} %get-tuple-element.54.refs_1_), channel_id=1, source_target_pairs={{0,1},{1,0},{2,3},{3,2},{4,5},{5,4},{6,7},{7,6},{8,9},{9,8},{10,11... | collective-permute-start | bytes 3538952 | tf_op jit(solution)/shard_map/ppermute | solution.py:501
  302.5 48.3 %collective-permute-start.24 = (bf16[384,1536]{1,0:T(8,128)(2,1)}, bf16[384,1536]{1,0:T(8,128)(2,1)S(1)}, u32[]{:S(2)}, u32[]{:S(2)}) collective-permute-start(bf16[384,1536]{1,0:T(8,128)(2,1)} %collective-permute-done.22.refs_8_), channel_id=1, source_target_pairs={{0,2},{1,3},{2,0},{3,1},{4,6},{5,7},{6,4},{7,5},{8,10},{9,11},{10,... | collective-permute-start | bytes 3538952 | tf_op jit(solution)/shard_map/ppermute | solution.py:501
  326.6 25.9 %collective-permute-start.31 = (bf16[384,1536]{1,0:T(8,128)(2,1)S(1)}, bf16[384,1536]{1,0:T(8,128)(2,1)S(1)}, u32[]{:S(2)}, u32[]{:S(2)}) collective-permute-start(bf16[384,1536]{1,0:T(8,128)(2,1)S(1)} %collective-permute-done.27.refs_14_), channel_id=1, source_target_pairs={{0,4},{1,5},{2,6},{3,7},{4,0},{5,1},{6,2},{7,3},{8,12},{9,13},{10,... | collective-permute-start | bytes 3538952 | tf_op jit(solution)/shard_map/ppermute | solution.py:501
  327.1 51.9 %collective-permute-start.26 = (bf16[384,1536]{1,0:T(8,128)(2,1)S(1)}, bf16[384,1536]{1,0:T(8,128)(2,1)}, u32[]{:S(2)}, u32[]{:S(2)}) collective-permute-start(bf16[384,1536]{1,0:T(8,128)(2,1)S(1)} %get-tuple-element.92.refs_12_), channel_id=1, source_target_pairs={{0,1},{1,0},{2,3},{3,2},{4,5},{5,4},{6,7},{7,6},{8,9},{9,8},{10,11... | collective-permute-start | bytes 3538952 | tf_op jit(solution)/shard_map/ppermute | solution.py:501
  328.7 50.3 %collective-permute-start.19 = (bf16[384,1536]{1,0:T(8,128)(2,1)S(1)}, bf16[384,1536]{1,0:T(8,128)(2,1)}, u32[]{:S(2)}, u32[]{:S(2)}) collective-permute-start(bf16[384,1536]{1,0:T(8,128)(2,1)S(1)} %get-tuple-element.93.refs_4_), channel_id=1, source_target_pairs={{0,1},{1,0},{2,3},{3,2},{4,5},{5,4},{6,7},{7,6},{8,9},{9,8},{10,11... | collective-permute-start | bytes 3538952 | tf_op jit(solution)/shard_map/ppermute | solution.py:501
  328.8 50.7 %collective-permute-start.17 = (bf16[192,3072]{1,0:T(8,128)(2,1)}, bf16[192,3072]{1,0:T(8,128)(2,1)}, u32[]{:S(2)}, u32[]{:S(2)}) collective-permute-start(bf16[192,3072]{1,0:T(8,128)(2,1)} %get-tuple-element.52.refs_0_), channel_id=1, source_target_pairs={{0,1},{1,0},{2,3},{3,2},{4,5},{5,4},{6,7},{7,6},{8,9},{9,8},{10,11... | collective-permute-start | bytes 3538952 | tf_op jit(solution)/shard_map/ppermute | solution.py:501
  350.9 28.7 %collective-permute-start.18 = (bf16[192,3072]{1,0:T(8,128)(2,1)}, bf16[192,3072]{1,0:T(8,128)(2,1)}, u32[]{:S(2)}, u32[]{:S(2)}) collective-permute-start(bf16[192,3072]{1,0:T(8,128)(2,1)} %get-tuple-element.60.refs_1_), channel_id=1, source_target_pairs={{0,1},{1,0},{2,3},{3,2},{4,5},{5,4},{6,7},{7,6},{8,9},{9,8},{10,11... | collective-permute-start | bytes 3538952 | tf_op jit(solution)/shard_map/ppermute | solution.py:501
  353.6 26.5 %collective-permute-start.21 = (bf16[384,1536]{1,0:T(8,128)(2,1)}, bf16[384,1536]{1,0:T(8,128)(2,1)}, u32[]{:S(2)}, u32[]{:S(2)}) collective-permute-start(bf16[384,1536]{1,0:T(8,128)(2,1)} %collective-permute-done.20.refs_6_), channel_id=1, source_target_pairs={{0,1},{1,0},{2,3},{3,2},{4,5},{5,4},{6,7},{7,6},{8,9},{9,8},{10,11... | collective-permute-start | bytes 3538952 | tf_op jit(solution)/shard_map/ppermute | solution.py:501
  379.1 4.7 collective-permute-start.28
  379.5 6.0 collective-permute-start.30
  379.6 7.7 %collective-permute-start.25 = (bf16[384,1536]{1,0:T(8,128)(2,1)}, bf16[384,1536]{1,0:T(8,128)(2,1)}, u32[]{:S(2)}, u32[]{:S(2)}) collective-permute-start(bf16[384,1536]{1,0:T(8,128)(2,1)} %copy-done.3), channel_id=1, source_target_pairs={{0,1},{1,0},{2,3},{3,2},{4,5},{5,4},{6,7},{7,6},{8,9},{9,8},{10,11... | collective-permute-start | bytes 3538952 | tf_op jit(solution)/shard_map/ppermute | solution.py:501
  380.1 8.9 %collective-permute-start.32 = (bf16[384,1536]{1,0:T(8,128)(2,1)}, bf16[384,1536]{1,0:T(8,128)(2,1)}, u32[]{:S(2)}, u32[]{:S(2)}) collective-permute-start(bf16[384,1536]{1,0:T(8,128)(2,1)} %copy-done.4), channel_id=1, source_target_pairs={{0,1},{1,0},{2,3},{3,2},{4,5},{5,4},{6,7},{7,6},{8,9},{9,8},{10,11... | collective-permute-start | bytes 3538952 | tf_op jit(solution)/shard_map/ppermute | solution.py:501
  382.1 28.7 %collective-permute-start.35 = (bf16[192,3072]{1,0:T(8,128)(2,1)}, bf16[192,3072]{1,0:T(8,128)(2,1)}, u32[]{:S(2)}, u32[]{:S(2)}) collective-permute-start(bf16[192,3072]{1,0:T(8,128)(2,1)} %get-tuple-element.52.refs_0_), channel_id=1, source_target_pairs={{0,2},{1,3},{2,0},{3,1},{4,6},{5,7},{6,4},{7,5},{8,10},{9,11},{10,... | collective-permute-start | bytes 3538952 | tf_op jit(solution)/shard_map/ppermute | solution.py:501
  383.8 27.7 %collective-permute-start = (bf16[192,3072]{1,0:T(8,128)(2,1)}, bf16[192,3072]{1,0:T(8,128)(2,1)}, u32[]{:S(2)}, u32[]{:S(2)}) collective-permute-start(bf16[192,3072]{1,0:T(8,128)(2,1)} %get-tuple-element.52.refs_0_), channel_id=1, source_target_pairs={{0,4},{1,5},{2,6},{3,7},{4,0},{5,1},{6,2},{7,3},{8,12},{9,13},{10,... | collective-permute-start | bytes 3538952 | tf_op jit(solution)/shard_map/ppermute | solution.py:501
  412.5 4.4 collective-permute-start.36
  412.5 27.2 %collective-permute-start.40 = (bf16[192,3072]{1,0:T(8,128)(2,1)S(1)}, bf16[192,3072]{1,0:T(8,128)(2,1)}, u32[]{:S(2)}, u32[]{:S(2)}) collective-permute-start(bf16[192,3072]{1,0:T(8,128)(2,1)S(1)} %copy-done.12), channel_id=1, source_target_pairs={{0,4},{1,5},{2,6},{3,7},{4,0},{5,1},{6,2},{7,3},{8,12},{9,13},{10,... | collective-permute-start | bytes 3538952 | tf_op jit(solution)/shard_map/ppermute | solution.py:501
  412.9 26.8 %collective-permute-start.34 = (bf16[192,3072]{1,0:T(8,128)(2,1)S(1)}, bf16[192,3072]{1,0:T(8,128)(2,1)}, u32[]{:S(2)}, u32[]{:S(2)}) collective-permute-start(bf16[192,3072]{1,0:T(8,128)(2,1)S(1)} %copy-done.12), channel_id=1, source_target_pairs={{0,2},{1,3},{2,0},{3,1},{4,6},{5,7},{6,4},{7,5},{8,10},{9,11},{10,... | collective-permute-start | bytes 3538952 | tf_op jit(solution)/shard_map/ppermute | solution.py:501
  439.8 4.3 collective-permute-start.39
  441.4 4.4 collective-permute-start.41
  441.4 28.5 %collective-permute-start.33 = (bf16[192,3072]{1,0:T(8,128)(2,1)}, bf16[192,3072]{1,0:T(8,128)(2,1)S(1)}, u32[]{:S(2)}, u32[]{:S(2)}) collective-permute-start(bf16[192,3072]{1,0:T(8,128)(2,1)} %collective-permute-done.refs_2_.refs_8_), channel_id=1, source_target_pairs={{0,2},{1,3},{2,0},{3,1},{4,6},{5,7},{6,4},{7,5},{8,10},{9,11},{10,... | collective-permute-start | bytes 3538952 | tf_op jit(solution)/shard_map/ppermute | solution.py:501
  442.9 27.1 %collective-permute-start.38 = (bf16[192,3072]{1,0:T(8,128)(2,1)}, bf16[192,3072]{1,0:T(8,128)(2,1)}, u32[]{:S(2)}, u32[]{:S(2)}) collective-permute-start(bf16[192,3072]{1,0:T(8,128)(2,1)} %collective-permute-done.34.refs_0_.refs_5_), channel_id=1, source_target_pairs={{0,4},{1,5},{2,6},{3,7},{4,0},{5,1},{6,2},{7,3},{8,12},{9,13},{10,... | collective-permute-start | bytes 3538952 | tf_op jit(solution)/shard_map/ppermute | solution.py:501
  471.6 38.7 %collective-permute-start.55 = (bf16[128,3072]{1,0:T(8,128)(2,1)}, bf16[128,3072]{1,0:T(8,128)(2,1)}, u32[]{:S(2)}, u32[]{:S(2)}) collective-permute-start(bf16[128,3072]{1,0:T(8,128)(2,1)} %get-tuple-element.78.refs_8_.refs_24_), channel_id=1, source_target_pairs={{0,4},{1,5},{2,6},{3,7},{4,0},{5,1},{6,2},{7,3},{8,12},{9,13},{10,... | collective-permute-start | bytes 2359304 | tf_op jit(solution)/shard_map/ppermute | solution.py:501
  471.7 35.8 %collective-permute-start.53 = (bf16[128,3072]{1,0:T(8,128)(2,1)}, bf16[128,3072]{1,0:T(8,128)(2,1)}, u32[]{:S(2)}, u32[]{:S(2)}) collective-permute-start(bf16[128,3072]{1,0:T(8,128)(2,1)} %get-tuple-element.78.refs_8_.refs_24_), channel_id=1, source_target_pairs={{0,2},{1,3},{2,0},{3,1},{4,6},{5,7},{6,4},{7,5},{8,10},{9,11},{10,... | collective-permute-start | bytes 2359304 | tf_op jit(solution)/shard_map/ppermute | solution.py:501
  472.7 34.8 %collective-permute-start.48 = (bf16[128,3072]{1,0:T(8,128)(2,1)}, bf16[128,3072]{1,0:T(8,128)(2,1)}, u32[]{:S(2)}, u32[]{:S(2)}) collective-permute-start(bf16[128,3072]{1,0:T(8,128)(2,1)} %get-tuple-element.55.refs_0_.refs_16_), channel_id=1, source_target_pairs={{0,4},{1,5},{2,6},{3,7},{4,0},{5,1},{6,2},{7,3},{8,12},{9,13},{10,... | collective-permute-start | bytes 2359304 | tf_op jit(solution)/shard_map/ppermute | solution.py:501
  474.1 36.3 %collective-permute-start.46 = (bf16[128,3072]{1,0:T(8,128)(2,1)}, bf16[128,3072]{1,0:T(8,128)(2,1)}, u32[]{:S(2)}, u32[]{:S(2)}) collective-permute-start(bf16[128,3072]{1,0:T(8,128)(2,1)} %get-tuple-element.55.refs_0_.refs_16_), channel_id=1, source_target_pairs={{0,2},{1,3},{2,0},{3,1},{4,6},{5,7},{6,4},{7,5},{8,10},{9,11},{10,... | collective-permute-start | bytes 2359304 | tf_op jit(solution)/shard_map/ppermute | solution.py:501
  507.4 18.1 %collective-permute-start.50 = (bf16[128,3072]{1,0:T(8,128)(2,1)}, bf16[128,3072]{1,0:T(8,128)(2,1)}, u32[]{:S(2)}, u32[]{:S(2)}) collective-permute-start(bf16[128,3072]{1,0:T(8,128)(2,1)} %collective-permute-done.48.refs_4_.refs_20_), channel_id=1, source_target_pairs={{0,2},{1,3},{2,0},{3,1},{4,6},{5,7},{6,4},{7,5},{8,10},{9,11},{10,... | collective-permute-start | bytes 2359304 | tf_op jit(solution)/shard_map/ppermute | solution.py:501
  507.4 20.3 %collective-permute-start.57 = (bf16[128,3072]{1,0:T(8,128)(2,1)}, bf16[128,3072]{1,0:T(8,128)(2,1)}, u32[]{:S(2)}, u32[]{:S(2)}) collective-permute-start(bf16[128,3072]{1,0:T(8,128)(2,1)} %collective-permute-done.53.refs_10_.refs_26_), channel_id=1, source_target_pairs={{0,4},{1,5},{2,6},{3,7},{4,0},{5,1},{6,2},{7,3},{8,12},{9,13},{10,... | collective-permute-start | bytes 2359304 | tf_op jit(solution)/shard_map/ppermute | solution.py:501
  508.5 19.3 %collective-permute-start.52 = (bf16[128,3072]{1,0:T(8,128)(2,1)}, bf16[128,3072]{1,0:T(8,128)(2,1)S(1)}, u32[]{:S(2)}, u32[]{:S(2)}) collective-permute-start(bf16[128,3072]{1,0:T(8,128)(2,1)} %get-tuple-element.78.refs_8_.refs_24_), channel_id=1, source_target_pairs={{0,1},{1,0},{2,3},{3,2},{4,5},{5,4},{6,7},{7,6},{8,9},{9,8},{10,11... | collective-permute-start | bytes 2359304 | tf_op jit(solution)/shard_map/ppermute | solution.py:501
  510.3 17.9 %collective-permute-start.45 = (bf16[128,3072]{1,0:T(8,128)(2,1)}, bf16[128,3072]{1,0:T(8,128)(2,1)S(1)}, u32[]{:S(2)}, u32[]{:S(2)}) collective-permute-start(bf16[128,3072]{1,0:T(8,128)(2,1)} %get-tuple-element.55.refs_0_.refs_16_), channel_id=1, source_target_pairs={{0,1},{1,0},{2,3},{3,2},{4,5},{5,4},{6,7},{7,6},{8,9},{9,8},{10,11... | collective-permute-start | bytes 2359304 | tf_op jit(solution)/shard_map/ppermute | solution.py:501
  510.4 17.9 %collective-permute-start.47 = (bf16[128,3072]{1,0:T(8,128)(2,1)}, bf16[128,3072]{1,0:T(8,128)(2,1)}, u32[]{:S(2)}, u32[]{:S(2)}) collective-permute-start(bf16[128,3072]{1,0:T(8,128)(2,1)} %collective-permute-done.46.refs_2_.refs_18_), channel_id=1, source_target_pairs={{0,1},{1,0},{2,3},{3,2},{4,5},{5,4},{6,7},{7,6},{8,9},{9,8},{10,11... | collective-permute-start | bytes 2359304 | tf_op jit(solution)/shard_map/ppermute | solution.py:501
  525.5 4.3 collective-permute-start.49
  527.7 4.3 collective-permute-start.56
  528.2 5.0 collective-permute-start.51
  528.3 6.2 collective-permute-start.58
  529.8 55.9 %collective-permute-start.62 = (bf16[192,3072]{1,0:T(8,128)(2,1)S(1)}, bf16[192,3072]{1,0:T(8,128)(2,1)S(1)}, u32[]{:S(2)}, u32[]{:S(2)}) collective-permute-start(bf16[192,3072]{1,0:T(8,128)(2,1)S(1)} %copy-done.9), channel_id=1, source_target_pairs={{0,2},{1,3},{2,0},{3,1},{4,6},{5,7},{6,4},{7,5},{8,10},{9,11},{10,... | collective-permute-start | bytes 3538952 | tf_op jit(solution)/shard_map/ppermute | solution.py:501
  530.9 54.8 %collective-permute-start.44 = (bf16[192,3072]{1,0:T(8,128)(2,1)S(1)}, bf16[192,3072]{1,0:T(8,128)(2,1)}, u32[]{:S(2)}, u32[]{:S(2)}) collective-permute-start(bf16[192,3072]{1,0:T(8,128)(2,1)S(1)} %copy-done.9), channel_id=1, source_target_pairs={{0,4},{1,5},{2,6},{3,7},{4,0},{5,1},{6,2},{7,3},{8,12},{9,13},{10,... | collective-permute-start | bytes 3538952 | tf_op jit(solution)/shard_map/ppermute | solution.py:501
  532.1 53.6 %collective-permute-start.65 = (bf16[192,3072]{1,0:T(8,128)(2,1)S(1)}, bf16[192,3072]{1,0:T(8,128)(2,1)}, u32[]{:S(2)}, u32[]{:S(2)}) collective-permute-start(bf16[192,3072]{1,0:T(8,128)(2,1)S(1)} %copy-done.10), channel_id=1, source_target_pairs={{0,4},{1,5},{2,6},{3,7},{4,0},{5,1},{6,2},{7,3},{8,12},{9,13},{10,... | collective-permute-start | bytes 3538952 | tf_op jit(solution)/shard_map/ppermute | solution.py:501
  533.2 52.5 %collective-permute-start.60 = (bf16[192,3072]{1,0:T(8,128)(2,1)S(1)}, bf16[192,3072]{1,0:T(8,128)(2,1)}, u32[]{:S(2)}, u32[]{:S(2)}) collective-permute-start(bf16[192,3072]{1,0:T(8,128)(2,1)S(1)} %copy-done.10), channel_id=1, source_target_pairs={{0,2},{1,3},{2,0},{3,1},{4,6},{5,7},{6,4},{7,5},{8,10},{9,11},{10,... | collective-permute-start | bytes 3538952 | tf_op jit(solution)/shard_map/ppermute | solution.py:501
  586.2 4.4 collective-permute-start.64
  586.3 5.9 collective-permute-start.63
  586.7 7.4 %collective-permute-start.67 = (bf16[192,3072]{1,0:T(8,128)(2,1)}, bf16[192,3072]{1,0:T(8,128)(2,1)}, u32[]{:S(2)}, u32[]{:S(2)}) collective-permute-start(bf16[192,3072]{1,0:T(8,128)(2,1)} %collective-permute-done.65.refs_5_.refs_9_), channel_id=1, source_target_pairs={{0,1},{1,0},{2,3},{3,2},{4,5},{5,4},{6,7},{7,6},{8,9},{9,8},{10,11... | collective-permute-start | bytes 3538952 | tf_op jit(solution)/shard_map/ppermute | solution.py:501
  586.8 46.7 %collective-permute-start.59 = (bf16[192,3072]{1,0:T(8,128)(2,1)}, bf16[192,3072]{1,0:T(8,128)(2,1)S(1)}, u32[]{:S(2)}, u32[]{:S(2)}) collective-permute-start(bf16[192,3072]{1,0:T(8,128)(2,1)} %collective-permute-done.44.refs_4_.refs_8_), channel_id=1, source_target_pairs={{0,2},{1,3},{2,0},{3,1},{4,6},{5,7},{6,4},{7,5},{8,10},{9,11},{10,... | collective-permute-start | bytes 3538952 | tf_op jit(solution)/shard_map/ppermute | solution.py:501
  589.0 44.5 %collective-permute-start.61 = (bf16[192,3072]{1,0:T(8,128)(2,1)}, bf16[192,3072]{1,0:T(8,128)(2,1)S(1)}, u32[]{:S(2)}, u32[]{:S(2)}) collective-permute-start(bf16[192,3072]{1,0:T(8,128)(2,1)} %collective-permute-done.60.refs_1_.refs_5_), channel_id=1, source_target_pairs={{0,4},{1,5},{2,6},{3,7},{4,0},{5,1},{6,2},{7,3},{8,12},{9,13},{10,... | collective-permute-start | bytes 3538952 | tf_op jit(solution)/shard_map/ppermute | solution.py:501
  633.9 4.3 collective-permute-start.69
  (42 other events, 984.4 us)

commit v5 on v4

--- a/solution.py
+++ b/solution.py
@@ -357,7 +357,7 @@
 def wgrad_kernel(by_rows, spots, unit, n_out, n_big, half_steps, me_ref, *refs):
     n_part = len(spots)
     parts, bigs = refs[:n_part], refs[n_part:n_part + n_big]
-    first_scratch = len(refs) - (4 if n_big == 1 else 6)
+    first_scratch = len(refs) - 6
     scratch, out_refs = refs[first_scratch:], refs[first_scratch - n_out:first_scratch]
     cat, acc, part_sems, out_sems = scratch[:4]
     step, n_steps = pl.program_id(0), pl.num_programs(0)
@@ -387,61 +387,69 @@
             row += part.shape[0]
         return out
 
+    big_scr, big_sems = scratch[4:]
+    n_dev = max(1, n_big // 2)
+
+    def big_copies(ins, at_step, at_slot):
+        if n_big == 1:
+            deep = pl.ds(pl.multiple_of(at_step * blk, blk), blk)
+            return [pltpu.make_async_copy(bigs[0].at[deep, :], big_scr.at[at_slot], big_sems.at[at_slot, 0])]
+        tokens = bigs[0].shape[0]
+        wide = pl.ds(pl.multiple_of(lax.rem(at_step, half_steps) * blk, blk), blk)
+        out = []
+        for rel, ref in enumerate(ins):
+            place = pl.ds(pl.multiple_of((me_ref[0] ^ rel) * tokens, tokens), tokens)
+            out.append(pltpu.make_async_copy(ref.at[:, wide], big_scr.at[at_slot, place, :], big_sems.at[at_slot, rel]))
+        return out
+
+    def fetch(at_step, at_slot):
+        @pl.when(at_step < half_steps)
+        def _():
+            for copy in big_copies(bigs[:n_dev], at_step, at_slot):
+                copy.start()
+
+        @pl.when(at_step >= half_steps)
+        def _():
+            for copy in big_copies(bigs[-n_dev:], at_step, at_slot):
+                copy.start()
+
     @pl.when(step == 0)
     def _():
+        fetch(step, slot)
         for copy in part_copies():
             copy.start()
 
-    if n_big > 1:
-        big_scr, big_sems = scratch[4:]
-        n_dev = n_big // 2
-        tokens = bigs[0].shape[0]
-
-        def big_copies(ins, at_step, at_slot):
-            wide = pl.ds(pl.multiple_of(lax.rem(at_step, half_steps) * blk, blk), blk)
-            out = []
-            for rel, ref in enumerate(ins):
-                place = pl.ds(pl.multiple_of((me_ref[0] ^ rel) * tokens, tokens), tokens)
-                out.append(pltpu.make_async_copy(ref.at[:, wide], big_scr.at[at_slot, place, :], big_sems.at[at_slot, rel]))
-            return out
-
-        def fetch(at_step, at_slot):
-            @pl.when(at_step < half_steps)
-            def _():
-                for copy in big_copies(bigs[:n_dev], at_step, at_slot):
-                    copy.start()
-
-            @pl.when(at_step >= half_steps)
-            def _():
-                for copy in big_copies(bigs[n_dev:], at_step, at_slot):
-                    copy.start()
-
-        @pl.when(step == 0)
-        def _():
-            fetch(step, slot)
-
-        @pl.when(step + 1 < n_steps)
-        def _():
-            fetch(step + 1, 1 - slot)
-
-    @pl.when(step == 0)
-    def _():
-        for copy in part_copies():
-            copy.wait()
-
-    if n_big > 1:
-        for copy in big_copies(bigs[:n_dev], step, slot):
-            copy.wait()
-        big = big_scr[slot]
-    else:
-        big = bigs[0][...]
+    @pl.when(step + 1 < n_steps)
+    def _():
+        fetch(step + 1, 1 - slot)
+
+    for copy in big_copies(bigs[:n_dev], step, slot):
+        copy.wait()
 
     @pl.when(step >= 2)
     def _():
         for copy in out_copies(step - 2, slot):
             copy.wait()
 
-    acc[slot] = dot_nn(cat[...], big) if by_rows else dot_nt(big, cat[...])
+    limit = 384 if by_rows else 768
+    at, row = 0, 0
+    while at < n_part:
+        until, height = at, 0
+        while until < n_part and height + parts[until].shape[0] <= limit:
+            height += parts[until].shape[0]
+            until += 1
+
+        @pl.when(step == 0)
+        def _(at=at, until=until):
+            for copy in part_copies()[at:until]:
+                copy.wait()
+
+        if by_rows:
+            acc[slot, row:row + height, :] = dot_nn(cat[row:row + height, :], big_scr[slot])
+        else:
+            acc[slot, :, row:row + height] = dot_nt(big_scr[slot], cat[row:row + height, :])
+        at, row = until, row + height
+
     for copy in out_copies(step, slot):
         copy.start()
 
@@ -462,7 +470,7 @@
     width = bigs[0].shape[0] if n_big == 1 else 2 * bigs[0].shape[1]
     cols = unit * n_dev
     shape = (cols, width) if by_rows else (width, cols)
-    big_specs = [pl.BlockSpec((blk, seq), lambda i, me: (i, 0))] if n_big == 1 else [any_spec] * n_big
+    big_specs = [any_spec] * n_big
     prev = [] if prev is None else list(prev)
     scratch = [
         pltpu.VMEM((rows, seq), BF16),
@@ -470,8 +478,7 @@
         pltpu.SemaphoreType.DMA((len(parts),)),
         pltpu.SemaphoreType.DMA((2, len(parts))),
     ]
-    if n_big > 1:
-        scratch += [pltpu.VMEM((2, seq, blk), BF16), pltpu.SemaphoreType.DMA((2, n_dev))]
+    scratch += [pltpu.VMEM((2, seq, blk) if by_rows else (2, blk, seq), BF16), pltpu.SemaphoreType.DMA((2, n_dev))]
     body = functools.partial(wgrad_kernel, by_rows, spots, unit, n_out, n_big, width // blk // 2)
     n_lead = 1 + len(parts) + n_big
 

time: 687 us -> 701 us (1.020)
  Pallas kernels: 385 us -> 395 us
    pallas_call x8, Pallas kernels: 224 us -> 234 us  [weight_grad(): pl.pallas_call(body, grid_spec=pltpu.PrefetchScalarGridSpec(num_scalar_pr...]
  transfers between devices with their start and end apart: 71 -> 71, of which waited for: 34 -> 35; matrix products, arithmetic and copies ran while one was open for 2% -> 2% of each run, Pallas kernels for 45% -> 45%
where the time goes in v5:
time: 701 us; the launch traced here: 696 us
  Pallas kernels  395 us (56%)
  waiting for transfers between devices  215 us (31%)
  starting transfers between devices  51 us (7%)
  other arithmetic  12.1 us (2%)
  blocking collectives  11.4 us (2%)
  local copies, waits for them, and re-layouts  10.8 us (2%)
    pallas_call x8, Pallas kernels, weight_grad(): pl.pallas_call(body, grid_spec=pltpu.PrefetchScalarGridSpec(num_scalar_pr...  234 us
    ppermute x70, waiting for transfers between devices, swap(): return lax.ppermute(values, 'sp', [(i, i ^ bit) for i in range(n_dev)])  215 us
    pallas_call x1, Pallas kernels, attention(): pl.pallas_call(functools.partial(attn_kernel, group), grid_spec=grid_spec...  67.6 us
    ppermute x70, starting transfers between devices, swap(): return lax.ppermute(values, 'sp', [(i, i ^ bit) for i in range(n_dev)])  45.6 us
    pallas_call x1, Pallas kernels, project(): pl.pallas_call(functools.partial(proj_kernel, group), grid=(n_dev,), in_s...  36.9 us
    pallas_call x2, Pallas kernels, own_product(): pl.pallas_call(functools.partial(own_kernel, kinds, turned), grid_spec=pl...  35.2 us
    pallas_call x2, Pallas kernels, assemble(): pl.pallas_call(body, grid_spec=pltpu.PrefetchScalarGridSpec(num_scalar_pr...  21.4 us
  transfers between devices with their start and end apart: 71, of which 35 were waited for; matrix products, arithmetic and copies ran while one was open for 2% of the time, Pallas kernels for 45%

profile of v5, /device:TPU:1, one launch (start us, length us, event | category | flops | bytes accessed | tf_op | source)
XLA Modules:
  0.0 696.1 jit_solution(1399941165012190216)
XLA Ops:
  2.7 11.4 %all-gather.1 = s32[8,2,384]{2,1,0:T(2,128)} all-gather(s32[1,2,384]{2,1,0:T(2,128)S(1)} %add_bitcast_fusion), channel_id=2, replica_groups=mesh['dp'=2,'sp'=8] {'sp'}, dimensions={0}, use_global_device_ids=true | all-gather | bytes 27648 | tf_op jit(solution)/shard_map/all_gather | solution.py:542
  15.8 36.9 %project.1 = bf16[8,384,1024]{2,1,0:T(8,128)(2,1)} custom-call(bf16[384,3072]{1,0:T(8,128)(2,1)} %x_ref, bf16[384,3072]{1,0:T(8,128)(2,1)} %g_ref, bf16[3072,3072]{1,0:T(8,128)(2,1)} %refs_32_.1, bf16[3072,1024]{1,0:T(8,128)(2,1)} %refs_33_.1, bf16[3072,1024]{1,0:T(8,128)(2,1)} %refs_34_.1, bf16[3072,3072]{1,0:T(8,128)(2,1)} %refs_16_.1, ...), custom_call_target="tpu_custom_call" | custom-call | flops 19327352832 | bytes 60000000 | tf_op jit(solution)/shard_map/project/pallas_call | solution.py:64
  52.7 5.4 all-to-all-start
  58.1 1.8 fusion.2
  59.9 1.4 collective-permute-start.6
  61.3 1.2 collective-permute-start.3
  62.8 1.2 collective-permute-start.13
  64.1 89.2 %collective-permute-done.6.refs_8_ = bf16[384,1536]{1,0:T(8,128)(2,1)} collective-permute-done((bf16[384,1536]{1,0:T(8,128)(2,1)S(1)}, bf16[384,1536]{1,0:T(8,128)(2,1)}, u32[]{:S(2)}, u32[]{:S(2)}) %collective-permute-start.6) | collective-permute-done | bytes 1179680 | tf_op jit(solution)/shard_map/ppermute | solution.py:508
  153.2 1.2 collective-permute-start.7
  154.8 4.6 convert_reduce_fusion
  159.4 1.3 slice.22
  160.7 1.3 and_select_fusion.lo_ref
  161.9 3.8 multiply_sine_fusion
  165.8 12.6 %collective-permute-done.15.refs_10_ = bf16[384,1536]{1,0:T(8,128)(2,1)S(1)} collective-permute-done((bf16[384,1536]{1,0:T(8,128)(2,1)S(1)}, bf16[384,1536]{1,0:T(8,128)(2,1)S(1)}, u32[]{:S(2)}, u32[]{:S(2)}) %collective-permute-start.15) | collective-permute-done | bytes 1179680 | tf_op jit(solution)/shard_map/ppermute | solution.py:508
  178.4 1.5 collective-permute-start.9
  180.4 23.3 %collective-permute-done.7.refs_2_ = bf16[384,1536]{1,0:T(8,128)(2,1)} collective-permute-done((bf16[384,1536]{1,0:T(8,128)(2,1)}, bf16[384,1536]{1,0:T(8,128)(2,1)}, u32[]{:S(2)}, u32[]{:S(2)}) %collective-permute-start.7) | collective-permute-done | bytes 1179680 | tf_op jit(solution)/shard_map/ppermute | solution.py:508
  204.7 67.6 %attention.1 = (bf16[192,3072]{1,0:T(8,128)(2,1)}, bf16[192,3072]{1,0:T(8,128)(2,1)}, bf16[192,3072]{1,0:T(8,128)(2,1)}, bf16[192,3072]{1,0:T(8,128)(2,1)}, bf16...) custom-call(s32[12]{0:T(128)} %and_select_fusion.lo_ref, bf16[3072,1024]{1,0:T(8,128)(2,1)} %bitcast.3.q_ref.do_ref.k_ref.v_ref, ...), custom_call_target="tpu_custom_call" | custom-call | flops 72477573120 | bytes 12000000 | tf_op jit(solution)/shard_map/attention/pallas_call | solution.py:229
  273.2 1.2 collective-permute-start.27
  274.7 1.2 collective-permute-start.29
  275.9 14.3 %shard_map.127.refs_4_ = bf16[3072,3072]{1,0:T(8,128)(2,1)} custom-call(s32[1]{0:T(128)} %bitcast.me_ref, bf16[384,1536]{1,0:T(8,128)(2,1)} %copy-done.8, bf16[384,1536]{1,0:T(8,128)(2,1)} %collective-permute-done.9.refs_1_, bf16[384,1536]{1,0:T(8,128)(2,1)} %collective-permute-done.10.refs_2_, bf16[384,1536]{1,0:T(8,128)(2,1)} %collective-permute-done.11.refs_3_, ...), custom_call_target="tpu_custom_call" | custom-call | bytes 28311552 | tf_op jit(solution)/shard_map/pallas_call | solution.py:290
  290.5 1.6 collective-permute-start.1
  292.1 7.0 %shard_map.128.refs_4_.refs_16_.refs_8_ = bf16[3072,3072]{1,0:T(8,128)(2,1)} custom-call(s32[1]{0:T(128)} %bitcast.me_ref, bf16[384,1536]{1,0:T(8,128)(2,1)} %collective-permute-done.4.refs_0_, bf16[384,1536]{1,0:T(8,128)(2,1)} %collective-permute-done.5.refs_1_, bf16[384,1536]{1,0:T(8,128)(2,1)} %collective-permute-done.7.refs_2_, ...), custom_call_target="tpu_custom_call", output_to_operand_aliasing={{}: (5, {})} | custom-call | bytes 9437184 | tf_op jit(solution)/shard_map/pallas_call | solution.py:290
  299.2 1.3 collective-permute-done.27.refs_14_
  300.4 2.1 collective-permute-start.2
  302.5 1.2 collective-permute-start.24
  303.7 22.9 %collective-permute-done.29.refs_16_ = bf16[384,1536]{1,0:T(8,128)(2,1)} collective-permute-done((bf16[384,1536]{1,0:T(8,128)(2,1)S(1)}, bf16[384,1536]{1,0:T(8,128)(2,1)}, u32[]{:S(2)}, u32[]{:S(2)}) %collective-permute-start.29) | collective-permute-done | bytes 1179680 | tf_op jit(solution)/shard_map/ppermute | solution.py:508
  327.1 1.7 collective-permute-start.26
  329.3 21.6 %collective-permute-done.24.refs_10_ = bf16[384,1536]{1,0:T(8,128)(2,1)S(1)} collective-permute-done((bf16[384,1536]{1,0:T(8,128)(2,1)}, bf16[384,1536]{1,0:T(8,128)(2,1)S(1)}, u32[]{:S(2)}, u32[]{:S(2)}) %collective-permute-start.24) | collective-permute-done | bytes 1179680 | tf_op jit(solution)/shard_map/ppermute | solution.py:508
  350.9 1.3 collective-permute-start.18
  353.6 2.4 collective-permute-start.21
  356.0 21.5 %shard_map.129.refs_9_ = f32[3072,3072]{1,0:T(8,128)} custom-call(s32[1]{0:T(128)} %bitcast.me_ref, bf16[192,3072]{1,0:T(8,128)(2,1)} %get-tuple-element.53.refs_0_, bf16[192,3072]{1,0:T(8,128)(2,1)} %get-tuple-element.54.refs_1_, bf16[192,3072]{1,0:T(8,128)(2,1)} %collective-permute-done.1.refs_2_, bf16[192,3072]{1,0:T(8,128)(2,1)} %copy-done.11, ...), custom_call_target="tpu_custom_call" | custom-call | flops 14495514624 | bytes 33030144 | tf_op jit(solution)/shard_map/pallas_call | solution.py:485
  378.6 2.0 collective-permute-done.23.refs_9_
  381.0 1.2 collective-permute-done.28.refs_15_
  382.7 1.4 collective-permute-done.30.refs_17_
  384.1 1.7 collective-permute-done.25.refs_11_
  385.8 1.7 collective-permute-done.32.refs_19_
  387.5 21.1 %shard_map.130.refs_20_ = f32[3072,3072]{1,0:T(8,128)} custom-call(s32[1]{0:T(128)} %bitcast.me_ref, bf16[192,3072]{1,0:T(8,128)(2,1)} %get-tuple-element.52.refs_0_, bf16[192,3072]{1,0:T(8,128)(2,1)} %get-tuple-element.60.refs_1_, bf16[192,3072]{1,0:T(8,128)(2,1)} %collective-permute-done.17.refs_2_, bf16[192,3072]{1,0:T(8,128)(2,1)} %collective-permute-done.18.refs_3_, ...), custom_call_target="tpu_custom_call" | custom-call | flops 14495514624 | bytes 33030144 | tf_op jit(solution)/shard_map/pallas_call | solution.py:485
  408.6 1.4 collective-permute-done.refs_2_.refs_8_
  411.5 1.5 collective-permute-start.34
  413.7 1.7 collective-permute-done.36.refs_1_.refs_6_
  416.4 20.9 %shard_map.131.refs_20_ = f32[3072,3072]{1,0:T(8,128)} custom-call(s32[1]{0:T(128)} %bitcast.me_ref, bf16[192,3072]{1,0:T(8,128)(2,1)} %collective-permute-done.35.refs_0_.refs_4_, bf16[192,3072]{1,0:T(8,128)(2,1)} %copy-done.14, bf16[192,3072]{1,0:T(8,128)(2,1)} %collective-permute-done.refs_2_.refs_8_, ...), custom_call_target="tpu_custom_call", output_to_operand_aliasing={{}: (21, {})} | custom-call | flops 14495514624 | bytes 33030144 | tf_op jit(solution)/shard_map/pallas_call | solution.py:485
  438.3 1.6 collective-permute-start.39
  439.9 1.5 collective-permute-start.33
  441.4 1.2 collective-permute-done.39.refs_1_.refs_7_
  442.6 1.7 collective-permute-done.41.refs_3_.refs_11_
  445.3 20.9 %shard_map.132.refs_20_ = f32[3072,3072]{1,0:T(8,128)} custom-call(s32[1]{0:T(128)} %bitcast.me_ref, bf16[192,3072]{1,0:T(8,128)(2,1)} %collective-permute-done.34.refs_0_.refs_5_, bf16[192,3072]{1,0:T(8,128)(2,1)} %copy-done.15, bf16[192,3072]{1,0:T(8,128)(2,1)} %collective-permute-done.40.refs_2_.refs_9_, ...), custom_call_target="tpu_custom_call", output_to_operand_aliasing={{}: (21, {})} | custom-call | flops 14495514624 | bytes 33030144 | tf_op jit(solution)/shard_map/pallas_call | solution.py:485
  466.3 2.2 collective-permute-done.38.refs_1_.refs_13_
  468.5 1.6 collective-permute-start.42
  473.1 1.2 collective-permute-done.43.refs_3_.refs_15_
  475.3 20.9 %shard_map.133 = f32[3072,3072]{1,0:T(8,128)} custom-call(s32[1]{0:T(128)} %bitcast.me_ref, bf16[192,3072]{1,0:T(8,128)(2,1)} %copy-done.17, bf16[192,3072]{1,0:T(8,128)(2,1)} %collective-permute-done.38.refs_1_.refs_13_, bf16[192,3072]{1,0:T(8,128)(2,1)} %copy-done.18, bf16[192,3072]{1,0:T(8,128)(2,1)} %copy-done.19, ...), custom_call_target="tpu_custom_call", output_to_operand_aliasing={{}: (21, {})} | custom-call | flops 14495514624 | bytes 33030144 | tf_op jit(solution)/shard_map/pallas_call | solution.py:485
  496.3 9.7 %collective-permute-done.48.refs_4_.refs_20_ = bf16[128,3072]{1,0:T(8,128)(2,1)} collective-permute-done((bf16[128,3072]{1,0:T(8,128)(2,1)}, bf16[128,3072]{1,0:T(8,128)(2,1)}, u32[]{:S(2)}, u32[]{:S(2)}) %collective-permute-start.48) | collective-permute-done | bytes 786464 | tf_op jit(solution)/shard_map/ppermute | solution.py:508
  507.0 1.9 collective-permute-start.52
  509.4 14.0 %shard_map.134 = bf16[384,3072]{1,0:T(8,128)(2,1)} custom-call(s32[1]{0:T(128)} %bitcast.me_ref, bf16[192,3072]{1,0:T(8,128)(2,1)} %get-tuple-element.52.refs_0_, bf16[192,3072]{1,0:T(8,128)(2,1)} %get-tuple-element.60.refs_1_, bf16[192,3072]{1,0:T(8,128)(2,1)} %collective-permute-done.17.refs_2_, bf16[192,3072]{1,0:T(8,128)(2,1)} %collective-permute-done.18.refs_3_, ...), custom_call_target="tpu_custom_call" | custom-call | flops 7247757312 | bytes 21233664 | tf_op jit(solution)/shard_map/pallas_call | solution.py:342
  524.0 2.2 collective-permute-start.49
  529.5 1.1 collective-permute-done.56.refs_13_.refs_29_
  533.0 60.1 %shard_map.135 = (f32[3072,1024]{1,0:T(8,128)}, f32[3072,1024]{1,0:T(8,128)}) custom-call(s32[1]{0:T(128)} %bitcast.me_ref, bf16[128,3072]{1,0:T(8,128)(2,1)} %get-tuple-element.55.refs_0_.refs_16_, bf16[128,3072]{1,0:T(8,128)(2,1)} %copy-done.29, bf16[128,3072]{1,0:T(8,128)(2,1)} %collective-permute-done.46.refs_2_.refs_18_, ...), custom_call_target="tpu_custom_call" | custom-call | flops 38654705664 | bytes 56623104 | tf_op jit(solution)/shard_map/pallas_call | solution.py:485
  594.7 1.7 collective-permute-done.66.refs_6_.refs_10_
  596.7 1.3 collective-permute-done.64.refs_3_.refs_7_
  597.9 1.7 collective-permute-done.63.refs_2_.refs_6_
  601.4 46.6 %shard_map.136.refs_5_ = f32[3072,3072]{1,0:T(8,128)} custom-call(s32[1]{0:T(128)} %bitcast.me_ref, bf16[192,3072]{1,0:T(8,128)(2,1)} %copy-done.25, bf16[192,3072]{1,0:T(8,128)(2,1)} %collective-permute-done.60.refs_1_.refs_5_, bf16[192,3072]{1,0:T(8,128)(2,1)} %copy-done.27, bf16[192,3072]{1,0:T(8,128)(2,1)} %copy-done.26, ...), custom_call_target="tpu_custom_call", output_to_operand_aliasing={{}: (10, {})} | custom-call | flops 28991029248 | bytes 47185920 | tf_op jit(solution)/shard_map/pallas_call | solution.py:485
  648.7 2.3 collective-permute-done.68.refs_2_.refs_14_
  651.0 1.8 collective-permute-done.69.refs_3_.refs_15_
  652.8 21.7 %shard_map.137 = f32[3072,3072]{1,0:T(8,128)} custom-call(s32[1]{0:T(128)} %bitcast.me_ref, bf16[192,3072]{1,0:T(8,128)(2,1)} %copy-done.20, bf16[192,3072]{1,0:T(8,128)(2,1)} %copy-done.21, bf16[192,3072]{1,0:T(8,128)(2,1)} %copy-done.22, bf16[192,3072]{1,0:T(8,128)(2,1)} %collective-permute-done.69.refs_3_.refs_15_, ...), custom_call_target="tpu_custom_call", output_to_operand_aliasing={{}: (6, {})} | custom-call | flops 14495514624 | bytes 33030144 | tf_op jit(solution)/shard_map/pallas_call | solution.py:485
  674.6 21.3 %shard_map.138 = bf16[384,3072]{1,0:T(8,128)(2,1)} custom-call(s32[1]{0:T(128)} %bitcast.me_ref, bf16[192,3072]{1,0:T(8,128)(2,1)} %get-tuple-element.53.refs_0_, bf16[192,3072]{1,0:T(8,128)(2,1)} %get-tuple-element.54.refs_1_, bf16[192,3072]{1,0:T(8,128)(2,1)} %collective-permute-done.1.refs_2_, bf16[192,3072]{1,0:T(8,128)(2,1)} %copy-done.11, ...), custom_call_target="tpu_custom_call" | custom-call | flops 12079595520 | bytes 35389440 | tf_op jit(solution)/shard_map/pallas_call | solution.py:342
  (177 shorter events, 33.2 us)
Async XLA Ops:
  52.7 152.0 %all-to-all-start = ((bf16[8,384,1024]{2,1,0:T(8,128)(2,1)}), bf16[8,384,1024]{2,1,0:T(8,128)(2,1)}, u32[]{:S(2)}, u32[]{:S(2)}) async-start(bf16[8,384,1024]{2,1,0:T(8,128)(2,1)} %project.1), calls=%async_computation | async-start | bytes 12582912 | tf_op jit(solution)/shard_map/all_to_all | solution.py:570
  59.9 93.3 %collective-permute-start.6 = (bf16[384,1536]{1,0:T(8,128)(2,1)S(1)}, bf16[384,1536]{1,0:T(8,128)(2,1)}, u32[]{:S(2)}, u32[]{:S(2)}) collective-permute-start(bf16[384,1536]{1,0:T(8,128)(2,1)S(1)} %get-tuple-element.94.refs_6_), channel_id=1, source_target_pairs={{0,2},{1,3},{2,0},{3,1},{4,6},{5,7},{6,4},{7,5},{8,10},{9,11},{10,... | collective-permute-start | bytes 3538952 | tf_op jit(solution)/shard_map/ppermute | solution.py:508
  61.3 93.1 %collective-permute-start.3 = (bf16[384,1536]{1,0:T(8,128)(2,1)S(1)}, bf16[384,1536]{1,0:T(8,128)(2,1)}, u32[]{:S(2)}, u32[]{:S(2)}) collective-permute-start(bf16[384,1536]{1,0:T(8,128)(2,1)S(1)} %get-tuple-element.95.refs_0_), channel_id=1, source_target_pairs={{0,4},{1,5},{2,6},{3,7},{4,0},{5,1},{6,2},{7,3},{8,12},{9,13},{10,... | collective-permute-start | bytes 3538952 | tf_op jit(solution)/shard_map/ppermute | solution.py:508
  62.5 115.8 %collective-permute-start.15 = (bf16[384,1536]{1,0:T(8,128)(2,1)S(1)}, bf16[384,1536]{1,0:T(8,128)(2,1)S(1)}, u32[]{:S(2)}, u32[]{:S(2)}) collective-permute-start(bf16[384,1536]{1,0:T(8,128)(2,1)S(1)} %get-tuple-element.94.refs_6_), channel_id=1, source_target_pairs={{0,4},{1,5},{2,6},{3,7},{4,0},{5,1},{6,2},{7,3},{8,12},{9,13},{10,... | collective-permute-start | bytes 3538952 | tf_op jit(solution)/shard_map/ppermute | solution.py:508
  62.8 117.0 %collective-permute-start.13 = (bf16[384,1536]{1,0:T(8,128)(2,1)S(1)}, bf16[384,1536]{1,0:T(8,128)(2,1)}, u32[]{:S(2)}, u32[]{:S(2)}) collective-permute-start(bf16[384,1536]{1,0:T(8,128)(2,1)S(1)} %get-tuple-element.94.refs_6_), channel_id=1, source_target_pairs={{0,1},{1,0},{2,3},{3,2},{4,5},{5,4},{6,7},{7,6},{8,9},{9,8},{10,11... | collective-permute-start | bytes 3538952 | tf_op jit(solution)/shard_map/ppermute | solution.py:508
  64.0 115.9 %collective-permute-start.10 = (bf16[384,1536]{1,0:T(8,128)(2,1)S(1)}, bf16[384,1536]{1,0:T(8,128)(2,1)}, u32[]{:S(2)}, u32[]{:S(2)}) collective-permute-start(bf16[384,1536]{1,0:T(8,128)(2,1)S(1)} %get-tuple-element.95.refs_0_), channel_id=1, source_target_pairs={{0,2},{1,3},{2,0},{3,1},{4,6},{5,7},{6,4},{7,5},{8,10},{9,11},{10,... | collective-permute-start | bytes 3538952 | tf_op jit(solution)/shard_map/ppermute | solution.py:508
  153.2 50.4 %collective-permute-start.7 = (bf16[384,1536]{1,0:T(8,128)(2,1)}, bf16[384,1536]{1,0:T(8,128)(2,1)}, u32[]{:S(2)}, u32[]{:S(2)}) collective-permute-start(bf16[384,1536]{1,0:T(8,128)(2,1)} %collective-permute-done.6.refs_8_), channel_id=1, source_target_pairs={{0,4},{1,5},{2,6},{3,7},{4,0},{5,1},{6,2},{7,3},{8,12},{9,13},{10,... | collective-permute-start | bytes 3538952 | tf_op jit(solution)/shard_map/ppermute | solution.py:508
  154.4 50.2 %collective-permute-start.4 = (bf16[384,1536]{1,0:T(8,128)(2,1)}, bf16[384,1536]{1,0:T(8,128)(2,1)}, u32[]{:S(2)}, u32[]{:S(2)}) collective-permute-start(bf16[384,1536]{1,0:T(8,128)(2,1)} %collective-permute-done.3.refs_4_), channel_id=1, source_target_pairs={{0,2},{1,3},{2,0},{3,1},{4,6},{5,7},{6,4},{7,5},{8,10},{9,11},{10,... | collective-permute-start | bytes 3538952 | tf_op jit(solution)/shard_map/ppermute | solution.py:508
  178.4 94.1 %collective-permute-start.9 = (bf16[384,1536]{1,0:T(8,128)(2,1)S(1)}, bf16[384,1536]{1,0:T(8,128)(2,1)}, u32[]{:S(2)}, u32[]{:S(2)}) collective-permute-start(bf16[384,1536]{1,0:T(8,128)(2,1)S(1)} %get-tuple-element.95.refs_0_), channel_id=1, source_target_pairs={{0,1},{1,0},{2,3},{3,2},{4,5},{5,4},{6,7},{7,6},{8,9},{9,8},{10,11... | collective-permute-start | bytes 3538952 | tf_op jit(solution)/shard_map/ppermute | solution.py:508
  179.9 93.3 %collective-permute-start.14 = (bf16[384,1536]{1,0:T(8,128)(2,1)}, bf16[384,1536]{1,0:T(8,128)(2,1)}, u32[]{:S(2)}, u32[]{:S(2)}) collective-permute-start(bf16[384,1536]{1,0:T(8,128)(2,1)} %collective-permute-done.6.refs_8_), channel_id=1, source_target_pairs={{0,1},{1,0},{2,3},{3,2},{4,5},{5,4},{6,7},{7,6},{8,9},{9,8},{10,11... | collective-permute-start | bytes 3538952 | tf_op jit(solution)/shard_map/ppermute | solution.py:508
  179.9 94.8 %collective-permute-start.12 = (bf16[384,1536]{1,0:T(8,128)(2,1)}, bf16[384,1536]{1,0:T(8,128)(2,1)}, u32[]{:S(2)}, u32[]{:S(2)}) collective-permute-start(bf16[384,1536]{1,0:T(8,128)(2,1)} %collective-permute-done.3.refs_4_), channel_id=1, source_target_pairs={{0,1},{1,0},{2,3},{3,2},{4,5},{5,4},{6,7},{7,6},{8,9},{9,8},{10,11... | collective-permute-start | bytes 3538952 | tf_op jit(solution)/shard_map/ppermute | solution.py:508
  203.6 69.3 %collective-permute-start.16 = (bf16[384,1536]{1,0:T(8,128)(2,1)S(1)}, bf16[384,1536]{1,0:T(8,128)(2,1)}, u32[]{:S(2)}, u32[]{:S(2)}) collective-permute-start(bf16[384,1536]{1,0:T(8,128)(2,1)S(1)} %collective-permute-done.15.refs_10_), channel_id=1, source_target_pairs={{0,1},{1,0},{2,3},{3,2},{4,5},{5,4},{6,7},{7,6},{8,9},{9,8},{10,11... | collective-permute-start | bytes 3538952 | tf_op jit(solution)/shard_map/ppermute | solution.py:508
  204.6 69.8 %collective-permute-start.11 = (bf16[384,1536]{1,0:T(8,128)(2,1)}, bf16[384,1536]{1,0:T(8,128)(2,1)}, u32[]{:S(2)}, u32[]{:S(2)}) collective-permute-start(bf16[384,1536]{1,0:T(8,128)(2,1)} %collective-permute-done.10.refs_2_), channel_id=1, source_target_pairs={{0,1},{1,0},{2,3},{3,2},{4,5},{5,4},{6,7},{7,6},{8,9},{9,8},{10,11... | collective-permute-start | bytes 3538952 | tf_op jit(solution)/shard_map/ppermute | solution.py:508
  272.4 17.8 %collective-permute-start.5 = (bf16[384,1536]{1,0:T(8,128)(2,1)}, bf16[384,1536]{1,0:T(8,128)(2,1)}, u32[]{:S(2)}, u32[]{:S(2)}) collective-permute-start(bf16[384,1536]{1,0:T(8,128)(2,1)} %collective-permute-done.4.refs_0_), channel_id=1, source_target_pairs={{0,1},{1,0},{2,3},{3,2},{4,5},{5,4},{6,7},{7,6},{8,9},{9,8},{10,11... | collective-permute-start | bytes 3538952 | tf_op jit(solution)/shard_map/ppermute | solution.py:508
  272.9 17.6 %collective-permute-start.8 = (bf16[384,1536]{1,0:T(8,128)(2,1)}, bf16[384,1536]{1,0:T(8,128)(2,1)}, u32[]{:S(2)}, u32[]{:S(2)}) collective-permute-start(bf16[384,1536]{1,0:T(8,128)(2,1)} %collective-permute-done.7.refs_2_), channel_id=1, source_target_pairs={{0,1},{1,0},{2,3},{3,2},{4,5},{5,4},{6,7},{7,6},{8,9},{9,8},{10,11... | collective-permute-start | bytes 3538952 | tf_op jit(solution)/shard_map/ppermute | solution.py:508
  273.2 27.2 %collective-permute-start.27 = (bf16[384,1536]{1,0:T(8,128)(2,1)S(1)}, bf16[384,1536]{1,0:T(8,128)(2,1)S(1)}, u32[]{:S(2)}, u32[]{:S(2)}) collective-permute-start(bf16[384,1536]{1,0:T(8,128)(2,1)S(1)} %get-tuple-element.92.refs_12_), channel_id=1, source_target_pairs={{0,2},{1,3},{2,0},{3,1},{4,6},{5,7},{6,4},{7,5},{8,10},{9,11},{10,... | collective-permute-start | bytes 3538952 | tf_op jit(solution)/shard_map/ppermute | solution.py:508
  274.4 28.1 %collective-permute-start.22 = (bf16[384,1536]{1,0:T(8,128)(2,1)S(1)}, bf16[384,1536]{1,0:T(8,128)(2,1)}, u32[]{:S(2)}, u32[]{:S(2)}) collective-permute-start(bf16[384,1536]{1,0:T(8,128)(2,1)S(1)} %get-tuple-element.93.refs_4_), channel_id=1, source_target_pairs={{0,4},{1,5},{2,6},{3,7},{4,0},{5,1},{6,2},{7,3},{8,12},{9,13},{10,... | collective-permute-start | bytes 3538952 | tf_op jit(solution)/shard_map/ppermute | solution.py:508
  274.7 51.9 %collective-permute-start.29 = (bf16[384,1536]{1,0:T(8,128)(2,1)S(1)}, bf16[384,1536]{1,0:T(8,128)(2,1)}, u32[]{:S(2)}, u32[]{:S(2)}) collective-permute-start(bf16[384,1536]{1,0:T(8,128)(2,1)S(1)} %get-tuple-element.92.refs_12_), channel_id=1, source_target_pairs={{0,4},{1,5},{2,6},{3,7},{4,0},{5,1},{6,2},{7,3},{8,12},{9,13},{10,... | collective-permute-start | bytes 3538952 | tf_op jit(solution)/shard_map/ppermute | solution.py:508
  290.2 36.8 %collective-permute-start.20 = (bf16[384,1536]{1,0:T(8,128)(2,1)S(1)}, bf16[384,1536]{1,0:T(8,128)(2,1)}, u32[]{:S(2)}, u32[]{:S(2)}) collective-permute-start(bf16[384,1536]{1,0:T(8,128)(2,1)S(1)} %get-tuple-element.93.refs_4_), channel_id=1, source_target_pairs={{0,2},{1,3},{2,0},{3,1},{4,6},{5,7},{6,4},{7,5},{8,10},{9,11},{10,... | collective-permute-start | bytes 3538952 | tf_op jit(solution)/shard_map/ppermute | solution.py:508
  290.5 38.2 %collective-permute-start.1 = (bf16[192,3072]{1,0:T(8,128)(2,1)}, bf16[192,3072]{1,0:T(8,128)(2,1)}, u32[]{:S(2)}, u32[]{:S(2)}) collective-permute-start(bf16[192,3072]{1,0:T(8,128)(2,1)} %get-tuple-element.53.refs_0_), channel_id=1, source_target_pairs={{0,1},{1,0},{2,3},{3,2},{4,5},{5,4},{6,7},{7,6},{8,9},{9,8},{10,11... | collective-permute-start | bytes 3538952 | tf_op jit(solution)/shard_map/ppermute | solution.py:508
  300.4 28.4 %collective-permute-start.2 = (bf16[192,3072]{1,0:T(8,128)(2,1)}, bf16[192,3072]{1,0:T(8,128)(2,1)S(1)}, u32[]{:S(2)}, u32[]{:S(2)}) collective-permute-start(bf16[192,3072]{1,0:T(8,128)(2,1)} %get-tuple-element.54.refs_1_), channel_id=1, source_target_pairs={{0,1},{1,0},{2,3},{3,2},{4,5},{5,4},{6,7},{7,6},{8,9},{9,8},{10,11... | collective-permute-start | bytes 3538952 | tf_op jit(solution)/shard_map/ppermute | solution.py:508
  302.5 48.3 %collective-permute-start.24 = (bf16[384,1536]{1,0:T(8,128)(2,1)}, bf16[384,1536]{1,0:T(8,128)(2,1)S(1)}, u32[]{:S(2)}, u32[]{:S(2)}) collective-permute-start(bf16[384,1536]{1,0:T(8,128)(2,1)} %collective-permute-done.22.refs_8_), channel_id=1, source_target_pairs={{0,2},{1,3},{2,0},{3,1},{4,6},{5,7},{6,4},{7,5},{8,10},{9,11},{10,... | collective-permute-start | bytes 3538952 | tf_op jit(solution)/shard_map/ppermute | solution.py:508
  326.6 25.9 %collective-permute-start.31 = (bf16[384,1536]{1,0:T(8,128)(2,1)S(1)}, bf16[384,1536]{1,0:T(8,128)(2,1)S(1)}, u32[]{:S(2)}, u32[]{:S(2)}) collective-permute-start(bf16[384,1536]{1,0:T(8,128)(2,1)S(1)} %collective-permute-done.27.refs_14_), channel_id=1, source_target_pairs={{0,4},{1,5},{2,6},{3,7},{4,0},{5,1},{6,2},{7,3},{8,12},{9,13},{10,... | collective-permute-start | bytes 3538952 | tf_op jit(solution)/shard_map/ppermute | solution.py:508
  327.1 50.4 %collective-permute-start.26 = (bf16[384,1536]{1,0:T(8,128)(2,1)S(1)}, bf16[384,1536]{1,0:T(8,128)(2,1)}, u32[]{:S(2)}, u32[]{:S(2)}) collective-permute-start(bf16[384,1536]{1,0:T(8,128)(2,1)S(1)} %get-tuple-element.92.refs_12_), channel_id=1, source_target_pairs={{0,1},{1,0},{2,3},{3,2},{4,5},{5,4},{6,7},{7,6},{8,9},{9,8},{10,11... | collective-permute-start | bytes 3538952 | tf_op jit(solution)/shard_map/ppermute | solution.py:508
  328.7 48.8 %collective-permute-start.19 = (bf16[384,1536]{1,0:T(8,128)(2,1)S(1)}, bf16[384,1536]{1,0:T(8,128)(2,1)}, u32[]{:S(2)}, u32[]{:S(2)}) collective-permute-start(bf16[384,1536]{1,0:T(8,128)(2,1)S(1)} %get-tuple-element.93.refs_4_), channel_id=1, source_target_pairs={{0,1},{1,0},{2,3},{3,2},{4,5},{5,4},{6,7},{7,6},{8,9},{9,8},{10,11... | collective-permute-start | bytes 3538952 | tf_op jit(solution)/shard_map/ppermute | solution.py:508
  328.8 49.3 %collective-permute-start.17 = (bf16[192,3072]{1,0:T(8,128)(2,1)}, bf16[192,3072]{1,0:T(8,128)(2,1)}, u32[]{:S(2)}, u32[]{:S(2)}) collective-permute-start(bf16[192,3072]{1,0:T(8,128)(2,1)} %get-tuple-element.52.refs_0_), channel_id=1, source_target_pairs={{0,1},{1,0},{2,3},{3,2},{4,5},{5,4},{6,7},{7,6},{8,9},{9,8},{10,11... | collective-permute-start | bytes 3538952 | tf_op jit(solution)/shard_map/ppermute | solution.py:508
  350.9 27.3 %collective-permute-start.18 = (bf16[192,3072]{1,0:T(8,128)(2,1)}, bf16[192,3072]{1,0:T(8,128)(2,1)}, u32[]{:S(2)}, u32[]{:S(2)}) collective-permute-start(bf16[192,3072]{1,0:T(8,128)(2,1)} %get-tuple-element.60.refs_1_), channel_id=1, source_target_pairs={{0,1},{1,0},{2,3},{3,2},{4,5},{5,4},{6,7},{7,6},{8,9},{9,8},{10,11... | collective-permute-start | bytes 3538952 | tf_op jit(solution)/shard_map/ppermute | solution.py:508
  353.6 25.0 %collective-permute-start.21 = (bf16[384,1536]{1,0:T(8,128)(2,1)}, bf16[384,1536]{1,0:T(8,128)(2,1)}, u32[]{:S(2)}, u32[]{:S(2)}) collective-permute-start(bf16[384,1536]{1,0:T(8,128)(2,1)} %collective-permute-done.20.refs_6_), channel_id=1, source_target_pairs={{0,1},{1,0},{2,3},{3,2},{4,5},{5,4},{6,7},{7,6},{8,9},{9,8},{10,11... | collective-permute-start | bytes 3538952 | tf_op jit(solution)/shard_map/ppermute | solution.py:508
  377.6 4.7 collective-permute-start.28
  378.1 6.0 collective-permute-start.30
  378.1 7.7 %collective-permute-start.25 = (bf16[384,1536]{1,0:T(8,128)(2,1)}, bf16[384,1536]{1,0:T(8,128)(2,1)}, u32[]{:S(2)}, u32[]{:S(2)}) collective-permute-start(bf16[384,1536]{1,0:T(8,128)(2,1)} %copy-done.3), channel_id=1, source_target_pairs={{0,1},{1,0},{2,3},{3,2},{4,5},{5,4},{6,7},{7,6},{8,9},{9,8},{10,11... | collective-permute-start | bytes 3538952 | tf_op jit(solution)/shard_map/ppermute | solution.py:508
  378.6 8.9 %collective-permute-start.32 = (bf16[384,1536]{1,0:T(8,128)(2,1)}, bf16[384,1536]{1,0:T(8,128)(2,1)}, u32[]{:S(2)}, u32[]{:S(2)}) collective-permute-start(bf16[384,1536]{1,0:T(8,128)(2,1)} %copy-done.4), channel_id=1, source_target_pairs={{0,1},{1,0},{2,3},{3,2},{4,5},{5,4},{6,7},{7,6},{8,9},{9,8},{10,11... | collective-permute-start | bytes 3538952 | tf_op jit(solution)/shard_map/ppermute | solution.py:508
  380.6 28.0 %collective-permute-start.35 = (bf16[192,3072]{1,0:T(8,128)(2,1)}, bf16[192,3072]{1,0:T(8,128)(2,1)}, u32[]{:S(2)}, u32[]{:S(2)}) collective-permute-start(bf16[192,3072]{1,0:T(8,128)(2,1)} %get-tuple-element.52.refs_0_), channel_id=1, source_target_pairs={{0,2},{1,3},{2,0},{3,1},{4,6},{5,7},{6,4},{7,5},{8,10},{9,11},{10,... | collective-permute-start | bytes 3538952 | tf_op jit(solution)/shard_map/ppermute | solution.py:508
  382.3 27.7 %collective-permute-start = (bf16[192,3072]{1,0:T(8,128)(2,1)}, bf16[192,3072]{1,0:T(8,128)(2,1)}, u32[]{:S(2)}, u32[]{:S(2)}) collective-permute-start(bf16[192,3072]{1,0:T(8,128)(2,1)} %get-tuple-element.52.refs_0_), channel_id=1, source_target_pairs={{0,4},{1,5},{2,6},{3,7},{4,0},{5,1},{6,2},{7,3},{8,12},{9,13},{10,... | collective-permute-start | bytes 3538952 | tf_op jit(solution)/shard_map/ppermute | solution.py:508
  411.0 4.4 collective-permute-start.36
  411.0 27.1 %collective-permute-start.40 = (bf16[192,3072]{1,0:T(8,128)(2,1)S(1)}, bf16[192,3072]{1,0:T(8,128)(2,1)}, u32[]{:S(2)}, u32[]{:S(2)}) collective-permute-start(bf16[192,3072]{1,0:T(8,128)(2,1)S(1)} %copy-done.12), channel_id=1, source_target_pairs={{0,4},{1,5},{2,6},{3,7},{4,0},{5,1},{6,2},{7,3},{8,12},{9,13},{10,... | collective-permute-start | bytes 3538952 | tf_op jit(solution)/shard_map/ppermute | solution.py:508
  411.5 26.8 %collective-permute-start.34 = (bf16[192,3072]{1,0:T(8,128)(2,1)S(1)}, bf16[192,3072]{1,0:T(8,128)(2,1)}, u32[]{:S(2)}, u32[]{:S(2)}) collective-permute-start(bf16[192,3072]{1,0:T(8,128)(2,1)S(1)} %copy-done.12), channel_id=1, source_target_pairs={{0,2},{1,3},{2,0},{3,1},{4,6},{5,7},{6,4},{7,5},{8,10},{9,11},{10,... | collective-permute-start | bytes 3538952 | tf_op jit(solution)/shard_map/ppermute | solution.py:508
  438.3 4.3 collective-permute-start.39
  439.9 4.4 collective-permute-start.41
  439.9 28.5 %collective-permute-start.33 = (bf16[192,3072]{1,0:T(8,128)(2,1)}, bf16[192,3072]{1,0:T(8,128)(2,1)S(1)}, u32[]{:S(2)}, u32[]{:S(2)}) collective-permute-start(bf16[192,3072]{1,0:T(8,128)(2,1)} %collective-permute-done.refs_2_.refs_8_), channel_id=1, source_target_pairs={{0,2},{1,3},{2,0},{3,1},{4,6},{5,7},{6,4},{7,5},{8,10},{9,11},{10,... | collective-permute-start | bytes 3538952 | tf_op jit(solution)/shard_map/ppermute | solution.py:508
  441.4 27.1 %collective-permute-start.38 = (bf16[192,3072]{1,0:T(8,128)(2,1)}, bf16[192,3072]{1,0:T(8,128)(2,1)}, u32[]{:S(2)}, u32[]{:S(2)}) collective-permute-start(bf16[192,3072]{1,0:T(8,128)(2,1)} %collective-permute-done.34.refs_0_.refs_5_), channel_id=1, source_target_pairs={{0,4},{1,5},{2,6},{3,7},{4,0},{5,1},{6,2},{7,3},{8,12},{9,13},{10,... | collective-permute-start | bytes 3538952 | tf_op jit(solution)/shard_map/ppermute | solution.py:508
  470.1 38.7 %collective-permute-start.55 = (bf16[128,3072]{1,0:T(8,128)(2,1)}, bf16[128,3072]{1,0:T(8,128)(2,1)}, u32[]{:S(2)}, u32[]{:S(2)}) collective-permute-start(bf16[128,3072]{1,0:T(8,128)(2,1)} %get-tuple-element.78.refs_8_.refs_24_), channel_id=1, source_target_pairs={{0,4},{1,5},{2,6},{3,7},{4,0},{5,1},{6,2},{7,3},{8,12},{9,13},{10,... | collective-permute-start | bytes 2359304 | tf_op jit(solution)/shard_map/ppermute | solution.py:508
  470.2 35.8 %collective-permute-start.53 = (bf16[128,3072]{1,0:T(8,128)(2,1)}, bf16[128,3072]{1,0:T(8,128)(2,1)}, u32[]{:S(2)}, u32[]{:S(2)}) collective-permute-start(bf16[128,3072]{1,0:T(8,128)(2,1)} %get-tuple-element.78.refs_8_.refs_24_), channel_id=1, source_target_pairs={{0,2},{1,3},{2,0},{3,1},{4,6},{5,7},{6,4},{7,5},{8,10},{9,11},{10,... | collective-permute-start | bytes 2359304 | tf_op jit(solution)/shard_map/ppermute | solution.py:508
  471.2 34.8 %collective-permute-start.48 = (bf16[128,3072]{1,0:T(8,128)(2,1)}, bf16[128,3072]{1,0:T(8,128)(2,1)}, u32[]{:S(2)}, u32[]{:S(2)}) collective-permute-start(bf16[128,3072]{1,0:T(8,128)(2,1)} %get-tuple-element.55.refs_0_.refs_16_), channel_id=1, source_target_pairs={{0,4},{1,5},{2,6},{3,7},{4,0},{5,1},{6,2},{7,3},{8,12},{9,13},{10,... | collective-permute-start | bytes 2359304 | tf_op jit(solution)/shard_map/ppermute | solution.py:508
  472.6 36.3 %collective-permute-start.46 = (bf16[128,3072]{1,0:T(8,128)(2,1)}, bf16[128,3072]{1,0:T(8,128)(2,1)}, u32[]{:S(2)}, u32[]{:S(2)}) collective-permute-start(bf16[128,3072]{1,0:T(8,128)(2,1)} %get-tuple-element.55.refs_0_.refs_16_), channel_id=1, source_target_pairs={{0,2},{1,3},{2,0},{3,1},{4,6},{5,7},{6,4},{7,5},{8,10},{9,11},{10,... | collective-permute-start | bytes 2359304 | tf_op jit(solution)/shard_map/ppermute | solution.py:508
  505.9 18.1 %collective-permute-start.50 = (bf16[128,3072]{1,0:T(8,128)(2,1)}, bf16[128,3072]{1,0:T(8,128)(2,1)}, u32[]{:S(2)}, u32[]{:S(2)}) collective-permute-start(bf16[128,3072]{1,0:T(8,128)(2,1)} %collective-permute-done.48.refs_4_.refs_20_), channel_id=1, source_target_pairs={{0,2},{1,3},{2,0},{3,1},{4,6},{5,7},{6,4},{7,5},{8,10},{9,11},{10,... | collective-permute-start | bytes 2359304 | tf_op jit(solution)/shard_map/ppermute | solution.py:508
  506.0 20.3 %collective-permute-start.57 = (bf16[128,3072]{1,0:T(8,128)(2,1)}, bf16[128,3072]{1,0:T(8,128)(2,1)}, u32[]{:S(2)}, u32[]{:S(2)}) collective-permute-start(bf16[128,3072]{1,0:T(8,128)(2,1)} %collective-permute-done.53.refs_10_.refs_26_), channel_id=1, source_target_pairs={{0,4},{1,5},{2,6},{3,7},{4,0},{5,1},{6,2},{7,3},{8,12},{9,13},{10,... | collective-permute-start | bytes 2359304 | tf_op jit(solution)/shard_map/ppermute | solution.py:508
  507.0 19.3 %collective-permute-start.52 = (bf16[128,3072]{1,0:T(8,128)(2,1)}, bf16[128,3072]{1,0:T(8,128)(2,1)S(1)}, u32[]{:S(2)}, u32[]{:S(2)}) collective-permute-start(bf16[128,3072]{1,0:T(8,128)(2,1)} %get-tuple-element.78.refs_8_.refs_24_), channel_id=1, source_target_pairs={{0,1},{1,0},{2,3},{3,2},{4,5},{5,4},{6,7},{7,6},{8,9},{9,8},{10,11... | collective-permute-start | bytes 2359304 | tf_op jit(solution)/shard_map/ppermute | solution.py:508
  508.9 17.9 %collective-permute-start.45 = (bf16[128,3072]{1,0:T(8,128)(2,1)}, bf16[128,3072]{1,0:T(8,128)(2,1)S(1)}, u32[]{:S(2)}, u32[]{:S(2)}) collective-permute-start(bf16[128,3072]{1,0:T(8,128)(2,1)} %get-tuple-element.55.refs_0_.refs_16_), channel_id=1, source_target_pairs={{0,1},{1,0},{2,3},{3,2},{4,5},{5,4},{6,7},{7,6},{8,9},{9,8},{10,11... | collective-permute-start | bytes 2359304 | tf_op jit(solution)/shard_map/ppermute | solution.py:508
  508.9 17.9 %collective-permute-start.47 = (bf16[128,3072]{1,0:T(8,128)(2,1)}, bf16[128,3072]{1,0:T(8,128)(2,1)}, u32[]{:S(2)}, u32[]{:S(2)}) collective-permute-start(bf16[128,3072]{1,0:T(8,128)(2,1)} %collective-permute-done.46.refs_2_.refs_18_), channel_id=1, source_target_pairs={{0,1},{1,0},{2,3},{3,2},{4,5},{5,4},{6,7},{7,6},{8,9},{9,8},{10,11... | collective-permute-start | bytes 2359304 | tf_op jit(solution)/shard_map/ppermute | solution.py:508
  524.0 4.3 collective-permute-start.49
  526.2 4.3 collective-permute-start.56
  526.7 5.0 collective-permute-start.51
  526.8 6.2 collective-permute-start.58
  528.3 64.8 %collective-permute-start.62 = (bf16[192,3072]{1,0:T(8,128)(2,1)S(1)}, bf16[192,3072]{1,0:T(8,128)(2,1)S(1)}, u32[]{:S(2)}, u32[]{:S(2)}) collective-permute-start(bf16[192,3072]{1,0:T(8,128)(2,1)S(1)} %copy-done.9), channel_id=1, source_target_pairs={{0,2},{1,3},{2,0},{3,1},{4,6},{5,7},{6,4},{7,5},{8,10},{9,11},{10,... | collective-permute-start | bytes 3538952 | tf_op jit(solution)/shard_map/ppermute | solution.py:508
  529.5 63.7 %collective-permute-start.44 = (bf16[192,3072]{1,0:T(8,128)(2,1)S(1)}, bf16[192,3072]{1,0:T(8,128)(2,1)}, u32[]{:S(2)}, u32[]{:S(2)}) collective-permute-start(bf16[192,3072]{1,0:T(8,128)(2,1)S(1)} %copy-done.9), channel_id=1, source_target_pairs={{0,4},{1,5},{2,6},{3,7},{4,0},{5,1},{6,2},{7,3},{8,12},{9,13},{10,... | collective-permute-start | bytes 3538952 | tf_op jit(solution)/shard_map/ppermute | solution.py:508
  530.6 62.5 %collective-permute-start.65 = (bf16[192,3072]{1,0:T(8,128)(2,1)S(1)}, bf16[192,3072]{1,0:T(8,128)(2,1)}, u32[]{:S(2)}, u32[]{:S(2)}) collective-permute-start(bf16[192,3072]{1,0:T(8,128)(2,1)S(1)} %copy-done.10), channel_id=1, source_target_pairs={{0,4},{1,5},{2,6},{3,7},{4,0},{5,1},{6,2},{7,3},{8,12},{9,13},{10,... | collective-permute-start | bytes 3538952 | tf_op jit(solution)/shard_map/ppermute | solution.py:508
  531.7 61.4 %collective-permute-start.60 = (bf16[192,3072]{1,0:T(8,128)(2,1)S(1)}, bf16[192,3072]{1,0:T(8,128)(2,1)}, u32[]{:S(2)}, u32[]{:S(2)}) collective-permute-start(bf16[192,3072]{1,0:T(8,128)(2,1)S(1)} %copy-done.10), channel_id=1, source_target_pairs={{0,2},{1,3},{2,0},{3,1},{4,6},{5,7},{6,4},{7,5},{8,10},{9,11},{10,... | collective-permute-start | bytes 3538952 | tf_op jit(solution)/shard_map/ppermute | solution.py:508
  593.6 4.4 collective-permute-start.64
  593.7 5.9 collective-permute-start.63
  594.1 7.4 %collective-permute-start.67 = (bf16[192,3072]{1,0:T(8,128)(2,1)}, bf16[192,3072]{1,0:T(8,128)(2,1)}, u32[]{:S(2)}, u32[]{:S(2)}) collective-permute-start(bf16[192,3072]{1,0:T(8,128)(2,1)} %collective-permute-done.65.refs_5_.refs_9_), channel_id=1, source_target_pairs={{0,1},{1,0},{2,3},{3,2},{4,5},{5,4},{6,7},{7,6},{8,9},{9,8},{10,11... | collective-permute-start | bytes 3538952 | tf_op jit(solution)/shard_map/ppermute | solution.py:508
  594.2 53.9 %collective-permute-start.59 = (bf16[192,3072]{1,0:T(8,128)(2,1)}, bf16[192,3072]{1,0:T(8,128)(2,1)S(1)}, u32[]{:S(2)}, u32[]{:S(2)}) collective-permute-start(bf16[192,3072]{1,0:T(8,128)(2,1)} %collective-permute-done.44.refs_4_.refs_8_), channel_id=1, source_target_pairs={{0,2},{1,3},{2,0},{3,1},{4,6},{5,7},{6,4},{7,5},{8,10},{9,11},{10,... | collective-permute-start | bytes 3538952 | tf_op jit(solution)/shard_map/ppermute | solution.py:508
  596.4 51.7 %collective-permute-start.61 = (bf16[192,3072]{1,0:T(8,128)(2,1)}, bf16[192,3072]{1,0:T(8,128)(2,1)S(1)}, u32[]{:S(2)}, u32[]{:S(2)}) collective-permute-start(bf16[192,3072]{1,0:T(8,128)(2,1)} %collective-permute-done.60.refs_1_.refs_5_), channel_id=1, source_target_pairs={{0,4},{1,5},{2,6},{3,7},{4,0},{5,1},{6,2},{7,3},{8,12},{9,13},{10,... | collective-permute-start | bytes 3538952 | tf_op jit(solution)/shard_map/ppermute | solution.py:508
  648.5 4.3 collective-permute-start.69
  (42 other events, 984.8 us)
